TPU v7x, 512 devices: a whole 4x4x16 slice. The times are simulated.
512 devices in a mesh: out: 8 (over y, core), ctr: 64 (over z, x).
Axes of the slice: x: 4, y: 4, z: 16, core: 2. Of those that a mesh axis runs over, the one named last changes fastest.
Arguments:
- centers: bfloat16 [65536, 1024], P('ctr'), may hold values from -6 to 6
- weights: float32 [65536, 1000], P('ctr', 'out'), may hold values from -1.2 to 1.2
- targets: float32 [512, 1000], P(None, 'out'), may hold values from -6 to 6
- batch_rows: int32 [512], replicated, may hold values from 0 to 65535, as said below
- subsample: int32 [32768], P('ctr'), may hold values from 0 to 65535, as said below
- eigvecs: bfloat16 [32768, 512], P('ctr'), may hold values from -0.25 to 0.25
- eig_scale: float32 [512], replicated, may hold values from 0.05 to 0.5
Outputs:
- updated: float32 [65536, 1000], P('ctr', 'out')
- residual: float32 [512, 1000], P(None, 'out')
Inputs may be any that keep to these rules, and one draw needn't show every extreme that they name: `batch_rows`: the entries are distinct. `subsample`: the entries are distinct; the 512 entries of block c (entries c * 512 to (c + 1) * 512 - 1) lie in the center rows c * 1024 to (c + 1) * 1024 - 1.
All inputs are finite; a program needn't handle non-finite values.
Results may differ from a plain program's by a relative error of at most 0.0065.
Values may be sent and summed in bfloat16 or wider, within the bound.
No kernel may reach another device: no remote copies, remote signals or barrier semaphores. Data moves between devices by JAX's collectives and lax.ppermute only.
A program may use at most 64 MiB of HBM per device.

v0:
```python
import jax
import jax.numpy as jnp
from jax import lax
from jax.sharding import PartitionSpec as P

step_size = 0.5


def in_blocks(shard, dim, length):
    before, after = (shard.shape[:dim], shard.shape[dim + 1 :])
    return jnp.moveaxis(shard.reshape(*before, length, -1, *after), dim, 0)


def sent_and_summed(shard, axis, dim):
    pieces = in_blocks(shard, dim, lax.axis_size(axis))
    arrived = lax.all_to_all(pieces, axis, split_axis=0, concat_axis=0, tiled=True)
    return arrived.astype(jnp.float32).sum(axis=0)


def padded_to(lines, length):
    spare = -lines.shape[0] % length
    if not spare:
        return lines
    return jnp.concatenate([lines, jnp.zeros((spare, *lines.shape[1:]), lines.dtype)])


def from_everyone(shard, axis):
    copies = jnp.broadcast_to(shard, (lax.axis_size(axis), *shard.shape))
    return lax.all_to_all(copies, axis, split_axis=0, concat_axis=0, tiled=True)


def joined_along(pieces, dim):
    lengths = list(pieces.shape[1:])
    lengths[dim] *= pieces.shape[0]
    return jnp.moveaxis(pieces, 0, dim).reshape(lengths)


def gathered_copies(shard, axis, dim):
    pieces = from_everyone(shard, axis)
    return joined_along(pieces, dim)


def nested_sum(shard, axes):
    lines = shard.reshape(-1, shard.shape[-1])
    own = sent_and_summed(padded_to(lines, lax.axis_size(axes)), axes, 0)
    whole = gathered_copies(own.astype(jnp.bfloat16), axes, 0)
    return whole[: len(lines)].reshape(shard.shape).astype(jnp.float32)


def kernel(left, right, feature_count):
    left_norm = jnp.sum(jnp.square(left.astype(jnp.float32)), axis=1)
    right_norm = jnp.sum(jnp.square(right.astype(jnp.float32)), axis=1)
    inner_prod = jnp.dot(left, right.T, preferred_element_type=jnp.float32)
    return jnp.exp(
        -(left_norm[:, None] + right_norm[None, :] - 2.0 * inner_prod) * (2.0 / feature_count)
    )


def body(centers, weights, targets, batch_rows, subsample, eigvecs, eig_scale):
    row_count = centers.shape[0]
    feature_count = centers.shape[1]
    position = lax.axis_index("ctr")
    local_rows = batch_rows - position * row_count
    owned_rows = (local_rows >= 0) & (local_rows < row_count)
    safe_rows = jnp.clip(local_rows, 0, row_count - 1)
    picked = jnp.where(owned_rows[:, None], centers[safe_rows].astype(jnp.float32), 0.0)
    batch_feats = nested_sum(picked.astype(jnp.bfloat16), "ctr").astype(jnp.bfloat16)
    batch_kernel = kernel(batch_feats, centers, feature_count).astype(jnp.bfloat16)
    pred_part = jnp.dot(
        batch_kernel, weights.astype(jnp.bfloat16), preferred_element_type=jnp.float32
    )
    sub_local = subsample - position * row_count
    sub_feats = centers[sub_local]
    sub_kernel = kernel(sub_feats, batch_feats, feature_count).astype(jnp.bfloat16)
    projected_part = lax.dot_general(
        eigvecs, sub_kernel, (((0,), (0,)), ((), ())), preferred_element_type=jnp.float32
    )
    prediction, projected = (
        nested_sum(pred_part.astype(jnp.bfloat16), "ctr"),
        nested_sum(projected_part.astype(jnp.bfloat16), "ctr"),
    )
    residual = prediction - targets
    coefficient = jnp.dot(projected, residual, precision=lax.Precision.HIGHEST)
    correction = jnp.dot(
        eigvecs.astype(jnp.float32),
        eig_scale[:, None] * coefficient,
        precision=lax.Precision.HIGHEST,
    )
    updated = weights.at[safe_rows].add(jnp.where(owned_rows[:, None], -step_size * residual, 0.0))
    updated = updated.at[sub_local].add(step_size * correction)
    return (updated, residual)


def solution(mesh):
    placed = (P("ctr", None), P("ctr", "out"), P(None, "out"), P(), P("ctr"), P("ctr", None), P())
    return jax.shard_map(
        body,
        mesh=mesh,
        in_specs=placed,
        out_specs=(P("ctr", "out"), P(None, "out")),
        check_vma=False,
    )
```

profile of v0, /device:TPU:8, one launch (start us, length us, event | category | flops | bytes accessed | tf_op | source)
XLA Modules:
  0.0 271.2 jit_solution(15182236618088000482)
XLA Ops:
  0.6 1.1 copy.15
  1.7 0.7 compare_select_fusion.1
  2.4 0.7 compare_and_fusion
  3.2 4.6 %gather_fusion = bf16[512,1024]{1,0:T(8,128)(2,1)S(1)} fusion(bf16[1024,1024]{1,0:T(8,128)(2,1)} %param.7, s32[1024]{0:T(1024)S(1)} %pad_clamp_fusion.1), kind=kCustom, calls=%fused_computation | custom fusion | bytes 2099200 | tf_op jit(solution)/shard_map/gather | solution.py:66
  7.8 0.2 fusion
  8.1 73.8 %all_to_all.30 = bf16[64,8,1024]{2,1,0:T(8,128)(2,1)} all-to-all(bf16[64,8,1024]{2,1,0:T(8,128)(2,1)S(1)} %fusion), channel_id=1, replica_groups=mesh['out'=8,'ctr'=64] {'ctr'}, dimensions={0} | all-to-all | bytes 2097152 | tf_op jit(solution)/shard_map/all_to_all | solution.py:16
  81.8 1.6 reduce_sum.67
  83.4 1.2 broadcast_in_dim.55
  84.6 6.1 %all-to-all-start.1 = ((bf16[64,8,1024]{2,1,0:T(8,128)(2,1)}), bf16[64,8,1024]{2,1,0:T(8,128)(2,1)}, u32[]{:S(2)}, u32[]{:S(2)}) async-start(bf16[64,8,1024]{2,1,0:T(8,128)(2,1)} %broadcast_in_dim.55), calls=%async_computation.1 | async-start | bytes 2097152 | tf_op jit(solution)/shard_map/all_to_all | solution.py:29
  90.7 2.8 %gather_fusion.1 = bf16[512,1024]{1,0:T(8,128)(2,1)} fusion(bf16[1024,1024]{1,0:T(8,128)(2,1)S(1)} %copy-done.1, s32[1024]{0:T(1024)S(1)} %pad_clamp_fusion), kind=kCustom, calls=%fused_computation.1 | custom fusion | bytes 2099200 | tf_op jit(solution)/shard_map/gather | solution.py:73
  93.5 0.5 multiply_reduce_fusion
  94.0 50.9 %all-to-all-done.1 = bf16[64,8,1024]{2,1,0:T(8,128)(2,1)} async-done(((bf16[64,8,1024]{2,1,0:T(8,128)(2,1)}), bf16[64,8,1024]{2,1,0:T(8,128)(2,1)}, u32[]{:S(2)}, u32[]{:S(2)}) %all-to-all-start.1) | async-done | bytes 1048608 | tf_op jit(solution)/shard_map/all_to_all | solution.py:29
  144.9 1.5 multiply_reduce_fusion.2
  146.5 3.7 %fusion.10 = bf16[64,8,125]{2,1,0:T(8,128)(2,1)} fusion(bf16[1024,1024]{1,0:T(8,128)(2,1)S(1)} %copy-done.1, bf16[64,8,1024]{2,1,0:T(8,128)(2,1)} %all-to-all-done.1, f32[1024]{0:T(1024)S(1)} %multiply_reduce_fusion, f32[512]{0:T(512)S(1)} %add.41, f32[1024,125]{1,0:T(8,128)S(1)} %copy.15), kind=kOutput, calls=%fused_computation.23 | convolution fusion | flops 1208151552 | bytes 3791872 | tf_op jit(solution)/shard_map/dot_general | solution.py:69
  150.2 5.8 %all-to-all-start.2 = ((bf16[64,8,125]{2,1,0:T(8,128)(2,1)}), bf16[64,8,125]{2,1,0:T(8,128)(2,1)S(1)}, u32[]{:S(2)}, u32[]{:S(2)}) async-start(bf16[64,8,125]{2,1,0:T(8,128)(2,1)} %fusion.10), calls=%async_computation.2 | async-start | bytes 262144 | tf_op jit(solution)/shard_map/all_to_all | solution.py:16
  156.0 1.5 multiply_reduce_fusion.1
  157.5 3.5 %fusion.6 = bf16[64,8,512]{2,1,0:T(8,128)(2,1)} fusion(bf16[512,512]{1,0:T(8,128)(2,1)S(1)} %copy-done, bf16[512,1024]{1,0:T(8,128)(2,1)} %gather_fusion.1, bf16[64,8,1024]{2,1,0:T(8,128)(2,1)} %all-to-all-done.1, f32[512]{0:T(512)S(1)} %add.41, f32[512]{0:T(512)S(1)} %multiply_reduce_fusion.1), kind=kOutput, calls=%fused_computation.17 | convolution fusion | flops 807141376 | bytes 3149824 | tf_op jit(solution)/shard_map/dot_general | solution.py:75
  161.0 11.4 %all-to-all-done.2 = bf16[64,8,125]{2,1,0:T(8,128)(2,1)S(1)} async-done(((bf16[64,8,125]{2,1,0:T(8,128)(2,1)}), bf16[64,8,125]{2,1,0:T(8,128)(2,1)S(1)}, u32[]{:S(2)}, u32[]{:S(2)}) %all-to-all-start.2) | async-done | bytes 128032 | tf_op jit(solution)/shard_map/all_to_all | solution.py:16
  172.4 4.6 %all-to-all-start.4 = ((bf16[64,8,512]{2,1,0:T(8,128)(2,1)}), bf16[64,8,512]{2,1,0:T(8,128)(2,1)S(1)}, u32[]{:S(2)}, u32[]{:S(2)}) async-start(bf16[64,8,512]{2,1,0:T(8,128)(2,1)} %fusion.6), calls=%async_computation.4 | async-start | bytes 1048576 | tf_op jit(solution)/shard_map/all_to_all | solution.py:16
  177.2 30.0 %all-to-all-done.4 = bf16[64,8,512]{2,1,0:T(8,128)(2,1)S(1)} async-done(((bf16[64,8,512]{2,1,0:T(8,128)(2,1)}), bf16[64,8,512]{2,1,0:T(8,128)(2,1)S(1)}, u32[]{:S(2)}, u32[]{:S(2)}) %all-to-all-start.4) | async-done | bytes 524320 | tf_op jit(solution)/shard_map/all_to_all | solution.py:16
  207.2 0.7 broadcast_in_dim.56
  207.9 5.7 %all-to-all-start.3 = ((bf16[64,8,125]{2,1,0:T(8,128)(2,1)}), bf16[64,8,125]{2,1,0:T(8,128)(2,1)S(1)}, u32[]{:S(2)}, u32[]{:S(2)}) async-start(bf16[64,8,125]{2,1,0:T(8,128)(2,1)} %broadcast_in_dim.56), calls=%async_computation.3 | async-start | bytes 262144 | tf_op jit(solution)/shard_map/all_to_all | solution.py:29
  213.7 16.2 %all-to-all-done.3 = bf16[64,8,125]{2,1,0:T(8,128)(2,1)S(1)} async-done(((bf16[64,8,125]{2,1,0:T(8,128)(2,1)}), bf16[64,8,125]{2,1,0:T(8,128)(2,1)S(1)}, u32[]{:S(2)}, u32[]{:S(2)}) %all-to-all-start.3) | async-done | bytes 128032 | tf_op jit(solution)/shard_map/all_to_all | solution.py:29
  229.9 0.8 broadcast_in_dim.59
  230.7 4.8 %all-to-all-start.5 = ((bf16[64,8,512]{2,1,0:T(8,128)(2,1)}), bf16[64,8,512]{2,1,0:T(8,128)(2,1)S(1)}, u32[]{:S(2)}, u32[]{:S(2)}) async-start(bf16[64,8,512]{2,1,0:T(8,128)(2,1)} %broadcast_in_dim.59), calls=%async_computation.5 | async-start | bytes 1048576 | tf_op jit(solution)/shard_map/all_to_all | solution.py:29
  235.6 4.4 %scatter_custom_fusion = f32[1024,125]{1,0:T(8,128)S(1)} fusion(f32[1024,125]{1,0:T(8,128)S(1)} %copy.15, s32[512]{0:T(512)S(1)} %compare_select_fusion.1, f32[512,125]{1,0:T(8,128)S(1)} %convert_subtract_fusion, f32[]{:T(128)} %constant.4.clone.1, f32[]{:T(128)} %constant.8.clone.1, pred[512]{0:T(512)(128)(4,1)S(1)} %compare_and_fusion), kind=kCustom, calls=%fused_computation.36 | custom fusion | flops 192000 | bytes 774664 | tf_op jit(solution)/shard_map/scatter-add | solution.py:89
  240.0 25.4 %all-to-all-done.5 = bf16[64,8,512]{2,1,0:T(8,128)(2,1)S(1)} async-done(((bf16[64,8,512]{2,1,0:T(8,128)(2,1)}), bf16[64,8,512]{2,1,0:T(8,128)(2,1)S(1)}, u32[]{:S(2)}, u32[]{:S(2)}) %all-to-all-start.5) | async-done | bytes 524320 | tf_op jit(solution)/shard_map/all_to_all | solution.py:29
  265.4 0.6 convolution_multiply_fusion.2
  266.0 0.7 fusion.7
  266.7 0.1 copy.11
  266.8 3.5 %scatter_fusion = f32[1024,125]{1,0:T(8,128)S(1)} fusion(f32[1024,125]{1,0:T(8,128)S(1)} %scatter_custom_fusion, s32[512]{0:T(512)S(1)} %compare_select_fusion, f32[512,125]{1,0:T(8,128)S(1)} %copy.11), kind=kCustom, calls=%fused_computation.3 | custom fusion | flops 64000 | bytes 770048 | tf_op jit(solution)/shard_map/scatter-add | solution.py:90
  270.4 0.8 copy-done.2
  (21 shorter events, 0.4 us)
Async XLA Ops:
  0.6 156.9 %copy-start = (bf16[512,512]{1,0:T(8,128)(2,1)S(1)}, bf16[512,512]{1,0:T(8,128)(2,1)}, u32[]{:S(2)}) copy-start(bf16[512,512]{1,0:T(8,128)(2,1)} %param.12) | copy-start | bytes 1572868
  81.8 8.8 %copy-start.6 = (s32[512]{0:T(512)S(1)}, s32[512]{0:T(512)}, u32[]{:S(2)}) copy-start(s32[512]{0:T(512)} %param.11) | copy-start | bytes 6148
  81.8 8.9 %copy-start.1 = (bf16[1024,1024]{1,0:T(8,128)(2,1)S(1)}, bf16[1024,1024]{1,0:T(8,128)(2,1)}, u32[]{:S(2)}) copy-start(bf16[1024,1024]{1,0:T(8,128)(2,1)} %param.7) | copy-start | bytes 6291460
  84.6 60.4 %all-to-all-start.1 = ((bf16[64,8,1024]{2,1,0:T(8,128)(2,1)}), bf16[64,8,1024]{2,1,0:T(8,128)(2,1)}, u32[]{:S(2)}, u32[]{:S(2)}) async-start(bf16[64,8,1024]{2,1,0:T(8,128)(2,1)} %broadcast_in_dim.55), calls=%async_computation.1 | async-start | bytes 2097152 | tf_op jit(solution)/shard_map/all_to_all | solution.py:29
  150.2 22.3 %all-to-all-start.2 = ((bf16[64,8,125]{2,1,0:T(8,128)(2,1)}), bf16[64,8,125]{2,1,0:T(8,128)(2,1)S(1)}, u32[]{:S(2)}, u32[]{:S(2)}) async-start(bf16[64,8,125]{2,1,0:T(8,128)(2,1)} %fusion.10), calls=%async_computation.2 | async-start | bytes 262144 | tf_op jit(solution)/shard_map/all_to_all | solution.py:16
  161.0 74.5 %copy-start.4 = (f32[512,125]{1,0:T(8,128)S(1)}, f32[512,125]{1,0:T(8,128)}, u32[]{:S(2)}) copy-start(f32[512,125]{1,0:T(8,128)} %param.9) | copy-start | bytes 768004
  172.4 34.7 %all-to-all-start.4 = ((bf16[64,8,512]{2,1,0:T(8,128)(2,1)}), bf16[64,8,512]{2,1,0:T(8,128)(2,1)S(1)}, u32[]{:S(2)}, u32[]{:S(2)}) async-start(bf16[64,8,512]{2,1,0:T(8,128)(2,1)} %fusion.6), calls=%async_computation.4 | async-start | bytes 1048576 | tf_op jit(solution)/shard_map/all_to_all | solution.py:16
  177.1 88.3 %copy-start.5 = (f32[512]{0:T(512)S(1)}, f32[512]{0:T(512)}, u32[]{:S(2)}) copy-start(f32[512]{0:T(512)} %param.13) | copy-start | bytes 6148
  207.9 22.0 %all-to-all-start.3 = ((bf16[64,8,125]{2,1,0:T(8,128)(2,1)}), bf16[64,8,125]{2,1,0:T(8,128)(2,1)S(1)}, u32[]{:S(2)}, u32[]{:S(2)}) async-start(bf16[64,8,125]{2,1,0:T(8,128)(2,1)} %broadcast_in_dim.56), calls=%async_computation.3 | async-start | bytes 262144 | tf_op jit(solution)/shard_map/all_to_all | solution.py:29
  230.7 34.7 %all-to-all-start.5 = ((bf16[64,8,512]{2,1,0:T(8,128)(2,1)}), bf16[64,8,512]{2,1,0:T(8,128)(2,1)S(1)}, u32[]{:S(2)}, u32[]{:S(2)}) async-start(bf16[64,8,512]{2,1,0:T(8,128)(2,1)} %broadcast_in_dim.59), calls=%async_computation.5 | async-start | bytes 1048576 | tf_op jit(solution)/shard_map/all_to_all | solution.py:29
  235.6 34.8 %copy-start.3 = (f32[512,125]{1,0:T(8,128)}, f32[512,125]{1,0:T(8,128)S(1)}, u32[]{:S(2)}) copy-start(f32[512,125]{1,0:T(8,128)S(1)} %convert_subtract_fusion) | copy-start | bytes 768004
  270.4 0.8 copy-start.2
where the time goes:
time: 272 us; the launch traced here: 271 us
  waiting for transfers between devices  134 us (49%)
  blocking collectives  73.8 us (27%)
  starting transfers between devices  27.1 us (10%)
  other arithmetic  14.8 us (5%)
  local copies, waits for them, and re-layouts  12.3 us (5%)
  matrix products  8.48 us (3%)
    all_to_all x3, waiting for transfers between devices, from_everyone(): return lax.all_to_all(copies, axis, split_axis=0, concat_axis=0, tiled=True)  92.5 us
    all_to_all x1, blocking collectives, sent_and_summed(): lax.all_to_all(pieces, axis, split_axis=0, concat_axis=0, tiled=True)  73.8 us
    all_to_all x2, waiting for transfers between devices, sent_and_summed(): lax.all_to_all(pieces, axis, split_axis=0, concat_axis=0, tiled=True)  41.4 us
    all_to_all x3, starting transfers between devices, from_everyone(): return lax.all_to_all(copies, axis, split_axis=0, concat_axis=0, tiled=True)  16.6 us
    all_to_all x2, starting transfers between devices, sent_and_summed(): lax.all_to_all(pieces, axis, split_axis=0, concat_axis=0, tiled=True)  10.5 us
  transfers between devices with their start and end apart: 5, of which 5 were waited for; matrix products, arithmetic and copies ran while one was open for 5% of the time, Pallas kernels for 0%

commit v1 on v0

v1 whole, which is shorter than its diff:
```python
import jax
import jax.numpy as jnp
from jax import lax
from jax.sharding import Mesh, PartitionSpec as P

step_size = 0.5
OUT = ("y", "core")
CTR = ("z", "x")
LANES = 128


def exchanged(pieces, axes):
    return lax.all_to_all(pieces, axes, split_axis=0, concat_axis=0, tiled=True)


def summed_share(pieces, axes):
    arrived = exchanged(pieces, axes)
    return arrived.astype(jnp.float32).sum(axis=0).astype(jnp.bfloat16)


def copied_to_all(shard, axes):
    return exchanged(jnp.broadcast_to(shard, (lax.axis_size(axes), *shard.shape)), axes)


def shifted(shard, dy, dc):
    ny, ncore = lax.axis_size("y"), lax.axis_size("core")
    if dy == 0 and dc == 0:
        return shard
    pairs = [
        (y * ncore + c, (y + dy) % ny * ncore + (c + dc) % ncore)
        for y in range(ny)
        for c in range(ncore)
    ]
    return lax.ppermute(shard, OUT, pairs)


def by_owner(blocks):
    for dim, name in enumerate(OUT):
        size = lax.axis_size(name)
        back = jnp.concatenate([lax.rev(blocks, (dim,))] * 2, axis=dim)
        start = size - 1 - lax.axis_index(name)
        blocks = lax.dynamic_slice_in_dim(back, start, size, axis=dim)
    return blocks


def one_hot(rows, length):
    return (lax.broadcasted_iota(jnp.int32, (rows.shape[0], length), 1) == rows[:, None]).astype(
        jnp.bfloat16
    )


def one_hot_columns(rows, length):
    return (lax.broadcasted_iota(jnp.int32, (length, rows.shape[0]), 0) == rows[None, :]).astype(
        jnp.bfloat16
    )


def dot(left, right):
    return jnp.dot(left, right, preferred_element_type=jnp.float32)


def summed_over_ctr(block):
    nx, nz = lax.axis_size("x"), lax.axis_size("z")
    width = block.shape[1]
    share = summed_share(block.reshape(nx, nz, width), "x")
    return summed_share(share.reshape(nz, width // LANES, LANES), "z")


def body(centers, weights, targets, batch_rows, subsample, eigvecs, eig_scale):
    low = jnp.bfloat16
    row_count, feature_count = centers.shape
    nout, nx, nz = lax.axis_size(OUT), lax.axis_size("x"), lax.axis_size("z")
    batch = batch_rows.shape[0]
    columns = weights.shape[1]
    block = batch // nout
    ny, ncore = lax.axis_size("y"), lax.axis_size("core")
    base = lax.axis_index(CTR) * row_count
    local_rows = batch_rows - base

    own_rows = lax.dynamic_slice(local_rows, (lax.axis_index(OUT) * block,), (block,))
    picked = dot(one_hot(own_rows, row_count), centers).astype(low)
    share = summed_over_ctr(picked)
    share = copied_to_all(share, "z").reshape(nz, feature_count)
    feats = copied_to_all(share, "x").reshape(block, feature_count)

    weights_low = jnp.pad(weights.astype(low), ((0, 0), (0, LANES - columns)))
    blocks = [shifted(weights_low, dy, dc) for dy in range(ny) for dc in range(ncore)]
    weights_all = jnp.concatenate(blocks, axis=1)

    sub_vecs = dot(one_hot_columns(subsample - base, row_count), eigvecs).astype(low)
    right_norm = jnp.sum(jnp.square(centers.astype(jnp.float32)), axis=1)

    left_norm = jnp.sum(jnp.square(feats.astype(jnp.float32)), axis=1)
    inner = lax.dot_general(
        feats, centers, (((1,), (1,)), ((), ())), preferred_element_type=jnp.float32
    )
    kernel = jnp.exp(
        -(left_norm[:, None] + right_norm[None, :] - 2.0 * inner) * (2.0 / feature_count)
    ).astype(low)

    parts = jnp.concatenate(
        [dot(kernel, weights_all).astype(low), dot(kernel, sub_vecs).astype(low)], axis=1
    )
    share = summed_over_ctr(parts)
    share = copied_to_all(share, "z")
    heads = jnp.moveaxis(share[:, :nout], 1, 0)
    heads = by_owner(heads.reshape(ny, ncore, nz, LANES)).reshape(heads.shape)
    tails = share[:, nout:].reshape(nz, -1)
    pieces = jnp.concatenate(
        [heads, jnp.broadcast_to(tails, (nout, *tails.shape))], axis=2
    )
    pieces = jnp.broadcast_to(pieces[:, None], (nout, nx, *pieces.shape[1:]))
    arrived = exchanged(pieces.reshape(nout * nx, *pieces.shape[2:]), (*OUT, "x"))
    arrived = arrived.reshape(batch, -1)
    residual = arrived[:, :columns].astype(jnp.float32) - targets
    projected = arrived[:, LANES:]
    coefficient = lax.dot_general(
        projected, residual.astype(low), (((0,), (0,)), ((), ())), preferred_element_type=jnp.float32
    )
    changes = jnp.concatenate(
        [(step_size * eig_scale[:, None] * coefficient).astype(low), (-step_size * residual).astype(low)]
    )
    spread = jnp.concatenate([sub_vecs, one_hot_columns(local_rows, row_count)], axis=1)
    updated = weights + dot(spread, changes)
    return (updated, residual)


def solution(mesh):
    axes = ("y", "core", "z", "x")
    fine = Mesh(mesh.devices.reshape(4, 2, 16, 4), axes)
    placed = (P(CTR, None), P(CTR, OUT), P(None, OUT), P(), P(CTR), P(CTR, None), P())
    return jax.shard_map(
        body,
        mesh=fine,
        in_specs=placed,
        out_specs=(P(CTR, OUT), P(None, OUT)),
        check_vma=False,
    )
```

time: 272 us -> 166 us (0.61)
  the two profiles are of different devices: /device:TPU:8 before, /device:TPU:1 now
where the time goes in v1:
time: 166 us; the launch traced here: 165 us
  starting transfers between devices  63.6 us (38%)
  waiting for transfers between devices  41.7 us (25%)
  blocking collectives  30.6 us (18%)
  local copies, waits for them, and re-layouts  15.2 us (9%)
  matrix products  9.2 us (6%)
  other arithmetic  3.51 us (2%)
    all_to_all x6, waiting for transfers between devices, exchanged(): return lax.all_to_all(pieces, axes, split_axis=0, concat_axis=0, tiled=True)  41.7 us
    all_to_all x6, starting transfers between devices, exchanged(): return lax.all_to_all(pieces, axes, split_axis=0, concat_axis=0, tiled=True)  35.1 us
    all_to_all x2, blocking collectives, exchanged(): return lax.all_to_all(pieces, axes, split_axis=0, concat_axis=0, tiled=True)  30.6 us
    ppermute x7, starting transfers between devices, shifted(): return lax.ppermute(shard, OUT, pairs)  28.6 us
    unnamed x27, local copies, waits for them, and re-layouts  9.63 us
    dot_general x5, matrix products, dot(): return jnp.dot(left, right, preferred_element_type=jnp.float32)  8.06 us
  transfers between devices with their start and end apart: 13, of which 5 were waited for; matrix products, arithmetic and copies ran while one was open for 11% of the time, Pallas kernels for 0%

profile of v1, /device:TPU:1, one launch (start us, length us, event | category | flops | bytes accessed | tf_op | source)
XLA Modules:
  0.0 164.8 jit_solution(11243010707922974780)
XLA Ops:
  0.7 1.1 convert_element_type.58
  1.8 0.8 fusion.26
  2.6 8.7 %collective-permute-start = (bf16[1024,128]{1,0:T(8,128)(2,1)S(1)}, bf16[1024,128]{1,0:T(8,128)(2,1)}, u32[]{:S(2)}, u32[]{:S(2)}) collective-permute-start(bf16[1024,128]{1,0:T(8,128)(2,1)S(1)} %get-tuple-element.4), channel_id=1, source_target_pairs={{0,64},{64,0},{128,192},{192,128},{256,320},{320,256},{384,448},{4... | collective-permute-start | bytes 786440 | tf_op jit(solution)/shard_map/ppermute | solution.py:34
  11.3 1.9 %collective-permute-start.1 = (bf16[1024,128]{1,0:T(8,128)(2,1)S(1)}, bf16[1024,128]{1,0:T(8,128)(2,1)}, u32[]{:S(2)}, u32[]{:S(2)}) collective-permute-start(bf16[1024,128]{1,0:T(8,128)(2,1)S(1)} %get-tuple-element.4), channel_id=1, source_target_pairs={{0,128},{64,192},{128,256},{192,320},{256,384},{320,448},{384,0},{... | collective-permute-start | bytes 786440 | tf_op jit(solution)/shard_map/ppermute | solution.py:34
  13.3 1.9 %collective-permute-start.2 = (bf16[1024,128]{1,0:T(8,128)(2,1)S(1)}, bf16[1024,128]{1,0:T(8,128)(2,1)}, u32[]{:S(2)}, u32[]{:S(2)}) collective-permute-start(bf16[1024,128]{1,0:T(8,128)(2,1)S(1)} %get-tuple-element.4), channel_id=1, source_target_pairs={{0,192},{64,128},{128,320},{192,256},{256,448},{320,384},{384,64},... | collective-permute-start | bytes 786440 | tf_op jit(solution)/shard_map/ppermute | solution.py:34
  15.2 5.9 %collective-permute-start.3 = (bf16[1024,128]{1,0:T(8,128)(2,1)S(1)}, bf16[1024,128]{1,0:T(8,128)(2,1)S(1)}, u32[]{:S(2)}, u32[]{:S(2)}) collective-permute-start(bf16[1024,128]{1,0:T(8,128)(2,1)S(1)} %get-tuple-element.4), channel_id=1, source_target_pairs={{0,256},{64,320},{128,384},{192,448},{256,0},{320,64},{384,128},{4... | collective-permute-start | bytes 786440 | tf_op jit(solution)/shard_map/ppermute | solution.py:34
  21.1 2.0 %collective-permute-start.4 = (bf16[1024,128]{1,0:T(8,128)(2,1)S(1)}, bf16[1024,128]{1,0:T(8,128)(2,1)S(1)}, u32[]{:S(2)}, u32[]{:S(2)}) collective-permute-start(bf16[1024,128]{1,0:T(8,128)(2,1)S(1)} %get-tuple-element.4), channel_id=1, source_target_pairs={{0,320},{64,256},{128,448},{192,384},{256,64},{320,0},{384,192},{4... | collective-permute-start | bytes 786440 | tf_op jit(solution)/shard_map/ppermute | solution.py:34
  23.9 2.8 %convolution_convert_fusion.1 = bf16[64,1024]{1,0:T(8,128)(2,1)} fusion(bf16[1024,1024]{1,0:T(8,128)(2,1)} %param.7, s32[64]{0:T(128)S(1)} %dynamic_slice.9), kind=kOutput, calls=%fused_computation.20 | convolution fusion | flops 134348800 | bytes 2228480 | tf_op jit(solution)/shard_map/dot_general | solution.py:59
  26.7 3.5 %all-to-all-start = ((bf16[4,16,1024]{2,1,0:T(8,128)(2,1)}), bf16[4,16,1024]{2,1,0:T(8,128)(2,1)S(1)}, u32[]{:S(2)}, u32[]{:S(2)}) async-start(bf16[4,16,1024]{2,1,0:T(8,128)(2,1)} %bitcast), calls=%async_computation | async-start | bytes 262144 | tf_op jit(solution)/shard_map/all_to_all | solution.py:13
  30.2 1.8 %fusion.6 = bf16[1024,512]{0,1:T(8,128)(2,1)} fusion(bf16[512,512]{1,0:T(8,128)(2,1)S(1)} %copy-done, s32[512]{0:T(512)S(1)} %broadcast_subtract_fusion.1), kind=kOutput, calls=%fused_computation.9 | convolution fusion | flops 537919488 | bytes 1574912 | tf_op jit(solution)/shard_map/dot_general | solution.py:59
  32.0 3.3 %all-to-all-done = bf16[4,16,1024]{2,1,0:T(8,128)(2,1)S(1)} async-done(((bf16[4,16,1024]{2,1,0:T(8,128)(2,1)}), bf16[4,16,1024]{2,1,0:T(8,128)(2,1)S(1)}, u32[]{:S(2)}, u32[]{:S(2)}) %all-to-all-start) | async-done | bytes 131104 | tf_op jit(solution)/shard_map/all_to_all | solution.py:13
  35.9 1.4 copy.12
  37.3 12.3 %all-to-all-start.1 = ((bf16[16,8,128]{2,1,0:T(8,128)(2,1)}), bf16[16,8,128]{2,1,0:T(8,128)(2,1)S(1)}, u32[]{:S(2)}, u32[]{:S(2)}) async-start(bf16[16,8,128]{2,1,0:T(8,128)(2,1)} %bitcast.9), calls=%async_computation.1 | async-start | bytes 65536 | tf_op jit(solution)/shard_map/all_to_all | solution.py:13
  50.0 11.1 %all-to-all-done.1 = bf16[16,8,128]{2,1,0:T(8,128)(2,1)S(1)} async-done(((bf16[16,8,128]{2,1,0:T(8,128)(2,1)}), bf16[16,8,128]{2,1,0:T(8,128)(2,1)S(1)}, u32[]{:S(2)}, u32[]{:S(2)}) %all-to-all-start.1) | async-done | bytes 32800 | tf_op jit(solution)/shard_map/all_to_all | solution.py:13
  61.7 3.5 %all-to-all-start.2 = ((bf16[16,8,128]{2,1,0:T(8,128)(2,1)}), bf16[16,8,128]{2,1,0:T(8,128)(2,1)S(1)}, u32[]{:S(2)}, u32[]{:S(2)}) async-start(bf16[16,8,128]{2,1,0:T(8,128)(2,1)} %broadcast_in_dim.10), calls=%async_computation.2 | async-start | bytes 65536 | tf_op jit(solution)/shard_map/all_to_all | solution.py:13
  65.3 2.9 %collective-permute-start.5 = (bf16[1024,128]{1,0:T(8,128)(2,1)S(1)}, bf16[1024,128]{1,0:T(8,128)(2,1)S(1)}, u32[]{:S(2)}, u32[]{:S(2)}) collective-permute-start(bf16[1024,128]{1,0:T(8,128)(2,1)S(1)} %get-tuple-element.4), channel_id=1, source_target_pairs={{0,384},{64,448},{128,0},{192,64},{256,128},{320,192},{384,256},{4... | collective-permute-start | bytes 786440 | tf_op jit(solution)/shard_map/ppermute | solution.py:34
  68.2 1.7 %constant_dynamic-update-slice_fusion.6 = bf16[1024,1024]{1,0:T(8,128)(2,1)} fusion(bf16[1024,1024]{1,0:T(8,128)(2,1)} %get-tuple-element.5, bf16[1024,128]{1,0:T(8,128)(2,1)} %collective-permute-done), kind=kLoop, calls=%fused_computation.49 | loop fusion | bytes 524288
  69.9 5.1 %collective-permute-start.6 = (bf16[1024,128]{1,0:T(8,128)(2,1)S(1)}, bf16[1024,128]{1,0:T(8,128)(2,1)}, u32[]{:S(2)}, u32[]{:S(2)}) collective-permute-start(bf16[1024,128]{1,0:T(8,128)(2,1)S(1)} %get-tuple-element.4), channel_id=1, source_target_pairs={{0,448},{64,384},{128,64},{192,0},{256,192},{320,128},{384,320},{4... | collective-permute-start | bytes 786440 | tf_op jit(solution)/shard_map/ppermute | solution.py:34
  75.0 1.7 %constant_dynamic-update-slice_fusion.5 = bf16[1024,1024]{1,0:T(8,128)(2,1)} fusion(bf16[1024,1024]{1,0:T(8,128)(2,1)} %constant_dynamic-update-slice_fusion.6, bf16[1024,128]{1,0:T(8,128)(2,1)} %collective-permute-done.1), kind=kLoop, calls=%fused_computation.48 | loop fusion | bytes 524288
  76.7 1.7 %constant_dynamic-update-slice_fusion.4 = bf16[1024,1024]{1,0:T(8,128)(2,1)} fusion(bf16[1024,1024]{1,0:T(8,128)(2,1)} %constant_dynamic-update-slice_fusion.5, bf16[1024,128]{1,0:T(8,128)(2,1)} %collective-permute-done.2), kind=kLoop, calls=%fused_computation.47 | loop fusion | bytes 524288
  81.4 3.3 %all-to-all-start.3 = ((bf16[4,16,1024]{2,1,0:T(8,128)(2,1)}), bf16[4,16,1024]{2,1,0:T(8,128)(2,1)S(1)}, u32[]{:S(2)}, u32[]{:S(2)}) async-start(bf16[4,16,1024]{2,1,0:T(8,128)(2,1)} %broadcast_in_dim.11), calls=%async_computation.3 | async-start | bytes 262144 | tf_op jit(solution)/shard_map/all_to_all | solution.py:13
  84.8 1.7 %constant_dynamic-update-slice_fusion = bf16[1024,1024]{1,0:T(8,128)(2,1)} fusion(bf16[1024,1024]{1,0:T(8,128)(2,1)} %constant_dynamic-update-slice_fusion.1, bf16[1024,128]{1,0:T(8,128)(2,1)} %collective-permute-done.6), kind=kLoop, calls=%fused_computation.43 | loop fusion | bytes 524288 | tf_op jit(solution)/shard_map/concatenate | solution.py:88
  86.5 3.4 %all-to-all-done.3 = bf16[4,16,1024]{2,1,0:T(8,128)(2,1)S(1)} async-done(((bf16[4,16,1024]{2,1,0:T(8,128)(2,1)}), bf16[4,16,1024]{2,1,0:T(8,128)(2,1)S(1)}, u32[]{:S(2)}, u32[]{:S(2)}) %all-to-all-start.3) | async-done | bytes 131104 | tf_op jit(solution)/shard_map/all_to_all | solution.py:13
  90.8 0.8 copy-done.2
  92.6 7.5 %all_to_all.40 = bf16[4,16,1536]{2,1,0:T(8,128)(2,1)S(1)} all-to-all(bf16[4,16,1536]{2,1,0:T(8,128)(2,1)S(1)} %bitcast.30), channel_id=1, replica_groups=mesh['y'=4,'core'=2,'z'=16,'x'=4] {'x'}, dimensions={0} | all-to-all | bytes 393216 | tf_op jit(solution)/shard_map/all_to_all | solution.py:13
  100.3 23.0 %all_to_all.41 = bf16[16,12,128]{2,1,0:T(8,128)(2,1)S(1)} all-to-all(bf16[16,12,128]{2,1,0:T(8,128)(2,1)S(1)} %reshape.52), channel_id=1, replica_groups=mesh['y'=4,'core'=2,'z'=16,'x'=4] {'z'}, dimensions={0} | all-to-all | bytes 98304 | tf_op jit(solution)/shard_map/all_to_all | solution.py:13
  124.0 3.5 %all-to-all-start.6 = ((bf16[16,12,128]{2,1,0:T(8,128)(2,1)}), bf16[16,12,128]{2,1,0:T(8,128)(2,1)S(1)}, u32[]{:S(2)}, u32[]{:S(2)}) async-start(bf16[16,12,128]{2,1,0:T(8,128)(2,1)} %broadcast_in_dim.12), calls=%async_computation.6 | async-start | bytes 131072 | tf_op jit(solution)/shard_map/all_to_all | solution.py:13
  127.5 11.6 %all-to-all-done.6 = bf16[16,12,128]{2,1,0:T(8,128)(2,1)S(1)} async-done(((bf16[16,12,128]{2,1,0:T(8,128)(2,1)}), bf16[16,12,128]{2,1,0:T(8,128)(2,1)S(1)}, u32[]{:S(2)}, u32[]{:S(2)}) %all-to-all-start.6) | async-done | bytes 49184 | tf_op jit(solution)/shard_map/all_to_all | solution.py:13
  139.3 0.9 broadcast_in_dim.28
  140.2 9.0 %all-to-all-start.7 = ((bf16[32,16,640]{2,1,0:T(8,128)(2,1)}), bf16[32,16,640]{2,1,0:T(8,128)(2,1)S(1)}, u32[]{:S(2)}, u32[]{:S(2)}) async-start(bf16[32,16,640]{2,1,0:T(8,128)(2,1)} %bitcast.6), calls=%async_computation.7 | async-start | bytes 1310720 | tf_op jit(solution)/shard_map/all_to_all | solution.py:13
  149.5 12.3 %all-to-all-done.7 = bf16[32,16,640]{2,1,0:T(8,128)(2,1)S(1)} async-done(((bf16[32,16,640]{2,1,0:T(8,128)(2,1)}), bf16[32,16,640]{2,1,0:T(8,128)(2,1)S(1)}, u32[]{:S(2)}, u32[]{:S(2)}) %all-to-all-start.7) | async-done | bytes 655392 | tf_op jit(solution)/shard_map/all_to_all | solution.py:13
  162.3 2.6 %fusion.7 = f32[1024,125]{1,0:T(8,128)} fusion(f32[1024,125]{1,0:T(8,128)} %param.8, bf16[1024,512]{0,1:T(8,128)(2,1)S(1)} %fusion.5, bf16[1024,512]{0,1:T(8,128)(2,1)S(1)} %copy-done.5, bf16[512,125]{1,0:T(8,128)(2,1)S(1)} %get-tuple-element.2, bf16[512,125]{1,0:T(8,128)(2,1)S(1)} %fusion.15), kind=kOutput, calls=%fused_computation.10 | convolution fusion | flops 266978304 | bytes 3377152 | tf_op jit(solution)/shard_map/dot_general | solution.py:59
  (61 shorter events, 9.0 us)
Async XLA Ops:
  0.6 29.6 %copy-start = (bf16[512,512]{1,0:T(8,128)(2,1)S(1)}, bf16[512,512]{1,0:T(8,128)(2,1)}, u32[]{:S(2)}) copy-start(bf16[512,512]{1,0:T(8,128)(2,1)} %param.12) | copy-start | bytes 1572868
  0.6 29.5 %copy-start.7 = (s32[512]{0:T(512)S(1)}, s32[512]{0:T(512)}, u32[]{:S(2)}) copy-start(s32[512]{0:T(512)} %param.11) | copy-start | bytes 6148
  2.6 62.7 %collective-permute-start = (bf16[1024,128]{1,0:T(8,128)(2,1)S(1)}, bf16[1024,128]{1,0:T(8,128)(2,1)}, u32[]{:S(2)}, u32[]{:S(2)}) collective-permute-start(bf16[1024,128]{1,0:T(8,128)(2,1)S(1)} %get-tuple-element.4), channel_id=1, source_target_pairs={{0,64},{64,0},{128,192},{192,128},{256,320},{320,256},{384,448},{4... | collective-permute-start | bytes 786440 | tf_op jit(solution)/shard_map/ppermute | solution.py:34
  11.3 58.6 %collective-permute-start.1 = (bf16[1024,128]{1,0:T(8,128)(2,1)S(1)}, bf16[1024,128]{1,0:T(8,128)(2,1)}, u32[]{:S(2)}, u32[]{:S(2)}) collective-permute-start(bf16[1024,128]{1,0:T(8,128)(2,1)S(1)} %get-tuple-element.4), channel_id=1, source_target_pairs={{0,128},{64,192},{128,256},{192,320},{256,384},{320,448},{384,0},{... | collective-permute-start | bytes 786440 | tf_op jit(solution)/shard_map/ppermute | solution.py:34
  13.3 63.5 %collective-permute-start.2 = (bf16[1024,128]{1,0:T(8,128)(2,1)S(1)}, bf16[1024,128]{1,0:T(8,128)(2,1)}, u32[]{:S(2)}, u32[]{:S(2)}) collective-permute-start(bf16[1024,128]{1,0:T(8,128)(2,1)S(1)} %get-tuple-element.4), channel_id=1, source_target_pairs={{0,192},{64,128},{128,320},{192,256},{256,448},{320,384},{384,64},... | collective-permute-start | bytes 786440 | tf_op jit(solution)/shard_map/ppermute | solution.py:34
  15.2 63.2 %collective-permute-start.3 = (bf16[1024,128]{1,0:T(8,128)(2,1)S(1)}, bf16[1024,128]{1,0:T(8,128)(2,1)S(1)}, u32[]{:S(2)}, u32[]{:S(2)}) collective-permute-start(bf16[1024,128]{1,0:T(8,128)(2,1)S(1)} %get-tuple-element.4), channel_id=1, source_target_pairs={{0,256},{64,320},{128,384},{192,448},{256,0},{320,64},{384,128},{4... | collective-permute-start | bytes 786440 | tf_op jit(solution)/shard_map/ppermute | solution.py:34
  21.1 58.1 %collective-permute-start.4 = (bf16[1024,128]{1,0:T(8,128)(2,1)S(1)}, bf16[1024,128]{1,0:T(8,128)(2,1)S(1)}, u32[]{:S(2)}, u32[]{:S(2)}) collective-permute-start(bf16[1024,128]{1,0:T(8,128)(2,1)S(1)} %get-tuple-element.4), channel_id=1, source_target_pairs={{0,320},{64,256},{128,448},{192,384},{256,64},{320,0},{384,192},{4... | collective-permute-start | bytes 786440 | tf_op jit(solution)/shard_map/ppermute | solution.py:34
  26.7 22.8 %copy-start.1 = (bf16[1024,1024]{1,0:T(8,128)(2,1)S(1)}, bf16[1024,1024]{1,0:T(8,128)(2,1)}, u32[]{:S(2)}) copy-start(bf16[1024,1024]{1,0:T(8,128)(2,1)} %param.7) | copy-start | bytes 6291460
  26.7 8.6 %all-to-all-start = ((bf16[4,16,1024]{2,1,0:T(8,128)(2,1)}), bf16[4,16,1024]{2,1,0:T(8,128)(2,1)S(1)}, u32[]{:S(2)}, u32[]{:S(2)}) async-start(bf16[4,16,1024]{2,1,0:T(8,128)(2,1)} %bitcast), calls=%async_computation | async-start | bytes 262144 | tf_op jit(solution)/shard_map/all_to_all | solution.py:13
  37.3 23.8 %all-to-all-start.1 = ((bf16[16,8,128]{2,1,0:T(8,128)(2,1)}), bf16[16,8,128]{2,1,0:T(8,128)(2,1)S(1)}, u32[]{:S(2)}, u32[]{:S(2)}) async-start(bf16[16,8,128]{2,1,0:T(8,128)(2,1)} %bitcast.9), calls=%async_computation.1 | async-start | bytes 65536 | tf_op jit(solution)/shard_map/all_to_all | solution.py:13
  61.7 19.0 %all-to-all-start.2 = ((bf16[16,8,128]{2,1,0:T(8,128)(2,1)}), bf16[16,8,128]{2,1,0:T(8,128)(2,1)S(1)}, u32[]{:S(2)}, u32[]{:S(2)}) async-start(bf16[16,8,128]{2,1,0:T(8,128)(2,1)} %broadcast_in_dim.10), calls=%async_computation.2 | async-start | bytes 65536 | tf_op jit(solution)/shard_map/all_to_all | solution.py:13
  65.3 14.7 %collective-permute-start.5 = (bf16[1024,128]{1,0:T(8,128)(2,1)S(1)}, bf16[1024,128]{1,0:T(8,128)(2,1)S(1)}, u32[]{:S(2)}, u32[]{:S(2)}) collective-permute-start(bf16[1024,128]{1,0:T(8,128)(2,1)S(1)} %get-tuple-element.4), channel_id=1, source_target_pairs={{0,384},{64,448},{128,0},{192,64},{256,128},{320,192},{384,256},{4... | collective-permute-start | bytes 786440 | tf_op jit(solution)/shard_map/ppermute | solution.py:34
  69.9 14.8 %collective-permute-start.6 = (bf16[1024,128]{1,0:T(8,128)(2,1)S(1)}, bf16[1024,128]{1,0:T(8,128)(2,1)}, u32[]{:S(2)}, u32[]{:S(2)}) collective-permute-start(bf16[1024,128]{1,0:T(8,128)(2,1)S(1)} %get-tuple-element.4), channel_id=1, source_target_pairs={{0,448},{64,384},{128,64},{192,0},{256,192},{320,128},{384,320},{4... | collective-permute-start | bytes 786440 | tf_op jit(solution)/shard_map/ppermute | solution.py:34
  81.4 8.4 %all-to-all-start.3 = ((bf16[4,16,1024]{2,1,0:T(8,128)(2,1)}), bf16[4,16,1024]{2,1,0:T(8,128)(2,1)S(1)}, u32[]{:S(2)}, u32[]{:S(2)}) async-start(bf16[4,16,1024]{2,1,0:T(8,128)(2,1)} %broadcast_in_dim.11), calls=%async_computation.3 | async-start | bytes 262144 | tf_op jit(solution)/shard_map/all_to_all | solution.py:13
  90.0 1.6 copy-start.2
  90.0 2.1 %copy-start.4 = (bf16[1024,512]{0,1:T(8,128)(2,1)S(1)}, bf16[1024,512]{0,1:T(8,128)(2,1)}, u32[]{:S(2)}) copy-start(bf16[1024,512]{0,1:T(8,128)(2,1)} %fusion.6) | copy-start | bytes 3145732
  92.6 56.6 %copy-start.8 = (f32[512]{0:T(512)S(1)}, f32[512]{0:T(512)}, u32[]{:S(2)}) copy-start(f32[512]{0:T(512)} %param.13) | copy-start | bytes 6148
  124.0 15.1 %all-to-all-start.6 = ((bf16[16,12,128]{2,1,0:T(8,128)(2,1)}), bf16[16,12,128]{2,1,0:T(8,128)(2,1)S(1)}, u32[]{:S(2)}, u32[]{:S(2)}) async-start(bf16[16,12,128]{2,1,0:T(8,128)(2,1)} %broadcast_in_dim.12), calls=%async_computation.6 | async-start | bytes 131072 | tf_op jit(solution)/shard_map/all_to_all | solution.py:13
  127.5 34.3 %copy-start.6 = (f32[512,125]{1,0:T(8,128)S(1)}, f32[512,125]{1,0:T(8,128)}, u32[]{:S(2)}) copy-start(f32[512,125]{1,0:T(8,128)} %param.9) | copy-start | bytes 768004
  140.2 22.0 %copy-start.5 = (bf16[1024,512]{0,1:T(8,128)(2,1)S(1)}, bf16[1024,512]{0,1:T(8,128)(2,1)}, u32[]{:S(2)}) copy-start(bf16[1024,512]{0,1:T(8,128)(2,1)} %fusion.6) | copy-start | bytes 3145732
  140.2 21.6 %all-to-all-start.7 = ((bf16[32,16,640]{2,1,0:T(8,128)(2,1)}), bf16[32,16,640]{2,1,0:T(8,128)(2,1)S(1)}, u32[]{:S(2)}, u32[]{:S(2)}) async-start(bf16[32,16,640]{2,1,0:T(8,128)(2,1)} %bitcast.6), calls=%async_computation.7 | async-start | bytes 1310720 | tf_op jit(solution)/shard_map/all_to_all | solution.py:13
  161.9 3.0 %copy-start.3 = (f32[512,125]{1,0:T(8,128)}, f32[512,125]{1,0:T(8,128)S(1)}, u32[]{:S(2)}) copy-start(f32[512,125]{1,0:T(8,128)S(1)} %get-tuple-element.3) | copy-start | bytes 768004

commit v2 on v1

--- a/solution.py
+++ b/solution.py
@@ -20,18 +20,6 @@
 
 def copied_to_all(shard, axes):
     return exchanged(jnp.broadcast_to(shard, (lax.axis_size(axes), *shard.shape)), axes)
-
-
-def shifted(shard, dy, dc):
-    ny, ncore = lax.axis_size("y"), lax.axis_size("core")
-    if dy == 0 and dc == 0:
-        return shard
-    pairs = [
-        (y * ncore + c, (y + dy) % ny * ncore + (c + dc) % ncore)
-        for y in range(ny)
-        for c in range(ncore)
-    ]
-    return lax.ppermute(shard, OUT, pairs)
 
 
 def by_owner(blocks):
@@ -59,11 +47,8 @@
     return jnp.dot(left, right, preferred_element_type=jnp.float32)
 
 
-def summed_over_ctr(block):
-    nx, nz = lax.axis_size("x"), lax.axis_size("z")
-    width = block.shape[1]
-    share = summed_share(block.reshape(nx, nz, width), "x")
-    return summed_share(share.reshape(nz, width // LANES, LANES), "z")
+def summed_row(block):
+    return summed_share(block.reshape(block.shape[0], -1, LANES), CTR)
 
 
 def body(centers, weights, targets, batch_rows, subsample, eigvecs, eig_scale):
@@ -79,13 +64,16 @@
 
     own_rows = lax.dynamic_slice(local_rows, (lax.axis_index(OUT) * block,), (block,))
     picked = dot(one_hot(own_rows, row_count), centers).astype(low)
-    share = summed_over_ctr(picked)
-    share = copied_to_all(share, "z").reshape(nz, feature_count)
-    feats = copied_to_all(share, "x").reshape(block, feature_count)
+    share = summed_row(picked)
+    feats = copied_to_all(share, CTR).reshape(block, feature_count)
 
     weights_low = jnp.pad(weights.astype(low), ((0, 0), (0, LANES - columns)))
-    blocks = [shifted(weights_low, dy, dc) for dy in range(ny) for dc in range(ncore)]
-    weights_all = jnp.concatenate(blocks, axis=1)
+    other = lax.ppermute(weights_low, "core", [(i, (i + 1) % ncore) for i in range(ncore)])
+    pair = jnp.stack([weights_low, other])
+    pairs = [pair] + [
+        lax.ppermute(pair, "y", [(i, (i + dy) % ny) for i in range(ny)]) for dy in range(1, ny)
+    ]
+    weights_all = jnp.concatenate([piece for pair in pairs for piece in pair], axis=1)
 
     sub_vecs = dot(one_hot_columns(subsample - base, row_count), eigvecs).astype(low)
     right_norm = jnp.sum(jnp.square(centers.astype(jnp.float32)), axis=1)
@@ -101,8 +89,7 @@
     parts = jnp.concatenate(
         [dot(kernel, weights_all).astype(low), dot(kernel, sub_vecs).astype(low)], axis=1
     )
-    share = summed_over_ctr(parts)
-    share = copied_to_all(share, "z")
+    share = copied_to_all(summed_row(parts), "z")
     heads = jnp.moveaxis(share[:, :nout], 1, 0)
     heads = by_owner(heads.reshape(ny, ncore, nz, LANES)).reshape(heads.shape)
     tails = share[:, nout:].reshape(nz, -1)
@@ -111,7 +98,7 @@
     )
     pieces = jnp.broadcast_to(pieces[:, None], (nout, nx, *pieces.shape[1:]))
     arrived = exchanged(pieces.reshape(nout * nx, *pieces.shape[2:]), (*OUT, "x"))
-    arrived = arrived.reshape(batch, -1)
+    arrived = arrived.reshape(nout, nx, nz, -1).swapaxes(1, 2).reshape(batch, -1)
     residual = arrived[:, :columns].astype(jnp.float32) - targets
     projected = arrived[:, LANES:]
     coefficient = lax.dot_general(

time: 166 us -> 148 us (0.89)
  waiting for transfers between devices: 41.7 us -> 30.8 us
  blocking collectives: 30.6 us -> 25.8 us
  starting transfers between devices: 63.6 us -> 59.6 us
  other arithmetic: 3.51 us -> 6.21 us
    all_to_all x6 -> x4, waiting for transfers between devices: 41.7 us -> 30.8 us  [exchanged(): return lax.all_to_all(pieces, axes, split_axis=0, concat_axis=0, tiled=True)]
    ppermute x7 -> x4, starting transfers between devices: 28.6 us -> 19.4 us  [the longest x3 10.7 us: body(): lax.ppermute(pair, 'y', [(i, (i + dy) % ny) for i in range(ny)])]
    all_to_all x6 -> x4, starting transfers between devices: 35.1 us -> 40.1 us  [exchanged(): return lax.all_to_all(pieces, axes, split_axis=0, concat_axis=0, tiled=True)]
    all_to_all x2 -> x1, blocking collectives: 30.6 us -> 25.8 us  [exchanged(): return lax.all_to_all(pieces, axes, split_axis=0, concat_axis=0, tiled=True)]
    unnamed x27 -> x24, local copies, waits for them, and re-layouts: 9.63 us -> 9.08 us
  transfers between devices with their start and end apart: 13 -> 8, of which waited for: 5 -> 4; matrix products, arithmetic and copies ran while one was open for 11% -> 12% of each run, Pallas kernels for 0% -> 0%
where the time goes in v2:
time: 148 us; the launch traced here: 147 us
  starting transfers between devices  59.6 us (40%)
  waiting for transfers between devices  30.8 us (21%)
  blocking collectives  25.8 us (17%)
  local copies, waits for them, and re-layouts  13.6 us (9%)
  matrix products  10.3 us (7%)
  other arithmetic  6.21 us (4%)
    all_to_all x4, starting transfers between devices, exchanged(): return lax.all_to_all(pieces, axes, split_axis=0, concat_axis=0, tiled=True)  40.1 us
    all_to_all x4, waiting for transfers between devices, exchanged(): return lax.all_to_all(pieces, axes, split_axis=0, concat_axis=0, tiled=True)  30.8 us
    all_to_all x1, blocking collectives, exchanged(): return lax.all_to_all(pieces, axes, split_axis=0, concat_axis=0, tiled=True)  25.8 us
    ppermute x3, starting transfers between devices, body(): lax.ppermute(pair, 'y', [(i, (i + dy) % ny) for i in range(ny)])  10.7 us
    dot_general x5, matrix products, dot(): return jnp.dot(left, right, preferred_element_type=jnp.float32)  9.19 us
    unnamed x24, local copies, waits for them, and re-layouts  9.08 us
    ppermute x1, starting transfers between devices, body(): lax.ppermute(weights_low, 'core', [(i, (i + 1) % ncore) for i in range(nc...  8.73 us
  transfers between devices with their start and end apart: 8, of which 4 were waited for; matrix products, arithmetic and copies ran while one was open for 12% of the time, Pallas kernels for 0%

profile of v2, /device:TPU:1, one launch (start us, length us, event | category | flops | bytes accessed | tf_op | source)
XLA Modules:
  0.0 147.2 jit_solution(70819046063122166)
XLA Ops:
  0.6 1.1 convert_element_type.54
  1.8 0.8 pad_bitcast_fusion
  2.6 8.7 %collective-permute-start = (bf16[1024,128]{1,0:T(8,128)(2,1)S(1)}, bf16[1024,128]{1,0:T(8,128)(2,1)S(1)}, u32[]{:S(2)}, u32[]{:S(2)}) collective-permute-start(bf16[1024,128]{1,0:T(8,128)(2,1)S(1)} %get-tuple-element.6), channel_id=1, source_target_pairs={{0,64},{64,0},{1,65},{65,1},{2,66},{66,2},{3,67},{67,3},{4,68},{68... | collective-permute-start | bytes 786440 | tf_op jit(solution)/shard_map/ppermute | solution.py:71
  11.4 0.7 broadcast_subtract_fusion
  12.1 2.1 %fusion.16 = bf16[8,8,8,128]{3,1,2,0:T(8,128)(2,1)S(1)} fusion(bf16[1024,1024]{1,0:T(8,128)(2,1)} %param.7, s32[64]{0:T(128)S(1)} %dynamic_slice.9), kind=kOutput, calls=%fused_computation.21 | convolution fusion | flops 134348800 | bytes 2228480 | tf_op jit(solution)/shard_map/dot_general | solution.py:47
  14.9 12.9 %all-to-all-start = ((bf16[64,8,128]{2,1,0:T(8,128)(2,1)}), bf16[64,8,128]{2,1,0:T(8,128)(2,1)S(1)}, u32[]{:S(2)}, u32[]{:S(2)}) async-start(bf16[64,8,128]{2,1,0:T(8,128)(2,1)} %bitcast.16), calls=%async_computation | async-start | bytes 262144 | tf_op jit(solution)/shard_map/all_to_all | solution.py:13
  28.4 0.8 pad_maximum_fusion
  29.2 3.2 %collective-permute-start.1 = (bf16[2,1024,128]{2,1,0:T(8,128)(2,1)}, bf16[2,1024,128]{2,1,0:T(8,128)(2,1)}, u32[]{:S(2)}, u32[]{:S(2)}) collective-permute-start(bf16[2,1024,128]{2,1,0:T(8,128)(2,1)} %pad_maximum_fusion), channel_id=1, source_target_pairs={{0,128},{128,256},{256,384},{384,0},{1,129},{129,257},{257,385},{3... | collective-permute-start | bytes 1572872 | tf_op jit(solution)/shard_map/ppermute | solution.py:74
  32.5 1.8 %fusion.6 = bf16[1024,512]{0,1:T(8,128)(2,1)} fusion(bf16[512,512]{1,0:T(8,128)(2,1)S(1)} %copy-done, s32[512]{0:T(512)S(1)} %broadcast_subtract_fusion.1), kind=kOutput, calls=%fused_computation.9 | convolution fusion | flops 537919488 | bytes 1574912 | tf_op jit(solution)/shard_map/dot_general | solution.py:47
  34.3 4.5 %collective-permute-start.2 = (bf16[2,1024,128]{2,1,0:T(8,128)(2,1)}, bf16[2,1024,128]{2,1,0:T(8,128)(2,1)}, u32[]{:S(2)}, u32[]{:S(2)}) collective-permute-start(bf16[2,1024,128]{2,1,0:T(8,128)(2,1)} %pad_maximum_fusion), channel_id=1, source_target_pairs={{0,256},{128,384},{256,0},{384,128},{1,257},{129,385},{257,1},{385... | collective-permute-start | bytes 1572872 | tf_op jit(solution)/shard_map/ppermute | solution.py:74
  38.8 3.0 %collective-permute-start.3 = (bf16[2,1024,128]{2,1,0:T(8,128)(2,1)}, bf16[2,1024,128]{2,1,0:T(8,128)(2,1)S(1)}, u32[]{:S(2)}, u32[]{:S(2)}) collective-permute-start(bf16[2,1024,128]{2,1,0:T(8,128)(2,1)} %pad_maximum_fusion), channel_id=1, source_target_pairs={{0,384},{128,0},{256,128},{384,256},{1,385},{129,1},{257,129},{385... | collective-permute-start | bytes 1572872 | tf_op jit(solution)/shard_map/ppermute | solution.py:74
  41.8 0.8 constant_dynamic-update-slice_fusion
  42.5 1.1 all-to-all-done
  44.4 13.4 %all-to-all-start.1 = ((bf16[64,8,128]{2,1,0:T(8,128)(2,1)}), bf16[64,8,128]{2,1,0:T(8,128)(2,1)S(1)}, u32[]{:S(2)}, u32[]{:S(2)}) async-start(bf16[64,8,128]{2,1,0:T(8,128)(2,1)} %broadcast_in_dim.8), calls=%async_computation.1 | async-start | bytes 262144 | tf_op jit(solution)/shard_map/all_to_all | solution.py:13
  57.8 1.7 %fusion.24 = bf16[1024,1024]{1,0:T(8,128)(2,1)} fusion(bf16[1024,1024]{1,0:T(8,128)(2,1)} %constant_dynamic-update-slice_fusion, bf16[2,1024,128]{2,1,0:T(8,128)(2,1)} %collective-permute-done.1), kind=kLoop, calls=%fused_computation.37 | loop fusion | bytes 524288
  59.5 1.7 %fusion.23 = bf16[1024,1024]{1,0:T(8,128)(2,1)} fusion(bf16[1024,1024]{1,0:T(8,128)(2,1)} %fusion.24, bf16[2,1024,128]{2,1,0:T(8,128)(2,1)} %collective-permute-done.1), kind=kLoop, calls=%fused_computation.35 | loop fusion | bytes 524288
  61.2 1.7 %fusion.22 = bf16[1024,1024]{1,0:T(8,128)(2,1)} fusion(bf16[1024,1024]{1,0:T(8,128)(2,1)} %fusion.23, bf16[2,1024,128]{2,1,0:T(8,128)(2,1)} %collective-permute-done.2), kind=kLoop, calls=%fused_computation.33 | loop fusion | bytes 524288
  63.0 1.7 %fusion.21 = bf16[1024,1024]{1,0:T(8,128)(2,1)} fusion(bf16[1024,1024]{1,0:T(8,128)(2,1)} %fusion.22, bf16[2,1024,128]{2,1,0:T(8,128)(2,1)} %collective-permute-done.2), kind=kLoop, calls=%fused_computation.31 | loop fusion | bytes 524288
  64.7 0.7 fusion.20
  65.4 0.7 fusion.19
  66.2 6.6 %all-to-all-done.1 = bf16[64,8,128]{2,1,0:T(8,128)(2,1)S(1)} async-done(((bf16[64,8,128]{2,1,0:T(8,128)(2,1)}), bf16[64,8,128]{2,1,0:T(8,128)(2,1)S(1)}, u32[]{:S(2)}, u32[]{:S(2)}) %all-to-all-start.1) | async-done | bytes 131104 | tf_op jit(solution)/shard_map/all_to_all | solution.py:13
  73.4 0.8 fusion.14
  74.2 2.1 %convolution_convert_fusion = bf16[64,1024]{1,0:T(8,128)(2,1)S(1)} fusion(bf16[64,1024]{1,0:T(8,128)(2,1)S(1)} %fusion.14, bf16[1024,1024]{1,0:T(8,128)(2,1)} %fusion.19), kind=kOutput, calls=%fused_computation.19 | convolution fusion | flops 134283264 | bytes 2359296 | tf_op jit(solution)/shard_map/dot_general | solution.py:47
  76.9 25.8 %all_to_all.25 = bf16[64,12,128]{2,1,0:T(8,128)(2,1)S(1)} all-to-all(bf16[64,12,128]{2,1,0:T(8,128)(2,1)S(1)} %reshape.41), channel_id=1, replica_groups=mesh['y'=4,'core'=2,'z'=16,'x'=4] {'z','x'}, dimensions={0} | all-to-all | bytes 393216 | tf_op jit(solution)/shard_map/all_to_all | solution.py:13
  103.4 5.8 %all-to-all-start.3 = ((bf16[16,12,128]{2,1,0:T(8,128)(2,1)}), bf16[16,12,128]{2,1,0:T(8,128)(2,1)S(1)}, u32[]{:S(2)}, u32[]{:S(2)}) async-start(bf16[16,12,128]{2,1,0:T(8,128)(2,1)} %broadcast_in_dim.9), calls=%async_computation.3 | async-start | bytes 131072 | tf_op jit(solution)/shard_map/all_to_all | solution.py:13
  109.2 11.6 %all-to-all-done.3 = bf16[16,12,128]{2,1,0:T(8,128)(2,1)S(1)} async-done(((bf16[16,12,128]{2,1,0:T(8,128)(2,1)}), bf16[16,12,128]{2,1,0:T(8,128)(2,1)S(1)}, u32[]{:S(2)}, u32[]{:S(2)}) %all-to-all-start.3) | async-done | bytes 49184 | tf_op jit(solution)/shard_map/all_to_all | solution.py:13
  121.0 0.9 broadcast_in_dim.11
  121.9 8.0 %all-to-all-start.4 = ((bf16[32,16,640]{2,1,0:T(8,128)(2,1)}), bf16[32,16,640]{2,1,0:T(8,128)(2,1)S(1)}, u32[]{:S(2)}, u32[]{:S(2)}) async-start(bf16[32,16,640]{2,1,0:T(8,128)(2,1)} %bitcast.11), calls=%async_computation.4 | async-start | bytes 1310720 | tf_op jit(solution)/shard_map/all_to_all | solution.py:13
  129.9 1.2 fusion.5
  131.2 11.4 %all-to-all-done.4 = bf16[32,16,640]{2,1,0:T(8,128)(2,1)S(1)} async-done(((bf16[32,16,640]{2,1,0:T(8,128)(2,1)}), bf16[32,16,640]{2,1,0:T(8,128)(2,1)S(1)}, u32[]{:S(2)}, u32[]{:S(2)}) %all-to-all-start.4) | async-done | bytes 655392 | tf_op jit(solution)/shard_map/all_to_all | solution.py:13
  143.0 1.0 multiply_convert_fusion
  144.5 2.8 %fusion.7 = f32[1024,125]{1,0:T(8,128)} fusion(f32[1024,125]{1,0:T(8,128)S(1)} %copy-done.5, bf16[1024,512]{0,1:T(8,128)(2,1)} %fusion.5, bf16[1024,512]{0,1:T(8,128)(2,1)S(1)} %copy-done.4, bf16[512,125]{1,0:T(8,128)(2,1)S(1)} %get-tuple-element.2, bf16[512,125]{1,0:T(8,128)(2,1)S(1)} %fusion.15), kind=kOutput, calls=%fused_computation.10 | convolution fusion | flops 266978304 | bytes 3377152 | tf_op jit(solution)/shard_map/dot_general | solution.py:47
  (46 shorter events, 4.9 us)
Async XLA Ops:
  0.6 31.8 %copy-start = (bf16[512,512]{1,0:T(8,128)(2,1)S(1)}, bf16[512,512]{1,0:T(8,128)(2,1)}, u32[]{:S(2)}) copy-start(bf16[512,512]{1,0:T(8,128)(2,1)} %param.12) | copy-start | bytes 1572868
  1.8 26.1 %copy-start.1 = (bf16[1024,1024]{1,0:T(8,128)(2,1)S(1)}, bf16[1024,1024]{1,0:T(8,128)(2,1)}, u32[]{:S(2)}) copy-start(bf16[1024,1024]{1,0:T(8,128)(2,1)} %param.7) | copy-start | bytes 6291460
  2.6 25.8 %collective-permute-start = (bf16[1024,128]{1,0:T(8,128)(2,1)S(1)}, bf16[1024,128]{1,0:T(8,128)(2,1)S(1)}, u32[]{:S(2)}, u32[]{:S(2)}) collective-permute-start(bf16[1024,128]{1,0:T(8,128)(2,1)S(1)} %get-tuple-element.6), channel_id=1, source_target_pairs={{0,64},{64,0},{1,65},{65,1},{2,66},{66,2},{3,67},{67,3},{4,68},{68... | collective-permute-start | bytes 786440 | tf_op jit(solution)/shard_map/ppermute | solution.py:71
  14.3 18.2 %copy-start.6 = (s32[512]{0:T(512)S(1)}, s32[512]{0:T(512)}, u32[]{:S(2)}) copy-start(s32[512]{0:T(512)} %param.11) | copy-start | bytes 6148
  14.9 28.7 %all-to-all-start = ((bf16[64,8,128]{2,1,0:T(8,128)(2,1)}), bf16[64,8,128]{2,1,0:T(8,128)(2,1)S(1)}, u32[]{:S(2)}, u32[]{:S(2)}) async-start(bf16[64,8,128]{2,1,0:T(8,128)(2,1)} %bitcast.16), calls=%async_computation | async-start | bytes 262144 | tf_op jit(solution)/shard_map/all_to_all | solution.py:13
  29.2 28.6 %collective-permute-start.1 = (bf16[2,1024,128]{2,1,0:T(8,128)(2,1)}, bf16[2,1024,128]{2,1,0:T(8,128)(2,1)}, u32[]{:S(2)}, u32[]{:S(2)}) collective-permute-start(bf16[2,1024,128]{2,1,0:T(8,128)(2,1)} %pad_maximum_fusion), channel_id=1, source_target_pairs={{0,128},{128,256},{256,384},{384,0},{1,129},{129,257},{257,385},{3... | collective-permute-start | bytes 1572872 | tf_op jit(solution)/shard_map/ppermute | solution.py:74
  34.3 27.0 %collective-permute-start.2 = (bf16[2,1024,128]{2,1,0:T(8,128)(2,1)}, bf16[2,1024,128]{2,1,0:T(8,128)(2,1)}, u32[]{:S(2)}, u32[]{:S(2)}) collective-permute-start(bf16[2,1024,128]{2,1,0:T(8,128)(2,1)} %pad_maximum_fusion), channel_id=1, source_target_pairs={{0,256},{128,384},{256,0},{384,128},{1,257},{129,385},{257,1},{385... | collective-permute-start | bytes 1572872 | tf_op jit(solution)/shard_map/ppermute | solution.py:74
  38.8 25.9 %collective-permute-start.3 = (bf16[2,1024,128]{2,1,0:T(8,128)(2,1)}, bf16[2,1024,128]{2,1,0:T(8,128)(2,1)S(1)}, u32[]{:S(2)}, u32[]{:S(2)}) collective-permute-start(bf16[2,1024,128]{2,1,0:T(8,128)(2,1)} %pad_maximum_fusion), channel_id=1, source_target_pairs={{0,384},{128,0},{256,128},{384,256},{1,385},{129,1},{257,129},{385... | collective-permute-start | bytes 1572872 | tf_op jit(solution)/shard_map/ppermute | solution.py:74
  44.4 28.4 %all-to-all-start.1 = ((bf16[64,8,128]{2,1,0:T(8,128)(2,1)}), bf16[64,8,128]{2,1,0:T(8,128)(2,1)S(1)}, u32[]{:S(2)}, u32[]{:S(2)}) async-start(bf16[64,8,128]{2,1,0:T(8,128)(2,1)} %broadcast_in_dim.8), calls=%async_computation.1 | async-start | bytes 262144 | tf_op jit(solution)/shard_map/all_to_all | solution.py:13
  73.4 2.9 %copy-start.3 = (bf16[1024,512]{0,1:T(8,128)(2,1)S(1)}, bf16[1024,512]{0,1:T(8,128)(2,1)}, u32[]{:S(2)}) copy-start(bf16[1024,512]{0,1:T(8,128)(2,1)} %fusion.6) | copy-start | bytes 3145732
  76.9 53.0 %copy-start.7 = (f32[512]{0:T(512)S(1)}, f32[512]{0:T(512)}, u32[]{:S(2)}) copy-start(f32[512]{0:T(512)} %param.13) | copy-start | bytes 6148
  103.4 17.4 %all-to-all-start.3 = ((bf16[16,12,128]{2,1,0:T(8,128)(2,1)}), bf16[16,12,128]{2,1,0:T(8,128)(2,1)S(1)}, u32[]{:S(2)}, u32[]{:S(2)}) async-start(bf16[16,12,128]{2,1,0:T(8,128)(2,1)} %broadcast_in_dim.9), calls=%async_computation.3 | async-start | bytes 131072 | tf_op jit(solution)/shard_map/all_to_all | solution.py:13
  121.9 20.7 %all-to-all-start.4 = ((bf16[32,16,640]{2,1,0:T(8,128)(2,1)}), bf16[32,16,640]{2,1,0:T(8,128)(2,1)S(1)}, u32[]{:S(2)}, u32[]{:S(2)}) async-start(bf16[32,16,640]{2,1,0:T(8,128)(2,1)} %bitcast.11), calls=%async_computation.4 | async-start | bytes 1310720 | tf_op jit(solution)/shard_map/all_to_all | solution.py:13
  142.6 1.8 %copy-start.4 = (bf16[1024,512]{0,1:T(8,128)(2,1)S(1)}, bf16[1024,512]{0,1:T(8,128)(2,1)}, u32[]{:S(2)}) copy-start(bf16[1024,512]{0,1:T(8,128)(2,1)} %fusion.6) | copy-start | bytes 3145732
  142.6 1.8 %copy-start.5 = (f32[1024,125]{1,0:T(8,128)S(1)}, f32[1024,125]{1,0:T(8,128)}, u32[]{:S(2)}) copy-start(f32[1024,125]{1,0:T(8,128)} %param.8) | copy-start | bytes 1536004
  144.1 3.2 %copy-start.2 = (f32[512,125]{1,0:T(8,128)}, f32[512,125]{1,0:T(8,128)S(1)}, u32[]{:S(2)}) copy-start(f32[512,125]{1,0:T(8,128)S(1)} %get-tuple-element.3) | copy-start | bytes 768004

commit v3 on v2

v3 whole, which is shorter than its diff:
```python
import jax
import jax.numpy as jnp
from jax import lax
from jax.experimental import pallas as pl
from jax.experimental.pallas import tpu as pltpu
from jax.sharding import Mesh, PartitionSpec as P

step_size = 0.5
OUT = ("y", "core")
CTR = ("z", "x")
LANES = 128
ROUND = 3


def exchanged(pieces, axes):
    return lax.all_to_all(pieces, axes, split_axis=0, concat_axis=0, tiled=True)


def copied_to_all(shard, axes):
    return exchanged(jnp.broadcast_to(shard, (lax.axis_size(axes), *shard.shape)), axes)


def one_hot(rows, length):
    return (lax.broadcasted_iota(jnp.int32, (rows.shape[0], length), 1) == rows[:, None]).astype(
        jnp.bfloat16
    )


def one_hot_columns(rows, length):
    return (lax.broadcasted_iota(jnp.int32, (length, rows.shape[0]), 0) == rows[None, :]).astype(
        jnp.bfloat16
    )


def dot(left, right):
    return jnp.dot(left, right, preferred_element_type=jnp.float32)


def by_owner(blocks, dim, name):
    size = lax.axis_size(name)
    back = jnp.concatenate([lax.rev(blocks, (dim,))] * 2, axis=dim)
    return lax.dynamic_slice_in_dim(back, size - 1 - lax.axis_index(name), size, axis=dim)


def products_kernel(feats_ref, centers_ref, norm_ref, mine_ref, other_ref, vecs_ref, out_ref):
    low = jnp.bfloat16
    feats = feats_ref[...]
    wide = feats.astype(jnp.float32)
    left_norm = jnp.sum(wide * wide, axis=1, keepdims=True)
    inner = lax.dot_general(
        feats, centers_ref[...], (((1,), (1,)), ((), ())), preferred_element_type=jnp.float32
    )
    kernel = jnp.exp(
        -(left_norm + norm_ref[...] - 2.0 * inner) * (2.0 / feats.shape[1])
    ).astype(low)
    at = 0
    for blocks in (mine_ref, other_ref):
        for j in range(blocks.shape[0]):
            out_ref[:, at : at + LANES] = dot(kernel, blocks[j]).astype(low)
            at += LANES
    out_ref[:, at:] = dot(kernel, vecs_ref[...]).astype(low)


def products(feats, centers, norm, mine, other, vecs):
    width = (mine.shape[0] + other.shape[0]) * LANES + vecs.shape[1]
    return pl.pallas_call(
        products_kernel,
        out_shape=jax.ShapeDtypeStruct((feats.shape[0], width), jnp.bfloat16),
        in_specs=[pl.BlockSpec(memory_space=pltpu.VMEM)] * 6,
        out_specs=pl.BlockSpec(memory_space=pltpu.VMEM),
        name="products",
    )(feats, centers, norm, mine, other, vecs)


def body(centers, weights, targets, batch_rows, subsample, eigvecs, eig_scale):
    low = jnp.bfloat16
    row_count, feature_count = centers.shape
    nout, nctr = lax.axis_size(OUT), lax.axis_size(CTR)
    nx, nz = lax.axis_size("x"), lax.axis_size("z")
    ny, ncore = lax.axis_size("y"), lax.axis_size("core")
    place, slice_at = lax.axis_index(CTR), lax.axis_index(OUT)
    batch = batch_rows.shape[0]
    columns = weights.shape[1]
    block = batch // nout
    base = place * row_count

    rank = jnp.sum((batch_rows[None, :] < batch_rows[:, None]).astype(jnp.int32), axis=1)
    edges = jnp.arange(nctr, dtype=jnp.int32) * row_count
    start = jnp.sum((batch_rows[None, :] < edges[:, None]).astype(jnp.int32), axis=1)
    stop = jnp.sum((batch_rows[None, :] < edges[:, None] + row_count).astype(jnp.int32), axis=1)
    most = jnp.max(stop - start)
    lead = start + (slice_at - start) % nout
    own_start = jnp.sum((batch_rows < base).astype(jnp.int32))
    own_stop = jnp.sum((batch_rows < base + row_count).astype(jnp.int32))
    own_lead = own_start + (slice_at - own_start) % nout

    def round_of(turn):
        rows = []
        for k in range(ROUND):
            position = own_lead + (turn * ROUND + k) * nout
            row = jnp.sum(jnp.where(rank == position, batch_rows - base, 0))
            row = lax.dynamic_slice(
                centers, (jnp.clip(row, 0, row_count - 1), 0), (1, feature_count)
            )
            rows.append(jnp.where(position < own_stop, row, jnp.zeros_like(row)))
        share = jnp.concatenate(rows).reshape(-1, LANES)
        arrived = copied_to_all(share, CTR).reshape(nctr * ROUND, feature_count)
        steps = turn * ROUND + jnp.arange(ROUND, dtype=jnp.int32)
        positions = lead[:, None] + steps[None, :] * nout
        slots = jnp.where(positions < stop[:, None], positions // nout, -1).reshape(-1)
        return dot(one_hot_columns(slots, block), arrived).astype(low)

    def more(carry):
        return carry[0] * (ROUND * nout) < most

    def next_round(carry):
        return carry[0] + 1, carry[1] + round_of(carry[0])

    feats = round_of(0)
    _, feats = lax.while_loop(more, next_round, (jnp.int32(1), feats))

    weights_low = jnp.pad(weights.astype(low), ((0, 0), (0, LANES - columns)))
    mine = jnp.stack(
        [weights_low]
        + [
            lax.ppermute(weights_low, "y", [(i, (i + dy) % ny) for i in range(ny)])
            for dy in range(1, ny)
        ]
    )
    other = lax.ppermute(mine, "core", [(i, (i + 1) % ncore) for i in range(ncore)])

    sub_vecs = dot(one_hot_columns(subsample - base, row_count), eigvecs).astype(low)
    right_norm = jnp.sum(jnp.square(centers.astype(jnp.float32)), axis=1)
    parts = products(feats, centers, right_norm[None, :], mine, other, sub_vecs)

    blocks = parts.shape[1] // LANES
    arrived = exchanged(parts.reshape(nctr, blocks // 4, 4, LANES), CTR)
    share = arrived.astype(jnp.float32).sum(axis=0).astype(low)
    share = copied_to_all(share, "z").reshape(nz, blocks, LANES)
    heads = jnp.moveaxis(share[:, :nout], 1, 0).reshape(ncore, ny, nz, LANES)
    heads = by_owner(by_owner(heads, 0, "core"), 1, "y")
    heads = jnp.moveaxis(heads, 0, 1).reshape(nout, nz, LANES)
    tails = share[:, nout:].reshape(nz, -1)
    pieces = jnp.concatenate([heads, jnp.broadcast_to(tails, (nout, *tails.shape))], axis=2)
    pieces = jnp.broadcast_to(pieces[:, None], (nout, nx, *pieces.shape[1:]))
    arrived = exchanged(pieces.reshape(nout * nx, *pieces.shape[2:]), (*OUT, "x"))
    arrived = arrived.reshape(batch, -1)

    slot = rank // nout
    line = (rank % nout) * block + (slot % nx) * nz + slot // nx
    to_batch = one_hot(line, batch)
    line_rows = jnp.sum(
        jnp.where(
            lax.broadcasted_iota(jnp.int32, (batch, batch), 0) == line[None, :],
            batch_rows[None, :],
            0,
        ),
        axis=1,
    )
    line_targets = lax.dot_general(
        to_batch.astype(jnp.float32),
        targets,
        (((0,), (0,)), ((), ())),
        precision=lax.Precision.HIGHEST,
    )
    spread = jnp.concatenate([sub_vecs, one_hot_columns(line_rows - base, row_count)], axis=1)

    line_prediction = arrived[:, :columns]
    line_residual = line_prediction.astype(jnp.float32) - line_targets
    coefficient = lax.dot_general(
        arrived[:, LANES:],
        line_residual.astype(low),
        (((0,), (0,)), ((), ())),
        preferred_element_type=jnp.float32,
    )
    changes = jnp.concatenate(
        [
            (step_size * eig_scale[:, None] * coefficient).astype(low),
            (-step_size * line_residual).astype(low),
        ]
    )
    updated = weights + dot(spread, changes)
    residual = dot(to_batch, line_prediction) - targets
    return (updated, residual)


def solution(mesh):
    axes = ("y", "core", "z", "x")
    fine = Mesh(mesh.devices.reshape(4, 2, 16, 4), axes)
    placed = (P(CTR, None), P(CTR, OUT), P(None, OUT), P(), P(CTR), P(CTR, None), P())
    return jax.shard_map(
        body,
        mesh=fine,
        in_specs=placed,
        out_specs=(P(CTR, OUT), P(None, OUT)),
        check_vma=False,
    )
```

time: 148 us -> 143 us (0.966)
  starting transfers between devices: 59.6 us -> 46.4 us
  local copies, waits for them, and re-layouts: 13.6 us -> 4.74 us
  other arithmetic: 6.21 us -> 13.4 us
  waiting for transfers between devices: 30.8 us -> 35.9 us
  between operations: 0.99 us -> 5.81 us
  matrix products: 10.3 us -> 5.93 us
  Pallas kernels: 0 us -> 3.9 us
    unnamed x24 -> x18, local copies, waits for them, and re-layouts: 9.08 us -> 0.05 us
    all_to_all x4 -> x3, starting transfers between devices: 40.1 us -> 31.1 us  [exchanged(): return lax.all_to_all(pieces, axes, split_axis=0, concat_axis=0, tiled=True)]
    all_to_all x4 -> x3, waiting for transfers between devices: 30.8 us -> 35.9 us  [exchanged(): return lax.all_to_all(pieces, axes, split_axis=0, concat_axis=0, tiled=True)]
    reduce_sum x3 -> x6, other arithmetic: 0.71 us -> 5.48 us  [the longest x1 1.98 us: round_of(): row = jnp.sum(jnp.where(rank == position, batch_rows - base, 0))]
    dot_general x5 -> x4, matrix products: 9.19 us -> 4.49 us  [dot(): return jnp.dot(left, right, preferred_element_type=jnp.float32)]
    ppermute x4, starting transfers between devices: 19.4 us -> 15.2 us  [the longest x3 11.5 us: body(): lax.ppermute(weights_low, 'y', [(i, (i + dy) % ny) for i in range(ny)])]
    pallas_call x0 -> x1, Pallas kernels: none -> 3.9 us  [products(): pl.pallas_call(products_kernel, out_shape=jax.ShapeDtypeStruct((feats.sha...]
  transfers between devices with their start and end apart: 8 -> 7, of which waited for: 4 -> 3; matrix products, arithmetic and copies ran while one was open for 12% -> 11% of each run, Pallas kernels for 0% -> 0%
where the time goes in v3:
time: 143 us; the launch traced here: 142 us
  starting transfers between devices  46.4 us (32%)
  waiting for transfers between devices  35.9 us (25%)
  blocking collectives  25.2 us (18%)
  other arithmetic  13.4 us (9%)
  matrix products  5.93 us (4%)
  between operations  5.81 us (4%)
  local copies, waits for them, and re-layouts  4.74 us (3%)
  Pallas kernels  3.9 us (3%)
    all_to_all x3, waiting for transfers between devices, exchanged(): return lax.all_to_all(pieces, axes, split_axis=0, concat_axis=0, tiled=True)  35.9 us
    all_to_all x3, starting transfers between devices, exchanged(): return lax.all_to_all(pieces, axes, split_axis=0, concat_axis=0, tiled=True)  31.1 us
    all_to_all x1, blocking collectives, exchanged(): return lax.all_to_all(pieces, axes, split_axis=0, concat_axis=0, tiled=True)  25.2 us
    ppermute x3, starting transfers between devices, body(): lax.ppermute(weights_low, 'y', [(i, (i + dy) % ny) for i in range(ny)])  11.5 us
    dot_general x4, matrix products, dot(): return jnp.dot(left, right, preferred_element_type=jnp.float32)  4.49 us
    pallas_call x1, Pallas kernels, products(): pl.pallas_call(products_kernel, out_shape=jax.ShapeDtypeStruct((feats.sha...  3.9 us
    ppermute x1, starting transfers between devices, body(): lax.ppermute(mine, 'core', [(i, (i + 1) % ncore) for i in range(ncore)])  3.69 us
  transfers between devices with their start and end apart: 7, of which 3 were waited for; matrix products, arithmetic and copies ran while one was open for 11% of the time, Pallas kernels for 0%

profile of v3, /device:TPU:1, one launch (start us, length us, event | category | flops | bytes accessed | tf_op | source)
XLA Modules:
  0.0 141.9 jit_solution(5845184391240051439)
XLA Ops:
  0.6 1.1 convert_element_type.66
  1.8 0.8 pad_bitcast_fusion
  2.6 4.0 %collective-permute-start = (bf16[1024,128]{1,0:T(8,128)(2,1)}, bf16[1024,128]{1,0:T(8,128)(2,1)}, u32[]{:S(2)}, u32[]{:S(2)}) collective-permute-start(bf16[1024,128]{1,0:T(8,128)(2,1)} %get-tuple-element.183), channel_id=1, source_target_pairs={{0,128},{128,256},{256,384},{384,0},{1,129},{129,257},{257,385},{3... | collective-permute-start | bytes 786440 | tf_op jit(solution)/shard_map/ppermute | solution.py:126
  6.6 4.5 %collective-permute-start.1 = (bf16[1024,128]{1,0:T(8,128)(2,1)}, bf16[1024,128]{1,0:T(8,128)(2,1)}, u32[]{:S(2)}, u32[]{:S(2)}) collective-permute-start(bf16[1024,128]{1,0:T(8,128)(2,1)} %get-tuple-element.183), channel_id=1, source_target_pairs={{0,256},{128,384},{256,0},{384,128},{1,257},{129,385},{257,1},{385... | collective-permute-start | bytes 786440 | tf_op jit(solution)/shard_map/ppermute | solution.py:126
  11.1 3.0 %collective-permute-start.2 = (bf16[1024,128]{1,0:T(8,128)(2,1)}, bf16[1024,128]{1,0:T(8,128)(2,1)}, u32[]{:S(2)}, u32[]{:S(2)}) collective-permute-start(bf16[1024,128]{1,0:T(8,128)(2,1)} %get-tuple-element.183), channel_id=1, source_target_pairs={{0,384},{128,0},{256,128},{384,256},{1,385},{129,1},{257,129},{385... | collective-permute-start | bytes 786440 | tf_op jit(solution)/shard_map/ppermute | solution.py:126
  14.1 1.3 convert_reduce_fusion.4
  16.1 1.0 convert_reduce_fusion
  17.8 2.0 %select_reduce_fusion.6 = (s32[]{:T(128)}, s32[]{:T(128)}, s32[]{:T(128)}, s32[]{:T(128)}, s32[512]{0:T(512)}) fusion(s32[512]{0:T(512)S(1)} %convert_reduce_fusion, s32[512]{0:T(512)} %param.12, s32[]{:T(128)} %add.259, s32[]{:T(128)} %mul.125, s32[]{:T(128)S(6)} %add.261, s32[]{:T(128)S(6)} %add.262, s32[]{:T(128)S(6)} %add.260), kind=kLoop, calls=%fused_computation.86 | loop fusion | flops 28156 | bytes 6180 | tf_op jit(solution)/shard_map/reduce_sum | solution.py:101
  23.3 0.8 broadcast_select_fusion.5
  24.1 0.9 convert_reduce_fusion.1
  25.0 0.8 broadcast_in_dim.70
  25.8 18.3 %all-to-all-start.1 = ((bf16[64,24,128]{2,1,0:T(8,128)(2,1)}), bf16[64,24,128]{2,1,0:T(8,128)(2,1)S(1)}, u32[]{:S(2)}, u32[]{:S(2)}) async-start(bf16[64,24,128]{2,1,0:T(8,128)(2,1)} %broadcast_in_dim.70), calls=%async_computation.1 | async-start | bytes 786432 | tf_op jit(solution)/shard_map/all_to_all | solution.py:16
  44.1 1.3 subtract_reduce_fusion
  45.4 0.7 broadcast_add_fusion.1
  46.5 2.3 %pad_maximum_fusion.1.mine_ref = bf16[4,1024,128]{2,1,0:T(8,128)(2,1)} fusion(bf16[1,1024,128]{2,1,0:T(8,128)(2,1)} %bitcast.4, bf16[1,1024,128]{2,1,0:T(8,128)(2,1)} %bitcast.3, bf16[1,1024,128]{2,1,0:T(8,128)(2,1)} %bitcast.2, bf16[1,1024,128]{2,1,0:T(8,128)(2,1)S(1)} %get-tuple-element.182), kind=kLoop, calls=%fused_computation.34 | loop fusion | flops 1572864 | bytes 2097152 | tf_op jit(solution)/shard_map/stack | solution.py:123
  48.8 3.7 %collective-permute-start.3 = (bf16[4,1024,128]{2,1,0:T(8,128)(2,1)}, bf16[4,1024,128]{2,1,0:T(8,128)(2,1)}, u32[]{:S(2)}, u32[]{:S(2)}) collective-permute-start(bf16[4,1024,128]{2,1,0:T(8,128)(2,1)} %pad_maximum_fusion.1.mine_ref), channel_id=1, source_target_pairs={{0,64},{64,0},{1,65},{65,1},{2,66},{66,2},{3,67},{67,3},{4,68},{68... | collective-permute-start | bytes 3145736 | tf_op jit(solution)/shard_map/ppermute | solution.py:130
  52.6 1.1 multiply_reduce_fusion
  53.6 1.7 %fusion.8.vecs_ref = bf16[1024,512]{1,0:T(8,128)(2,1)} fusion(bf16[512,512]{1,0:T(8,128)(2,1)S(1)} %copy-done, s32[512]{0:T(512)S(1)} %broadcast_subtract_fusion.1), kind=kOutput, calls=%fused_computation.27 | convolution fusion | flops 537919488 | bytes 1574912 | tf_op jit(solution)/shard_map/dot_general | solution.py:36
  55.3 12.4 %all-to-all-done.1 = bf16[64,24,128]{2,1,0:T(8,128)(2,1)S(1)} async-done(((bf16[64,24,128]{2,1,0:T(8,128)(2,1)}), bf16[64,24,128]{2,1,0:T(8,128)(2,1)S(1)}, u32[]{:S(2)}, u32[]{:S(2)}) %all-to-all-start.1) | async-done | bytes 393248 | tf_op jit(solution)/shard_map/all_to_all | solution.py:16
  68.1 0.7 while.12
  68.8 3.9 %products.1 = bf16[64,1536]{1,0:T(8,128)(2,1)} custom-call(bf16[64,1024]{1,0:T(8,128)(2,1)S(1)} %get-tuple-element.144.feats_ref, bf16[1024,1024]{1,0:T(8,128)(2,1)S(1)} %get-tuple-element.328, f32[1,1024]{1,0:T(1,128)} %bitcast.34, bf16[4,1024,128]{2,1,0:T(8,128)(2,1)} %pad_maximum_fusion.1.mine_ref, ...), custom_call_target="tpu_custom_call" | custom-call | tf_op jit(solution)/shard_map/products/pallas_call | solution.py:66
  72.7 1.0 reshape.291
  73.7 25.2 %all_to_all.29 = bf16[64,3,4,128]{3,2,1,0:T(4,128)(2,1)S(1)} all-to-all(bf16[64,3,4,128]{3,2,1,0:T(4,128)(2,1)S(1)} %reshape.291), channel_id=1, replica_groups=mesh['y'=4,'core'=2,'z'=16,'x'=4] {'z','x'}, dimensions={0} | all-to-all | bytes 393216 | tf_op jit(solution)/shard_map/all_to_all | solution.py:16
  99.0 0.6 broadcast_in_dim.72
  99.6 5.0 %all-to-all-start.3 = ((bf16[16,3,4,128]{3,2,1,0:T(4,128)(2,1)}), bf16[16,3,4,128]{3,2,1,0:T(4,128)(2,1)S(1)}, u32[]{:S(2)}, u32[]{:S(2)}) async-start(bf16[16,3,4,128]{3,2,1,0:T(4,128)(2,1)} %broadcast_in_dim.72), calls=%async_computation.3 | async-start | bytes 98304 | tf_op jit(solution)/shard_map/all_to_all | solution.py:16
  104.7 11.5 %all-to-all-done.3 = bf16[16,3,4,128]{3,2,1,0:T(4,128)(2,1)S(1)} async-done(((bf16[16,3,4,128]{3,2,1,0:T(4,128)(2,1)}), bf16[16,3,4,128]{3,2,1,0:T(4,128)(2,1)S(1)}, u32[]{:S(2)}, u32[]{:S(2)}) %all-to-all-start.3) | async-done | bytes 49184 | tf_op jit(solution)/shard_map/all_to_all | solution.py:16
  116.4 0.9 broadcast_in_dim.74
  117.3 7.9 %all-to-all-start.4 = ((bf16[32,16,640]{2,1,0:T(8,128)(2,1)}), bf16[32,16,640]{2,1,0:T(8,128)(2,1)S(1)}, u32[]{:S(2)}, u32[]{:S(2)}) async-start(bf16[32,16,640]{2,1,0:T(8,128)(2,1)} %bitcast.10), calls=%async_computation.4 | async-start | bytes 1310720 | tf_op jit(solution)/shard_map/all_to_all | solution.py:16
  125.9 12.0 %all-to-all-done.4 = bf16[32,16,640]{2,1,0:T(8,128)(2,1)S(1)} async-done(((bf16[32,16,640]{2,1,0:T(8,128)(2,1)}), bf16[32,16,640]{2,1,0:T(8,128)(2,1)S(1)}, u32[]{:S(2)}, u32[]{:S(2)}) %all-to-all-start.4) | async-done | bytes 655392 | tf_op jit(solution)/shard_map/all_to_all | solution.py:16
  137.9 1.1 multiply_convert_fusion
  139.0 1.1 convolution_subtract_fusion
  140.4 1.5 %fusion.9 = f32[1024,125]{1,0:T(8,128)} fusion(f32[1024,125]{1,0:T(8,128)S(1)} %copy-done.3, bf16[1024,512]{1,0:T(8,128)(2,1)S(1)} %fusion.7, bf16[1024,512]{1,0:T(8,128)(2,1)S(1)} %copy-done.2, bf16[512,125]{1,0:T(8,128)(2,1)S(1)} %get-tuple-element.187, bf16[512,125]{1,0:T(8,128)(2,1)S(1)} %fusion.12), kind=kOutput, calls=%fused_computation.28 | convolution fusion | flops 266978304 | bytes 3377152 | tf_op jit(solution)/shard_map/dot_general | solution.py:36
  (49 shorter events, 2.1 us)
Async XLA Ops:
  0.6 53.0 %copy-start = (bf16[512,512]{1,0:T(8,128)(2,1)S(1)}, bf16[512,512]{1,0:T(8,128)(2,1)}, u32[]{:S(2)}) copy-start(bf16[512,512]{1,0:T(8,128)(2,1)} %param.14) | copy-start | bytes 1572868
  1.8 50.7 %copy-start.7 = (s32[512]{0:T(512)S(1)}, s32[512]{0:T(512)}, u32[]{:S(2)}) copy-start(s32[512]{0:T(512)} %param.13) | copy-start | bytes 6148
  1.8 50.8 %copy-start.1 = (bf16[1024,1024]{1,0:T(8,128)(2,1)S(1)}, bf16[1024,1024]{1,0:T(8,128)(2,1)}, u32[]{:S(2)}) copy-start(bf16[1024,1024]{1,0:T(8,128)(2,1)} %centers_ref.1) | copy-start | bytes 6291460
  2.6 43.9 %collective-permute-start = (bf16[1024,128]{1,0:T(8,128)(2,1)}, bf16[1024,128]{1,0:T(8,128)(2,1)}, u32[]{:S(2)}, u32[]{:S(2)}) collective-permute-start(bf16[1024,128]{1,0:T(8,128)(2,1)} %get-tuple-element.183), channel_id=1, source_target_pairs={{0,128},{128,256},{256,384},{384,0},{1,129},{129,257},{257,385},{3... | collective-permute-start | bytes 786440 | tf_op jit(solution)/shard_map/ppermute | solution.py:126
  6.6 39.9 %collective-permute-start.1 = (bf16[1024,128]{1,0:T(8,128)(2,1)}, bf16[1024,128]{1,0:T(8,128)(2,1)}, u32[]{:S(2)}, u32[]{:S(2)}) collective-permute-start(bf16[1024,128]{1,0:T(8,128)(2,1)} %get-tuple-element.183), channel_id=1, source_target_pairs={{0,256},{128,384},{256,0},{384,128},{1,257},{129,385},{257,1},{385... | collective-permute-start | bytes 786440 | tf_op jit(solution)/shard_map/ppermute | solution.py:126
  11.1 35.4 %collective-permute-start.2 = (bf16[1024,128]{1,0:T(8,128)(2,1)}, bf16[1024,128]{1,0:T(8,128)(2,1)}, u32[]{:S(2)}, u32[]{:S(2)}) collective-permute-start(bf16[1024,128]{1,0:T(8,128)(2,1)} %get-tuple-element.183), channel_id=1, source_target_pairs={{0,384},{128,0},{256,128},{384,256},{1,385},{129,1},{257,129},{385... | collective-permute-start | bytes 786440 | tf_op jit(solution)/shard_map/ppermute | solution.py:126
  25.8 41.9 %all-to-all-start.1 = ((bf16[64,24,128]{2,1,0:T(8,128)(2,1)}), bf16[64,24,128]{2,1,0:T(8,128)(2,1)S(1)}, u32[]{:S(2)}, u32[]{:S(2)}) async-start(bf16[64,24,128]{2,1,0:T(8,128)(2,1)} %broadcast_in_dim.70), calls=%async_computation.1 | async-start | bytes 786432 | tf_op jit(solution)/shard_map/all_to_all | solution.py:16
  48.8 19.3 %collective-permute-start.3 = (bf16[4,1024,128]{2,1,0:T(8,128)(2,1)}, bf16[4,1024,128]{2,1,0:T(8,128)(2,1)}, u32[]{:S(2)}, u32[]{:S(2)}) collective-permute-start(bf16[4,1024,128]{2,1,0:T(8,128)(2,1)} %pad_maximum_fusion.1.mine_ref), channel_id=1, source_target_pairs={{0,64},{64,0},{1,65},{65,1},{2,66},{66,2},{3,67},{67,3},{4,68},{68... | collective-permute-start | bytes 3145736 | tf_op jit(solution)/shard_map/ppermute | solution.py:130
  53.6 14.5 %copy-start.5 = (s32[512]{0:T(512)S(1)}, s32[512]{0:T(512)}, u32[]{:S(2)}) copy-start(s32[512]{0:T(512)} %param.12) | copy-start | bytes 6148
  72.7 52.5 %copy-start.8 = (f32[512]{0:T(512)S(1)}, f32[512]{0:T(512)}, u32[]{:S(2)}) copy-start(f32[512]{0:T(512)} %param.15) | copy-start | bytes 6148
  72.7 52.5 %copy-start.6 = (s32[512]{0:T(512)S(1)}, s32[512]{0:T(512)}, u32[]{:S(2)}) copy-start(s32[512]{0:T(512)} %get-tuple-element.184) | copy-start | bytes 6148
  99.6 16.5 %all-to-all-start.3 = ((bf16[16,3,4,128]{3,2,1,0:T(4,128)(2,1)}), bf16[16,3,4,128]{3,2,1,0:T(4,128)(2,1)S(1)}, u32[]{:S(2)}, u32[]{:S(2)}) async-start(bf16[16,3,4,128]{3,2,1,0:T(4,128)(2,1)} %broadcast_in_dim.72), calls=%async_computation.3 | async-start | bytes 98304 | tf_op jit(solution)/shard_map/all_to_all | solution.py:16
  104.6 33.2 %copy-start.4 = (f32[512,125]{1,0:T(8,128)S(1)}, f32[512,125]{1,0:T(8,128)}, u32[]{:S(2)}) copy-start(f32[512,125]{1,0:T(8,128)} %param.11) | copy-start | bytes 768004
  117.3 23.1 %copy-start.2 = (bf16[1024,512]{1,0:T(8,128)(2,1)S(1)}, bf16[1024,512]{1,0:T(8,128)(2,1)}, u32[]{:S(2)}) copy-start(bf16[1024,512]{1,0:T(8,128)(2,1)} %fusion.8.vecs_ref) | copy-start | bytes 3145732
  117.3 20.6 %all-to-all-start.4 = ((bf16[32,16,640]{2,1,0:T(8,128)(2,1)}), bf16[32,16,640]{2,1,0:T(8,128)(2,1)S(1)}, u32[]{:S(2)}, u32[]{:S(2)}) async-start(bf16[32,16,640]{2,1,0:T(8,128)(2,1)} %bitcast.10), calls=%async_computation.4 | async-start | bytes 1310720 | tf_op jit(solution)/shard_map/all_to_all | solution.py:16
  137.9 2.5 %copy-start.3 = (f32[1024,125]{1,0:T(8,128)S(1)}, f32[1024,125]{1,0:T(8,128)}, u32[]{:S(2)}) copy-start(f32[1024,125]{1,0:T(8,128)} %param.10) | copy-start | bytes 1536004

commit v4 on v3

--- a/solution.py
+++ b/solution.py
@@ -1,3 +1,4 @@
+import functools
 import jax
 import jax.numpy as jnp
 from jax import lax
@@ -42,7 +43,62 @@
     return lax.dynamic_slice_in_dim(back, size - 1 - lax.axis_index(name), size, axis=dim)
 
 
-def products_kernel(feats_ref, centers_ref, norm_ref, mine_ref, other_ref, vecs_ref, out_ref):
+def whole(kernel, shape, count):
+    vmem = pl.BlockSpec(memory_space=pltpu.VMEM)
+    return pl.pallas_call(
+        kernel,
+        out_shape=shape,
+        in_specs=[pl.BlockSpec(memory_space=pltpu.SMEM)] + [vmem] * count,
+        out_specs=vmem,
+        compiler_params=pltpu.CompilerParams(vmem_limit_bytes=12 << 20),
+    )
+
+
+def rows_below(rows, edge):
+    return jnp.sum((rows < edge).astype(jnp.float32), axis=1, keepdims=True).astype(jnp.int32)
+
+
+def pick_kernel(at_ref, rows_ref, centers_ref, out_ref):
+    count = centers_ref.shape[0]
+    base, slice_at, step, nout = at_ref[0] * count, at_ref[1], at_ref[2], at_ref[3]
+    rows = rows_ref[...]
+    here = lax.broadcasted_iota(jnp.int32, (count, 1), 0) + base
+    start = rows_below(rows, jnp.full((1, 1), base, jnp.int32))
+    lead = start + ((slice_at - start) & (nout - 1))
+    held = jnp.sum((rows == here).astype(jnp.float32), axis=1, keepdims=True) > 0
+    position = jnp.where(held, rows_below(rows, here), -1)
+    steps = lax.broadcasted_iota(jnp.int32, (1, LANES), 1)
+    wanted = jnp.where(steps < ROUND, lead + (steps + step) * nout, -2)
+    pick = (position == wanted).astype(jnp.float32).astype(jnp.bfloat16)
+    found = lax.dot_general(
+        pick, centers_ref[...], (((0,), (0,)), ((), ())), preferred_element_type=jnp.float32
+    )
+    out_ref[...] = found[: out_ref.shape[0]].astype(jnp.bfloat16)
+
+
+def slot_kernel(at_ref, rows_ref, arrived_ref, out_ref, *, count):
+    slice_at, step, nout = at_ref[1], at_ref[2], at_ref[3]
+    rows = rows_ref[...]
+    line = lax.broadcasted_iota(jnp.int32, (arrived_ref.shape[0], 1), 0)
+    scale = (1 << 16) // ROUND + 1
+    place = (line * scale) >> 16
+    start = rows_below(rows, place * count)
+    stop = rows_below(rows, place * count + count)
+    lead = start + ((slice_at - start) & (nout - 1))
+    position = lead + (line - place * ROUND + step) * nout
+    slots = lax.broadcasted_iota(jnp.int32, (1, LANES), 1) * nout + slice_at
+    fits = (jnp.where(position < stop, position, -1) == slots).astype(jnp.float32)
+    feats = lax.dot_general(
+        fits.astype(jnp.bfloat16),
+        arrived_ref[...],
+        (((0,), (0,)), ((), ())),
+        preferred_element_type=jnp.float32,
+    )
+    out_ref[...] = feats[: out_ref.shape[0]].astype(jnp.bfloat16)
+
+
+def products_kernel(at_ref, feats_ref, centers_ref, norm_ref, mine_ref, other_ref, vecs_ref, out_ref):
+    del at_ref
     low = jnp.bfloat16
     feats = feats_ref[...]
     wide = feats.astype(jnp.float32)
@@ -61,15 +117,12 @@
     out_ref[:, at:] = dot(kernel, vecs_ref[...]).astype(low)
 
 
-def products(feats, centers, norm, mine, other, vecs):
+def products(at, feats, centers, norm, mine, other, vecs):
     width = (mine.shape[0] + other.shape[0]) * LANES + vecs.shape[1]
-    return pl.pallas_call(
-        products_kernel,
-        out_shape=jax.ShapeDtypeStruct((feats.shape[0], width), jnp.bfloat16),
-        in_specs=[pl.BlockSpec(memory_space=pltpu.VMEM)] * 6,
-        out_specs=pl.BlockSpec(memory_space=pltpu.VMEM),
-        name="products",
-    )(feats, centers, norm, mine, other, vecs)
+    shape = jax.ShapeDtypeStruct((feats.shape[0], width), jnp.bfloat16)
+    return whole(products_kernel, shape, 6)(
+        at, feats, centers, norm, mine, other, vecs
+    )
 
 
 def body(centers, weights, targets, batch_rows, subsample, eigvecs, eig_scale):
@@ -84,31 +137,23 @@
     block = batch // nout
     base = place * row_count
 
-    rank = jnp.sum((batch_rows[None, :] < batch_rows[:, None]).astype(jnp.int32), axis=1)
-    edges = jnp.arange(nctr, dtype=jnp.int32) * row_count
-    start = jnp.sum((batch_rows[None, :] < edges[:, None]).astype(jnp.int32), axis=1)
-    stop = jnp.sum((batch_rows[None, :] < edges[:, None] + row_count).astype(jnp.int32), axis=1)
-    most = jnp.max(stop - start)
-    lead = start + (slice_at - start) % nout
-    own_start = jnp.sum((batch_rows < base).astype(jnp.int32))
-    own_stop = jnp.sum((batch_rows < base + row_count).astype(jnp.int32))
-    own_lead = own_start + (slice_at - own_start) % nout
+    edges = jnp.arange(nctr, dtype=jnp.int32)[:, None] * row_count
+    owned = (batch_rows[None, :] >= edges) & (batch_rows[None, :] < edges + row_count)
+    most = jnp.max(jnp.sum(owned.astype(jnp.int32), axis=1))
+    batch_line = batch_rows[None, :]
+
+    def places(turn):
+        return jnp.stack([place, slice_at, jnp.int32(turn * ROUND), jnp.int32(nout)])
 
     def round_of(turn):
-        rows = []
-        for k in range(ROUND):
-            position = own_lead + (turn * ROUND + k) * nout
-            row = jnp.sum(jnp.where(rank == position, batch_rows - base, 0))
-            row = lax.dynamic_slice(
-                centers, (jnp.clip(row, 0, row_count - 1), 0), (1, feature_count)
-            )
-            rows.append(jnp.where(position < own_stop, row, jnp.zeros_like(row)))
-        share = jnp.concatenate(rows).reshape(-1, LANES)
-        arrived = copied_to_all(share, CTR).reshape(nctr * ROUND, feature_count)
-        steps = turn * ROUND + jnp.arange(ROUND, dtype=jnp.int32)
-        positions = lead[:, None] + steps[None, :] * nout
-        slots = jnp.where(positions < stop[:, None], positions // nout, -1).reshape(-1)
-        return dot(one_hot_columns(slots, block), arrived).astype(low)
+        at = places(turn)
+        shape = jax.ShapeDtypeStruct((ROUND, feature_count), low)
+        share = whole(pick_kernel, shape, 2)(at, batch_line, centers)
+        arrived = copied_to_all(share.reshape(-1, LANES), CTR)
+        arrived = arrived.reshape(nctr * ROUND, feature_count)
+        shape = jax.ShapeDtypeStruct((block, feature_count), low)
+        slot = functools.partial(slot_kernel, count=row_count)
+        return whole(slot, shape, 2)(at, batch_line, arrived)
 
     def more(carry):
         return carry[0] * (ROUND * nout) < most
@@ -131,7 +176,7 @@
 
     sub_vecs = dot(one_hot_columns(subsample - base, row_count), eigvecs).astype(low)
     right_norm = jnp.sum(jnp.square(centers.astype(jnp.float32)), axis=1)
-    parts = products(feats, centers, right_norm[None, :], mine, other, sub_vecs)
+    parts = products(places(0), feats, centers, right_norm[None, :], mine, other, sub_vecs)
 
     blocks = parts.shape[1] // LANES
     arrived = exchanged(parts.reshape(nctr, blocks // 4, 4, LANES), CTR)
@@ -146,6 +191,7 @@
     arrived = exchanged(pieces.reshape(nout * nx, *pieces.shape[2:]), (*OUT, "x"))
     arrived = arrived.reshape(batch, -1)
 
+    rank = jnp.sum((batch_rows[None, :] < batch_rows[:, None]).astype(jnp.int32), axis=1)
     slot = rank // nout
     line = (rank % nout) * block + (slot % nx) * nz + slot // nx
     to_batch = one_hot(line, batch)
@@ -163,7 +209,9 @@
         (((0,), (0,)), ((), ())),
         precision=lax.Precision.HIGHEST,
     )
-    spread = jnp.concatenate([sub_vecs, one_hot_columns(line_rows - base, row_count)], axis=1)
+    batch_spread = one_hot_columns(line_rows - base, row_count)
+    line_targets, batch_spread = lax.optimization_barrier((line_targets, batch_spread))
+    spread = jnp.concatenate([sub_vecs, batch_spread], axis=1)
 
     line_prediction = arrived[:, :columns]
     line_residual = line_prediction.astype(jnp.float32) - line_targets

time: 143 us -> 133 us (0.930)
  blocking collectives: 25.2 us -> 0 us
  starting transfers between devices: 46.4 us -> 59.7 us
  waiting for transfers between devices: 35.9 us -> 48.6 us
  other arithmetic: 13.4 us -> 5.26 us
  between operations: 5.81 us -> 1.01 us
  Pallas kernels: 3.9 us -> 6.91 us
    all_to_all x1 -> x0, blocking collectives: 25.2 us -> none  [exchanged(): return lax.all_to_all(pieces, axes, split_axis=0, concat_axis=0, tiled=True)]
    all_to_all x3 -> x4, starting transfers between devices: 31.1 us -> 44.6 us  [exchanged(): return lax.all_to_all(pieces, axes, split_axis=0, concat_axis=0, tiled=True)]
    ppermute x3, waiting for transfers between devices: 0.01 us -> 8.88 us  [body(): lax.ppermute(weights_low, 'y', [(i, (i + dy) % ny) for i in range(ny)])]
    reduce_sum x3 -> x1, other arithmetic: 4.17 us -> 0.18 us  [body(): most = jnp.max(jnp.sum(owned.astype(jnp.int32), axis=1))]
    all_to_all x3 -> x4, waiting for transfers between devices: 35.9 us -> 39.7 us  [exchanged(): return lax.all_to_all(pieces, axes, split_axis=0, concat_axis=0, tiled=True)]
    pallas_call x1 -> x3, Pallas kernels: 3.9 us -> 6.91 us  [the longest x1 3.26 us: products(): whole(products_kernel, shape, 6)]
    another operation x1, other arithmetic: 2.28 us -> 0.13 us  [body(): jnp.stack([weights_low] + [lax.ppermute(weights_low, 'y', [(i, (i + dy) %...]
    dot_general x4 -> x3, matrix products: 4.49 us -> 3.31 us  [dot(): return jnp.dot(left, right, preferred_element_type=jnp.float32)]
  transfers between devices with their start and end apart: 7 -> 8, of which waited for: 3 -> 5; matrix products, arithmetic and copies ran while one was open for 11% -> 5% of each run, Pallas kernels for 0% -> 1%
where the time goes in v4:
time: 133 us; the launch traced here: 132 us
  starting transfers between devices  59.7 us (45%)
  waiting for transfers between devices  48.6 us (37%)
  Pallas kernels  6.91 us (5%)
  matrix products  6.41 us (5%)
  other arithmetic  5.26 us (4%)
  local copies, waits for them, and re-layouts  3.41 us (3%)
    all_to_all x4, starting transfers between devices, exchanged(): return lax.all_to_all(pieces, axes, split_axis=0, concat_axis=0, tiled=True)  44.6 us
    all_to_all x4, waiting for transfers between devices, exchanged(): return lax.all_to_all(pieces, axes, split_axis=0, concat_axis=0, tiled=True)  39.7 us
    ppermute x3, starting transfers between devices, body(): lax.ppermute(weights_low, 'y', [(i, (i + dy) % ny) for i in range(ny)])  10.1 us
    ppermute x3, waiting for transfers between devices, body(): lax.ppermute(weights_low, 'y', [(i, (i + dy) % ny) for i in range(ny)])  8.88 us
    ppermute x1, starting transfers between devices, body(): lax.ppermute(mine, 'core', [(i, (i + 1) % ncore) for i in range(ncore)])  4.99 us
    dot_general x3, matrix products, dot(): return jnp.dot(left, right, preferred_element_type=jnp.float32)  3.31 us
    pallas_call x1, Pallas kernels, products(): whole(products_kernel, shape, 6)  3.26 us
    pallas_call x1, Pallas kernels, round_of(): share = whole(pick_kernel, shape, 2)(at, batch_line, centers)  2.71 us
  transfers between devices with their start and end apart: 8, of which 5 were waited for; matrix products, arithmetic and copies ran while one was open for 5% of the time, Pallas kernels for 1%

profile of v4, /device:TPU:1, one launch (start us, length us, event | category | flops | bytes accessed | tf_op | source)
XLA Modules:
  0.0 131.9 jit_solution(15638850491855448588)
XLA Ops:
  0.7 2.7 %shard_map.86 = bf16[3,1024]{1,0:T(4,128)(2,1)S(1)} custom-call(s32[4]{0:T(128)S(1)} %pad_add_fusion.1.at_ref, s32[1,512]{1,0:T(1,128)} %bitcast.38, bf16[1024,1024]{1,0:T(8,128)(2,1)} %centers_ref.3), custom_call_target="tpu_custom_call" | custom-call | tf_op jit(solution)/shard_map/pallas_call | solution.py:151
  3.5 0.8 broadcast_in_dim.23
  4.3 19.1 %all-to-all-start.1 = ((bf16[64,24,128]{2,1,0:T(8,128)(2,1)}), bf16[64,24,128]{2,1,0:T(8,128)(2,1)S(1)}, u32[]{:S(2)}, u32[]{:S(2)}) async-start(bf16[64,24,128]{2,1,0:T(8,128)(2,1)} %broadcast_in_dim.23), calls=%async_computation.1 | async-start | bytes 786432 | tf_op jit(solution)/shard_map/all_to_all | solution.py:17
  23.5 4.6 %collective-permute-start.2 = (bf16[1024,128]{1,0:T(8,128)(2,1)S(1)}, bf16[1024,128]{1,0:T(8,128)(2,1)S(1)}, u32[]{:S(2)}, u32[]{:S(2)}) collective-permute-start(bf16[1024,128]{1,0:T(8,128)(2,1)S(1)} %get-tuple-element.60), channel_id=1, source_target_pairs={{0,384},{128,0},{256,128},{384,256},{1,385},{129,1},{257,129},{385... | collective-permute-start | bytes 786440 | tf_op jit(solution)/shard_map/ppermute | solution.py:171
  28.2 1.9 %collective-permute-start = (bf16[1024,128]{1,0:T(8,128)(2,1)S(1)}, bf16[1024,128]{1,0:T(8,128)(2,1)S(1)}, u32[]{:S(2)}, u32[]{:S(2)}) collective-permute-start(bf16[1024,128]{1,0:T(8,128)(2,1)S(1)} %get-tuple-element.60), channel_id=1, source_target_pairs={{0,128},{128,256},{256,384},{384,0},{1,129},{129,257},{257,385},{3... | collective-permute-start | bytes 786440 | tf_op jit(solution)/shard_map/ppermute | solution.py:171
  30.1 3.5 %collective-permute-start.1 = (bf16[1024,128]{1,0:T(8,128)(2,1)S(1)}, bf16[1024,128]{1,0:T(8,128)(2,1)S(1)}, u32[]{:S(2)}, u32[]{:S(2)}) collective-permute-start(bf16[1024,128]{1,0:T(8,128)(2,1)S(1)} %get-tuple-element.60), channel_id=1, source_target_pairs={{0,256},{128,384},{256,0},{384,128},{1,257},{129,385},{257,1},{385... | collective-permute-start | bytes 786440 | tf_op jit(solution)/shard_map/ppermute | solution.py:171
  33.7 5.3 %collective-permute-done = bf16[1024,128]{1,0:T(8,128)(2,1)S(1)} collective-permute-done((bf16[1024,128]{1,0:T(8,128)(2,1)S(1)}, bf16[1024,128]{1,0:T(8,128)(2,1)S(1)}, u32[]{:S(2)}, u32[]{:S(2)}) %collective-permute-start) | collective-permute-done | bytes 262176 | tf_op jit(solution)/shard_map/ppermute | solution.py:171
  38.9 3.6 %collective-permute-done.1 = bf16[1024,128]{1,0:T(8,128)(2,1)S(1)} collective-permute-done((bf16[1024,128]{1,0:T(8,128)(2,1)S(1)}, bf16[1024,128]{1,0:T(8,128)(2,1)S(1)}, u32[]{:S(2)}, u32[]{:S(2)}) %collective-permute-start.1) | collective-permute-done | bytes 262176 | tf_op jit(solution)/shard_map/ppermute | solution.py:171
  42.7 5.0 %collective-permute-start.3 = (bf16[4,1024,128]{2,1,0:T(8,128)(2,1)S(1)}, bf16[4,1024,128]{2,1,0:T(8,128)(2,1)}, u32[]{:S(2)}, u32[]{:S(2)}) collective-permute-start(bf16[4,1024,128]{2,1,0:T(8,128)(2,1)S(1)} %pad_maximum_fusion.mine_ref), channel_id=1, source_target_pairs={{0,64},{64,0},{1,65},{65,1},{2,66},{66,2},{3,67},{67,3},{4,68},{68... | collective-permute-start | bytes 3145736 | tf_op jit(solution)/shard_map/ppermute | solution.py:175
  47.9 0.7 reduce_max.9
  48.6 2.1 %multiply_reduce_fusion = f32[1024]{0:T(1024)S(1)} fusion(bf16[1024,1024]{1,0:T(8,128)(2,1)} %centers_ref.3), kind=kLoop, calls=%fused_computation.1 | loop fusion | flops 3144704 | bytes 2101248 | tf_op jit(solution)/shard_map/reduce_sum | solution.py:178
  50.7 0.7 fusion.6.vecs_ref
  51.6 0.9 shard_map.87
  52.5 0.6 while.10
  53.2 3.3 %shard_map.88 = bf16[64,1536]{1,0:T(8,128)(2,1)S(1)} custom-call(s32[4]{0:T(128)S(1)} %pad_add_fusion.1.at_ref, bf16[64,1024]{1,0:T(8,128)(2,1)S(1)} %get-tuple-element.43.feats_ref, bf16[1024,1024]{1,0:T(8,128)(2,1)} %get-tuple-element.138, f32[1,1024]{1,0:T(1,128)S(1)} %bitcast.34, bf16[4,1024,128]{2,1,0:T(8,128)(2,1)S(1)} %pad_maximum_fusion.mine_ref, ...), custom_call_target="tpu_custom_call" | custom-call | tf_op jit(solution)/shard_map/pallas_call | solution.py:123
  56.4 0.7 reshape.172
  57.1 14.5 %all-to-all-start.2 = ((bf16[64,3,4,128]{3,2,1,0:T(4,128)(2,1)}), bf16[64,3,4,128]{3,2,1,0:T(4,128)(2,1)S(1)}, u32[]{:S(2)}, u32[]{:S(2)}) async-start(bf16[64,3,4,128]{3,2,1,0:T(4,128)(2,1)} %reshape.172), calls=%async_computation.2 | async-start | bytes 393216 | tf_op jit(solution)/shard_map/all_to_all | solution.py:17
  71.7 0.2 convert_reduce_fusion
  72.0 17.9 %all-to-all-done.2 = bf16[64,3,4,128]{3,2,1,0:T(4,128)(2,1)S(1)} async-done(((bf16[64,3,4,128]{3,2,1,0:T(4,128)(2,1)}), bf16[64,3,4,128]{3,2,1,0:T(4,128)(2,1)S(1)}, u32[]{:S(2)}, u32[]{:S(2)}) %all-to-all-start.2) | async-done | bytes 196640 | tf_op jit(solution)/shard_map/all_to_all | solution.py:17
  89.9 0.6 broadcast_in_dim.29
  90.6 4.2 %all-to-all-start.3 = ((bf16[16,3,4,128]{3,2,1,0:T(4,128)(2,1)}), bf16[16,3,4,128]{3,2,1,0:T(4,128)(2,1)S(1)}, u32[]{:S(2)}, u32[]{:S(2)}) async-start(bf16[16,3,4,128]{3,2,1,0:T(4,128)(2,1)} %broadcast_in_dim.29), calls=%async_computation.3 | async-start | bytes 98304 | tf_op jit(solution)/shard_map/all_to_all | solution.py:17
  94.7 1.8 %fusion.11 = f32[512,125]{1,0:T(8,128)} fusion(f32[512,125]{1,0:T(8,128)S(1)} %copy-done.1, s32[512]{0:T(512)S(1)} %fusion.28), kind=kOutput, calls=%fused_computation.20 | convolution fusion | flops 393478144 | bytes 514048 | tf_op jit(solution)/shard_map/dot_general | solution.py:206
  96.6 0.2 select_reduce_fusion
  96.8 9.6 %all-to-all-done.3 = bf16[16,3,4,128]{3,2,1,0:T(4,128)(2,1)S(1)} async-done(((bf16[16,3,4,128]{3,2,1,0:T(4,128)(2,1)}), bf16[16,3,4,128]{3,2,1,0:T(4,128)(2,1)S(1)}, u32[]{:S(2)}, u32[]{:S(2)}) %all-to-all-start.3) | async-done | bytes 49184 | tf_op jit(solution)/shard_map/all_to_all | solution.py:17
  106.6 0.9 broadcast_in_dim.51
  107.5 6.9 %all-to-all-start.4 = ((bf16[32,16,640]{2,1,0:T(8,128)(2,1)}), bf16[32,16,640]{2,1,0:T(8,128)(2,1)S(1)}, u32[]{:S(2)}, u32[]{:S(2)}) async-start(bf16[32,16,640]{2,1,0:T(8,128)(2,1)} %bitcast.16), calls=%async_computation.4 | async-start | bytes 1310720 | tf_op jit(solution)/shard_map/all_to_all | solution.py:17
  114.4 0.4 fusion.5
  114.8 12.2 %all-to-all-done.4 = bf16[32,16,640]{2,1,0:T(8,128)(2,1)S(1)} async-done(((bf16[32,16,640]{2,1,0:T(8,128)(2,1)}), bf16[32,16,640]{2,1,0:T(8,128)(2,1)S(1)}, u32[]{:S(2)}, u32[]{:S(2)}) %all-to-all-start.4) | async-done | bytes 655392 | tf_op jit(solution)/shard_map/all_to_all | solution.py:17
  127.0 1.1 convolution_subtract_fusion
  128.1 1.0 multiply_convert_fusion
  129.1 1.3 fusion.10
  130.4 1.5 %fusion.7 = f32[1024,125]{1,0:T(8,128)} fusion(f32[1024,125]{1,0:T(8,128)S(1)} %copy-done.4, bf16[1024,512]{1,0:T(8,128)(2,1)S(1)} %fusion.5, bf16[1024,512]{1,0:T(8,128)(2,1)S(1)} %fusion.6.vecs_ref, bf16[512,125]{1,0:T(8,128)(2,1)S(1)} %multiply_convert_fusion, bf16[512,125]{1,0:T(8,128)(2,1)S(1)} %fusion.10), kind=kOutput, calls=%fused_computation.11 | convolution fusion | flops 266978304 | bytes 3377152 | tf_op jit(solution)/shard_map/dot_general | solution.py:37
  (42 shorter events, 1.0 us)
Async XLA Ops:
  0.6 50.0 %copy-start = (bf16[512,512]{1,0:T(8,128)(2,1)S(1)}, bf16[512,512]{1,0:T(8,128)(2,1)}, u32[]{:S(2)}) copy-start(bf16[512,512]{1,0:T(8,128)(2,1)} %param.14) | copy-start | bytes 1572868
  0.6 2.8 %copy-start.3 = (f32[1024,125]{1,0:T(8,128)S(1)}, f32[1024,125]{1,0:T(8,128)}, u32[]{:S(2)}) copy-start(f32[1024,125]{1,0:T(8,128)} %param.10) | copy-start | bytes 1536004
  3.5 44.2 %copy-start.5 = (s32[512]{0:T(512)S(1)}, s32[512]{0:T(512)}, u32[]{:S(2)}) copy-start(s32[512]{0:T(512)} %param.12) | copy-start | bytes 6148
  3.5 45.0 %copy-start.6 = (s32[512]{0:T(512)S(1)}, s32[512]{0:T(512)}, u32[]{:S(2)}) copy-start(s32[512]{0:T(512)} %param.13) | copy-start | bytes 6148
  4.3 47.0 %all-to-all-start.1 = ((bf16[64,24,128]{2,1,0:T(8,128)(2,1)}), bf16[64,24,128]{2,1,0:T(8,128)(2,1)S(1)}, u32[]{:S(2)}, u32[]{:S(2)}) async-start(bf16[64,24,128]{2,1,0:T(8,128)(2,1)} %broadcast_in_dim.23), calls=%async_computation.1 | async-start | bytes 786432 | tf_op jit(solution)/shard_map/all_to_all | solution.py:17
  23.5 10.1 %collective-permute-start.2 = (bf16[1024,128]{1,0:T(8,128)(2,1)S(1)}, bf16[1024,128]{1,0:T(8,128)(2,1)S(1)}, u32[]{:S(2)}, u32[]{:S(2)}) collective-permute-start(bf16[1024,128]{1,0:T(8,128)(2,1)S(1)} %get-tuple-element.60), channel_id=1, source_target_pairs={{0,384},{128,0},{256,128},{384,256},{1,385},{129,1},{257,129},{385... | collective-permute-start | bytes 786440 | tf_op jit(solution)/shard_map/ppermute | solution.py:171
  28.2 10.8 %collective-permute-start = (bf16[1024,128]{1,0:T(8,128)(2,1)S(1)}, bf16[1024,128]{1,0:T(8,128)(2,1)S(1)}, u32[]{:S(2)}, u32[]{:S(2)}) collective-permute-start(bf16[1024,128]{1,0:T(8,128)(2,1)S(1)} %get-tuple-element.60), channel_id=1, source_target_pairs={{0,128},{128,256},{256,384},{384,0},{1,129},{129,257},{257,385},{3... | collective-permute-start | bytes 786440 | tf_op jit(solution)/shard_map/ppermute | solution.py:171
  30.1 12.4 %collective-permute-start.1 = (bf16[1024,128]{1,0:T(8,128)(2,1)S(1)}, bf16[1024,128]{1,0:T(8,128)(2,1)S(1)}, u32[]{:S(2)}, u32[]{:S(2)}) collective-permute-start(bf16[1024,128]{1,0:T(8,128)(2,1)S(1)} %get-tuple-element.60), channel_id=1, source_target_pairs={{0,256},{128,384},{256,0},{384,128},{1,257},{129,385},{257,1},{385... | collective-permute-start | bytes 786440 | tf_op jit(solution)/shard_map/ppermute | solution.py:171
  42.7 9.8 %collective-permute-start.3 = (bf16[4,1024,128]{2,1,0:T(8,128)(2,1)S(1)}, bf16[4,1024,128]{2,1,0:T(8,128)(2,1)}, u32[]{:S(2)}, u32[]{:S(2)}) collective-permute-start(bf16[4,1024,128]{2,1,0:T(8,128)(2,1)S(1)} %pad_maximum_fusion.mine_ref), channel_id=1, source_target_pairs={{0,64},{64,0},{1,65},{65,1},{2,66},{66,2},{3,67},{67,3},{4,68},{68... | collective-permute-start | bytes 3145736 | tf_op jit(solution)/shard_map/ppermute | solution.py:175
  53.1 41.6 %copy-start.1 = (f32[512,125]{1,0:T(8,128)S(1)}, f32[512,125]{1,0:T(8,128)}, u32[]{:S(2)}) copy-start(f32[512,125]{1,0:T(8,128)} %param.11) | copy-start | bytes 768004
  57.1 32.7 %all-to-all-start.2 = ((bf16[64,3,4,128]{3,2,1,0:T(4,128)(2,1)}), bf16[64,3,4,128]{3,2,1,0:T(4,128)(2,1)S(1)}, u32[]{:S(2)}, u32[]{:S(2)}) async-start(bf16[64,3,4,128]{3,2,1,0:T(4,128)(2,1)} %reshape.172), calls=%async_computation.2 | async-start | bytes 393216 | tf_op jit(solution)/shard_map/all_to_all | solution.py:17
  90.6 15.8 %all-to-all-start.3 = ((bf16[16,3,4,128]{3,2,1,0:T(4,128)(2,1)}), bf16[16,3,4,128]{3,2,1,0:T(4,128)(2,1)S(1)}, u32[]{:S(2)}, u32[]{:S(2)}) async-start(bf16[16,3,4,128]{3,2,1,0:T(4,128)(2,1)} %broadcast_in_dim.29), calls=%async_computation.3 | async-start | bytes 98304 | tf_op jit(solution)/shard_map/all_to_all | solution.py:17
  96.7 18.0 %copy-start.7 = (f32[512]{0:T(512)S(1)}, f32[512]{0:T(512)}, u32[]{:S(2)}) copy-start(f32[512]{0:T(512)} %param.15) | copy-start | bytes 6148
  96.7 30.3 %copy-start.2 = (f32[512,125]{1,0:T(8,128)S(1)}, f32[512,125]{1,0:T(8,128)}, u32[]{:S(2)}) copy-start(f32[512,125]{1,0:T(8,128)} %param.11) | copy-start | bytes 768004
  107.5 19.5 %all-to-all-start.4 = ((bf16[32,16,640]{2,1,0:T(8,128)(2,1)}), bf16[32,16,640]{2,1,0:T(8,128)(2,1)S(1)}, u32[]{:S(2)}, u32[]{:S(2)}) async-start(bf16[32,16,640]{2,1,0:T(8,128)(2,1)} %bitcast.16), calls=%async_computation.4 | async-start | bytes 1310720 | tf_op jit(solution)/shard_map/all_to_all | solution.py:17
  127.0 3.4 %copy-start.4 = (f32[1024,125]{1,0:T(8,128)S(1)}, f32[1024,125]{1,0:T(8,128)}, u32[]{:S(2)}) copy-start(f32[1024,125]{1,0:T(8,128)} %param.10) | copy-start | bytes 1536004

commit v5 on v4

--- a/solution.py
+++ b/solution.py
@@ -49,7 +49,7 @@
         kernel,
         out_shape=shape,
         in_specs=[pl.BlockSpec(memory_space=pltpu.SMEM)] + [vmem] * count,
-        out_specs=vmem,
+        out_specs=jax.tree.map(lambda _: vmem, shape),
         compiler_params=pltpu.CompilerParams(vmem_limit_bytes=12 << 20),
     )
 
@@ -76,16 +76,17 @@
     out_ref[...] = found[: out_ref.shape[0]].astype(jnp.bfloat16)
 
 
-def slot_kernel(at_ref, rows_ref, arrived_ref, out_ref, *, count):
+def slot_kernel(at_ref, rows_ref, arrived_ref, out_ref, *, count, nx, nz):
     slice_at, step, nout = at_ref[1], at_ref[2], at_ref[3]
     rows = rows_ref[...]
     line = lax.broadcasted_iota(jnp.int32, (arrived_ref.shape[0], 1), 0)
     scale = (1 << 16) // ROUND + 1
-    place = (line * scale) >> 16
+    source = (line * scale) >> 16
+    place = (source & (nz - 1)) * nx + (source >> (nz.bit_length() - 1))
     start = rows_below(rows, place * count)
     stop = rows_below(rows, place * count + count)
     lead = start + ((slice_at - start) & (nout - 1))
-    position = lead + (line - place * ROUND + step) * nout
+    position = lead + (line - source * ROUND + step) * nout
     slots = lax.broadcasted_iota(jnp.int32, (1, LANES), 1) * nout + slice_at
     fits = (jnp.where(position < stop, position, -1) == slots).astype(jnp.float32)
     feats = lax.dot_general(
@@ -123,6 +124,39 @@
     return whole(products_kernel, shape, 6)(
         at, feats, centers, norm, mine, other, vecs
     )
+
+
+def tail_kernel(
+    at_ref,
+    arrived_ref,
+    line_targets_ref,
+    sub_vecs_ref,
+    batch_spread_ref,
+    to_batch_ref,
+    scale_ref,
+    weights_ref,
+    targets_ref,
+    updated_ref,
+    residual_ref,
+):
+    del at_ref
+    low = jnp.bfloat16
+    columns = weights_ref.shape[1]
+    prediction = arrived_ref[:, :LANES][:, :columns]
+    residual = prediction.astype(jnp.float32) - line_targets_ref[...]
+    coefficient = lax.dot_general(
+        arrived_ref[:, LANES:],
+        residual.astype(low),
+        (((0,), (0,)), ((), ())),
+        preferred_element_type=jnp.float32,
+    )
+    correction = (step_size * scale_ref[...] * coefficient).astype(low)
+    updated_ref[...] = (
+        weights_ref[...]
+        + dot(sub_vecs_ref[...], correction)
+        + dot(batch_spread_ref[...], (-step_size * residual).astype(low))
+    )
+    residual_ref[...] = dot(to_batch_ref[...], prediction) - targets_ref[...]
 
 
 def body(centers, weights, targets, batch_rows, subsample, eigvecs, eig_scale):
@@ -149,10 +183,11 @@
         at = places(turn)
         shape = jax.ShapeDtypeStruct((ROUND, feature_count), low)
         share = whole(pick_kernel, shape, 2)(at, batch_line, centers)
-        arrived = copied_to_all(share.reshape(-1, LANES), CTR)
+        arrived = copied_to_all(share.reshape(-1, LANES), "z")
+        arrived = copied_to_all(arrived.reshape(-1, LANES), "x")
         arrived = arrived.reshape(nctr * ROUND, feature_count)
         shape = jax.ShapeDtypeStruct((block, feature_count), low)
-        slot = functools.partial(slot_kernel, count=row_count)
+        slot = functools.partial(slot_kernel, count=row_count, nx=nx, nz=nz)
         return whole(slot, shape, 2)(at, batch_line, arrived)
 
     def more(carry):
@@ -165,13 +200,14 @@
     _, feats = lax.while_loop(more, next_round, (jnp.int32(1), feats))
 
     weights_low = jnp.pad(weights.astype(low), ((0, 0), (0, LANES - columns)))
-    mine = jnp.stack(
-        [weights_low]
-        + [
-            lax.ppermute(weights_low, "y", [(i, (i + dy) % ny) for i in range(ny)])
-            for dy in range(1, ny)
-        ]
-    )
+    ahead = [(i, (i + 1) % ny) for i in range(ny)]
+    back = [(i, (i - 1) % ny) for i in range(ny)]
+    one, three = lax.ppermute(weights_low, "y", ahead), lax.ppermute(weights_low, "y", back)
+    half = row_count // 2
+    two = jnp.concatenate(
+        [lax.ppermute(one[:half], "y", ahead), lax.ppermute(three[half:], "y", back)]
+    )
+    mine = jnp.stack([weights_low, one, two, three])
     other = lax.ppermute(mine, "core", [(i, (i + 1) % ncore) for i in range(ncore)])
 
     sub_vecs = dot(one_hot_columns(subsample - base, row_count), eigvecs).astype(low)
@@ -179,7 +215,9 @@
     parts = products(places(0), feats, centers, right_norm[None, :], mine, other, sub_vecs)
 
     blocks = parts.shape[1] // LANES
-    arrived = exchanged(parts.reshape(nctr, blocks // 4, 4, LANES), CTR)
+    arrived = exchanged(parts.reshape(nx, nz, parts.shape[1]), "x")
+    share = arrived.astype(jnp.float32).sum(axis=0).astype(low)
+    arrived = exchanged(share.reshape(nz, blocks // 4, 4, LANES), "z")
     share = arrived.astype(jnp.float32).sum(axis=0).astype(low)
     share = copied_to_all(share, "z").reshape(nz, blocks, LANES)
     heads = jnp.moveaxis(share[:, :nout], 1, 0).reshape(ncore, ny, nz, LANES)
@@ -192,8 +230,7 @@
     arrived = arrived.reshape(batch, -1)
 
     rank = jnp.sum((batch_rows[None, :] < batch_rows[:, None]).astype(jnp.int32), axis=1)
-    slot = rank // nout
-    line = (rank % nout) * block + (slot % nx) * nz + slot // nx
+    line = (rank % nout) * block + rank // nout
     to_batch = one_hot(line, batch)
     line_rows = jnp.sum(
         jnp.where(
@@ -210,26 +247,21 @@
         precision=lax.Precision.HIGHEST,
     )
     batch_spread = one_hot_columns(line_rows - base, row_count)
-    line_targets, batch_spread = lax.optimization_barrier((line_targets, batch_spread))
-    spread = jnp.concatenate([sub_vecs, batch_spread], axis=1)
-
-    line_prediction = arrived[:, :columns]
-    line_residual = line_prediction.astype(jnp.float32) - line_targets
-    coefficient = lax.dot_general(
-        arrived[:, LANES:],
-        line_residual.astype(low),
-        (((0,), (0,)), ((), ())),
-        preferred_element_type=jnp.float32,
-    )
-    changes = jnp.concatenate(
-        [
-            (step_size * eig_scale[:, None] * coefficient).astype(low),
-            (-step_size * line_residual).astype(low),
-        ]
-    )
-    updated = weights + dot(spread, changes)
-    residual = dot(to_batch, line_prediction) - targets
-    return (updated, residual)
+    shapes = (
+        jax.ShapeDtypeStruct(weights.shape, jnp.float32),
+        jax.ShapeDtypeStruct(targets.shape, jnp.float32),
+    )
+    return whole(tail_kernel, shapes, 8)(
+        places(0),
+        arrived,
+        line_targets,
+        sub_vecs,
+        batch_spread,
+        to_batch,
+        eig_scale[:, None],
+        weights,
+        targets,
+    )
 
 
 def solution(mesh):

time: 133 us -> 139 us (1.045)
  local copies, waits for them, and re-layouts: 3.41 us -> 7.78 us
  matrix products: 6.41 us -> 2.52 us
  Pallas kernels: 6.91 us -> 9.66 us
  starting transfers between devices: 59.7 us -> 61.6 us
    ppermute x3 -> x4, waiting for transfers between devices: 8.88 us -> 0.01 us  [the longest x1 0.01 us: body(): lax.ppermute(weights_low, 'y', ahead)]
    all_to_all x4 -> x6, waiting for transfers between devices: 39.7 us -> 48.5 us  [exchanged(): return lax.all_to_all(pieces, axes, split_axis=0, concat_axis=0, tiled=True)]
    ppermute x3 -> x4, starting transfers between devices: 10.1 us -> 14.2 us  [the longest x1 4.26 us: body(): lax.ppermute(three[half:], 'y', back)]
    pallas_call x0 -> x1, Pallas kernels: none -> 3.28 us  [body(): whole(tail_kernel, shapes, 8)]
    unnamed x16 -> x20, local copies, waits for them, and re-layouts: 0.05 us -> 2.98 us
    dot_general x3 -> x1, matrix products: 3.31 us -> 0.72 us  [dot(): return jnp.dot(left, right, preferred_element_type=jnp.float32)]
    all_to_all x4 -> x6, starting transfers between devices: 44.6 us -> 43.2 us  [exchanged(): return lax.all_to_all(pieces, axes, split_axis=0, concat_axis=0, tiled=True)]
  transfers between devices with their start and end apart: 8 -> 11, of which waited for: 5 -> 6; matrix products, arithmetic and copies ran while one was open for 5% -> 7% of each run, Pallas kernels for 1% -> 2%
where the time goes in v5:
time: 139 us; the launch traced here: 138 us
  starting transfers between devices  61.6 us (44%)
  waiting for transfers between devices  48.5 us (35%)
  Pallas kernels  9.66 us (7%)
  local copies, waits for them, and re-layouts  7.78 us (6%)
  other arithmetic  6.4 us (5%)
  matrix products  2.52 us (2%)
    all_to_all x6, waiting for transfers between devices, exchanged(): return lax.all_to_all(pieces, axes, split_axis=0, concat_axis=0, tiled=True)  48.5 us
    all_to_all x6, starting transfers between devices, exchanged(): return lax.all_to_all(pieces, axes, split_axis=0, concat_axis=0, tiled=True)  43.2 us
    ppermute x1, starting transfers between devices, body(): lax.ppermute(three[half:], 'y', back)  4.26 us
    ppermute x1, starting transfers between devices, body(): lax.ppermute(mine, 'core', [(i, (i + 1) % ncore) for i in range(ncore)])  4.21 us
    ppermute x1, starting transfers between devices, body(): lax.ppermute(weights_low, 'y', ahead)  4.02 us
    pallas_call x1, Pallas kernels, products(): whole(products_kernel, shape, 6)  3.91 us
    ppermute x1, starting transfers between devices, body(): lax.ppermute(weights_low, 'y', back)  3.36 us
    pallas_call x1, Pallas kernels, body(): whole(tail_kernel, shapes, 8)  3.28 us
  transfers between devices with their start and end apart: 11, of which 6 were waited for; matrix products, arithmetic and copies ran while one was open for 7% of the time, Pallas kernels for 2%

profile of v5, /device:TPU:1, one launch (start us, length us, event | category | flops | bytes accessed | tf_op | source)
XLA Modules:
  0.0 138.1 jit_solution(10662875119308855464)
XLA Ops:
  0.7 1.1 convert_element_type.31
  1.9 4.0 %collective-permute-start = (bf16[1024,128]{1,0:T(8,128)(2,1)S(1)}, bf16[1024,128]{1,0:T(8,128)(2,1)S(1)}, u32[]{:S(2)}, u32[]{:S(2)}) collective-permute-start(bf16[1024,128]{1,0:T(8,128)(2,1)S(1)} %get-tuple-element.56), channel_id=1, source_target_pairs={{0,128},{128,256},{256,384},{384,0},{1,129},{129,257},{257,385},{3... | collective-permute-start | bytes 786440 | tf_op jit(solution)/shard_map/ppermute | solution.py:205
  5.9 3.4 %collective-permute-start.2 = (bf16[1024,128]{1,0:T(8,128)(2,1)S(1)}, bf16[1024,128]{1,0:T(8,128)(2,1)S(1)}, u32[]{:S(2)}, u32[]{:S(2)}) collective-permute-start(bf16[1024,128]{1,0:T(8,128)(2,1)S(1)} %get-tuple-element.56), channel_id=1, source_target_pairs={{0,384},{128,0},{256,128},{384,256},{1,385},{129,1},{257,129},{385... | collective-permute-start | bytes 786440 | tf_op jit(solution)/shard_map/ppermute | solution.py:205
  9.3 2.2 %multiply_reduce_fusion = f32[1024]{0:T(1024)S(1)} fusion(bf16[1024,1024]{1,0:T(8,128)(2,1)} %centers_ref.3), kind=kLoop, calls=%fused_computation.1 | loop fusion | flops 3144704 | bytes 2101248 | tf_op jit(solution)/shard_map/reduce_sum | solution.py:214
  11.5 2.5 %collective-permute-start.1 = (bf16[512,128]{1,0:T(8,128)(2,1)S(1)}, bf16[512,128]{1,0:T(8,128)(2,1)S(1)}, u32[]{:S(2)}, u32[]{:S(2)}) collective-permute-start(bf16[512,128]{1,0:T(8,128)(2,1)S(1)} %slice.16), channel_id=1, source_target_pairs={{0,128},{128,256},{256,384},{384,0},{1,129},{129,257},{257,385},{3... | collective-permute-start | bytes 393224 | tf_op jit(solution)/shard_map/ppermute | solution.py:208
  14.1 4.3 %collective-permute-start.3 = (bf16[512,128]{1,0:T(8,128)(2,1)S(1)}, bf16[512,128]{1,0:T(8,128)(2,1)S(1)}, u32[]{:S(2)}, u32[]{:S(2)}) collective-permute-start(bf16[512,128]{1,0:T(8,128)(2,1)S(1)} %slice.17), channel_id=1, source_target_pairs={{0,384},{128,0},{256,128},{384,256},{1,385},{129,1},{257,129},{385... | collective-permute-start | bytes 393224 | tf_op jit(solution)/shard_map/ppermute | solution.py:208
  18.5 1.5 %shard_map.86 = bf16[3,1024]{1,0:T(4,128)(2,1)S(1)} custom-call(s32[4]{0:T(128)S(1)} %pad_add_fusion.1.at_ref, s32[1,512]{1,0:T(1,128)S(1)} %bitcast.45, bf16[1024,1024]{1,0:T(8,128)(2,1)S(1)} %copy-done.6), custom_call_target="tpu_custom_call" | custom-call | tf_op jit(solution)/shard_map/pallas_call | solution.py:185
  20.7 16.2 %all-to-all-start.2 = ((bf16[16,24,128]{2,1,0:T(8,128)(2,1)}), bf16[16,24,128]{2,1,0:T(8,128)(2,1)S(1)}, u32[]{:S(2)}, u32[]{:S(2)}) async-start(bf16[16,24,128]{2,1,0:T(8,128)(2,1)} %broadcast_in_dim.54), calls=%async_computation.2 | async-start | bytes 196608 | tf_op jit(solution)/shard_map/all_to_all | solution.py:17
  37.1 4.2 %collective-permute-start.4 = (bf16[4,1024,128]{2,1,0:T(8,128)(2,1)S(1)}, bf16[4,1024,128]{2,1,0:T(8,128)(2,1)}, u32[]{:S(2)}, u32[]{:S(2)}) collective-permute-start(bf16[4,1024,128]{2,1,0:T(8,128)(2,1)S(1)} %pad_maximum_fusion.mine_ref), channel_id=1, source_target_pairs={{0,64},{64,0},{1,65},{65,1},{2,66},{66,2},{3,67},{67,3},{4,68},{68... | collective-permute-start | bytes 3145736 | tf_op jit(solution)/shard_map/ppermute | solution.py:211
  41.3 7.4 %all-to-all-done.2 = bf16[16,24,128]{2,1,0:T(8,128)(2,1)S(1)} async-done(((bf16[16,24,128]{2,1,0:T(8,128)(2,1)}), bf16[16,24,128]{2,1,0:T(8,128)(2,1)S(1)}, u32[]{:S(2)}, u32[]{:S(2)}) %all-to-all-start.2) | async-done | bytes 98336 | tf_op jit(solution)/shard_map/all_to_all | solution.py:17
  48.7 0.8 broadcast_in_dim.55
  49.5 4.0 %all-to-all-start.3 = ((bf16[4,384,128]{2,1,0:T(8,128)(2,1)}), bf16[4,384,128]{2,1,0:T(8,128)(2,1)S(1)}, u32[]{:S(2)}, u32[]{:S(2)}) async-start(bf16[4,384,128]{2,1,0:T(8,128)(2,1)} %broadcast_in_dim.55), calls=%async_computation.3 | async-start | bytes 786432 | tf_op jit(solution)/shard_map/all_to_all | solution.py:17
  54.4 0.7 fusion.2.vecs_ref.sub_vecs_ref
  55.1 4.7 %all-to-all-done.3 = bf16[4,384,128]{2,1,0:T(8,128)(2,1)S(1)} async-done(((bf16[4,384,128]{2,1,0:T(8,128)(2,1)}), bf16[4,384,128]{2,1,0:T(8,128)(2,1)S(1)}, u32[]{:S(2)}, u32[]{:S(2)}) %all-to-all-start.3) | async-done | bytes 393248 | tf_op jit(solution)/shard_map/all_to_all | solution.py:17
  60.0 1.0 shard_map.87
  61.5 3.9 %shard_map.88 = bf16[64,1536]{1,0:T(8,128)(2,1)} custom-call(s32[4]{0:T(128)S(1)} %pad_add_fusion.1.at_ref, bf16[64,1024]{1,0:T(8,128)(2,1)S(1)} %get-tuple-element.40.feats_ref, bf16[1024,1024]{1,0:T(8,128)(2,1)} %get-tuple-element.134, f32[1,1024]{1,0:T(1,128)S(1)} %bitcast.41, bf16[4,1024,128]{2,1,0:T(8,128)(2,1)S(1)} %pad_maximum_fusion.mine_ref, ...), custom_call_target="tpu_custom_call" | custom-call | tf_op jit(solution)/shard_map/pallas_call | solution.py:124
  65.4 3.4 %all-to-all-start.4 = ((bf16[4,16,1536]{2,1,0:T(8,128)(2,1)}), bf16[4,16,1536]{2,1,0:T(8,128)(2,1)S(1)}, u32[]{:S(2)}, u32[]{:S(2)}) async-start(bf16[4,16,1536]{2,1,0:T(8,128)(2,1)} %bitcast.13), calls=%async_computation.4 | async-start | bytes 393216 | tf_op jit(solution)/shard_map/all_to_all | solution.py:17
  69.1 4.9 %all-to-all-done.4 = bf16[4,16,1536]{2,1,0:T(8,128)(2,1)S(1)} async-done(((bf16[4,16,1536]{2,1,0:T(8,128)(2,1)}), bf16[4,16,1536]{2,1,0:T(8,128)(2,1)S(1)}, u32[]{:S(2)}, u32[]{:S(2)}) %all-to-all-start.4) | async-done | bytes 196640 | tf_op jit(solution)/shard_map/all_to_all | solution.py:17
  74.6 4.3 %all-to-all-start.5 = ((bf16[16,3,4,128]{3,2,1,0:T(4,128)(2,1)}), bf16[16,3,4,128]{3,2,1,0:T(4,128)(2,1)S(1)}, u32[]{:S(2)}, u32[]{:S(2)}) async-start(bf16[16,3,4,128]{3,2,1,0:T(4,128)(2,1)} %reshape.125), calls=%async_computation.5 | async-start | bytes 98304 | tf_op jit(solution)/shard_map/all_to_all | solution.py:17
  79.0 11.6 %all-to-all-done.5 = bf16[16,3,4,128]{3,2,1,0:T(4,128)(2,1)S(1)} async-done(((bf16[16,3,4,128]{3,2,1,0:T(4,128)(2,1)}), bf16[16,3,4,128]{3,2,1,0:T(4,128)(2,1)S(1)}, u32[]{:S(2)}, u32[]{:S(2)}) %all-to-all-start.5) | async-done | bytes 49184 | tf_op jit(solution)/shard_map/all_to_all | solution.py:17
  91.3 3.5 %all-to-all-start.6 = ((bf16[16,3,4,128]{3,2,1,0:T(4,128)(2,1)}), bf16[16,3,4,128]{3,2,1,0:T(4,128)(2,1)S(1)}, u32[]{:S(2)}, u32[]{:S(2)}) async-start(bf16[16,3,4,128]{3,2,1,0:T(4,128)(2,1)} %broadcast_in_dim.57), calls=%async_computation.6 | async-start | bytes 98304 | tf_op jit(solution)/shard_map/all_to_all | solution.py:17
  94.8 0.9 fusion.3.to_batch_ref
  95.7 0.8 copy.25.scale_ref
  96.7 9.4 %all-to-all-done.6 = bf16[16,3,4,128]{3,2,1,0:T(4,128)(2,1)S(1)} async-done(((bf16[16,3,4,128]{3,2,1,0:T(4,128)(2,1)}), bf16[16,3,4,128]{3,2,1,0:T(4,128)(2,1)S(1)}, u32[]{:S(2)}, u32[]{:S(2)}) %all-to-all-start.6) | async-done | bytes 49184 | tf_op jit(solution)/shard_map/all_to_all | solution.py:17
  106.4 0.9 broadcast_in_dim.59
  107.3 11.8 %all-to-all-start.7 = ((bf16[32,16,640]{2,1,0:T(8,128)(2,1)}), bf16[32,16,640]{2,1,0:T(8,128)(2,1)}, u32[]{:S(2)}, u32[]{:S(2)}) async-start(bf16[32,16,640]{2,1,0:T(8,128)(2,1)} %bitcast.19), calls=%async_computation.7 | async-start | bytes 1310720 | tf_op jit(solution)/shard_map/all_to_all | solution.py:17
  119.1 1.8 %fusion.4.line_targets_ref = f32[512,125]{1,0:T(8,128)} fusion(f32[512,125]{1,0:T(8,128)S(1)} %copy-done.3, s32[512]{0:T(512)S(1)} %fusion.11), kind=kOutput, calls=%fused_computation.13 | convolution fusion | flops 393478144 | bytes 514048 | tf_op jit(solution)/shard_map/dot_general | solution.py:243
  121.4 10.5 %all-to-all-done.7 = bf16[32,16,640]{2,1,0:T(8,128)(2,1)} async-done(((bf16[32,16,640]{2,1,0:T(8,128)(2,1)}), bf16[32,16,640]{2,1,0:T(8,128)(2,1)}, u32[]{:S(2)}, u32[]{:S(2)}) %all-to-all-start.7) | async-done | bytes 655392 | tf_op jit(solution)/shard_map/all_to_all | solution.py:17
  131.9 1.0 copy-done.2
  132.9 0.9 copy-done.4
  133.8 0.9 copy-done.5
  134.8 3.3 %shard_map.89 = (f32[1024,125]{1,0:T(8,128)}, f32[512,125]{1,0:T(8,128)}) custom-call(s32[4]{0:T(128)S(1)} %pad_add_fusion.1.at_ref, bf16[512,640]{1,0:T(8,128)(2,1)} %bitcast.20.arrived_ref, f32[512,125]{1,0:T(8,128)S(1)} %copy-done.5, bf16[1024,512]{1,0:T(8,128)(2,1)S(1)} %fusion.2.vecs_ref.sub_vecs_ref, bf16[1024,512]{1,0:T(8,128)(2,1)S(1)} %fusion.1.batch_spread_ref, ...), custom_call_target="tpu_custom_call" | custom-call | tf_op jit(solution)/shard_map/pallas_call | solution.py:254
  (55 shorter events, 5.0 us)
Async XLA Ops:
  0.6 53.7 %copy-start = (bf16[512,512]{1,0:T(8,128)(2,1)S(1)}, bf16[512,512]{1,0:T(8,128)(2,1)}, u32[]{:S(2)}) copy-start(bf16[512,512]{1,0:T(8,128)(2,1)} %param.14) | copy-start | bytes 1572868
  0.6 17.8 %copy-start.7 = (s32[512]{0:T(512)S(1)}, s32[512]{0:T(512)}, u32[]{:S(2)}) copy-start(s32[512]{0:T(512)} %param.12) | copy-start | bytes 6148
  1.9 9.6 %collective-permute-start = (bf16[1024,128]{1,0:T(8,128)(2,1)S(1)}, bf16[1024,128]{1,0:T(8,128)(2,1)S(1)}, u32[]{:S(2)}, u32[]{:S(2)}) collective-permute-start(bf16[1024,128]{1,0:T(8,128)(2,1)S(1)} %get-tuple-element.56), channel_id=1, source_target_pairs={{0,128},{128,256},{256,384},{384,0},{1,129},{129,257},{257,385},{3... | collective-permute-start | bytes 786440 | tf_op jit(solution)/shard_map/ppermute | solution.py:205
  5.9 8.2 %collective-permute-start.2 = (bf16[1024,128]{1,0:T(8,128)(2,1)S(1)}, bf16[1024,128]{1,0:T(8,128)(2,1)S(1)}, u32[]{:S(2)}, u32[]{:S(2)}) collective-permute-start(bf16[1024,128]{1,0:T(8,128)(2,1)S(1)} %get-tuple-element.56), channel_id=1, source_target_pairs={{0,384},{128,0},{256,128},{384,256},{1,385},{129,1},{257,129},{385... | collective-permute-start | bytes 786440 | tf_op jit(solution)/shard_map/ppermute | solution.py:205
  9.3 9.2 %copy-start.6 = (bf16[1024,1024]{1,0:T(8,128)(2,1)S(1)}, bf16[1024,1024]{1,0:T(8,128)(2,1)}, u32[]{:S(2)}) copy-start(bf16[1024,1024]{1,0:T(8,128)(2,1)} %centers_ref.3) | copy-start | bytes 6291460
  11.5 25.4 %collective-permute-start.1 = (bf16[512,128]{1,0:T(8,128)(2,1)S(1)}, bf16[512,128]{1,0:T(8,128)(2,1)S(1)}, u32[]{:S(2)}, u32[]{:S(2)}) collective-permute-start(bf16[512,128]{1,0:T(8,128)(2,1)S(1)} %slice.16), channel_id=1, source_target_pairs={{0,128},{128,256},{256,384},{384,0},{1,129},{129,257},{257,385},{3... | collective-permute-start | bytes 393224 | tf_op jit(solution)/shard_map/ppermute | solution.py:208
  14.1 22.8 %collective-permute-start.3 = (bf16[512,128]{1,0:T(8,128)(2,1)S(1)}, bf16[512,128]{1,0:T(8,128)(2,1)S(1)}, u32[]{:S(2)}, u32[]{:S(2)}) collective-permute-start(bf16[512,128]{1,0:T(8,128)(2,1)S(1)} %slice.17), channel_id=1, source_target_pairs={{0,384},{128,0},{256,128},{384,256},{1,385},{129,1},{257,129},{385... | collective-permute-start | bytes 393224 | tf_op jit(solution)/shard_map/ppermute | solution.py:208
  18.5 22.8 %copy-start.9 = (s32[512]{0:T(512)S(1)}, s32[512]{0:T(512)}, u32[]{:S(2)}) copy-start(s32[512]{0:T(512)} %param.13) | copy-start | bytes 6148
  20.7 28.0 %all-to-all-start.2 = ((bf16[16,24,128]{2,1,0:T(8,128)(2,1)}), bf16[16,24,128]{2,1,0:T(8,128)(2,1)S(1)}, u32[]{:S(2)}, u32[]{:S(2)}) async-start(bf16[16,24,128]{2,1,0:T(8,128)(2,1)} %broadcast_in_dim.54), calls=%async_computation.2 | async-start | bytes 196608 | tf_op jit(solution)/shard_map/all_to_all | solution.py:17
  37.1 24.4 %collective-permute-start.4 = (bf16[4,1024,128]{2,1,0:T(8,128)(2,1)S(1)}, bf16[4,1024,128]{2,1,0:T(8,128)(2,1)}, u32[]{:S(2)}, u32[]{:S(2)}) collective-permute-start(bf16[4,1024,128]{2,1,0:T(8,128)(2,1)S(1)} %pad_maximum_fusion.mine_ref), channel_id=1, source_target_pairs={{0,64},{64,0},{1,65},{65,1},{2,66},{66,2},{3,67},{67,3},{4,68},{68... | collective-permute-start | bytes 3145736 | tf_op jit(solution)/shard_map/ppermute | solution.py:211
  49.5 10.2 %all-to-all-start.3 = ((bf16[4,384,128]{2,1,0:T(8,128)(2,1)}), bf16[4,384,128]{2,1,0:T(8,128)(2,1)S(1)}, u32[]{:S(2)}, u32[]{:S(2)}) async-start(bf16[4,384,128]{2,1,0:T(8,128)(2,1)} %broadcast_in_dim.55), calls=%async_computation.3 | async-start | bytes 786432 | tf_op jit(solution)/shard_map/all_to_all | solution.py:17
  61.5 34.2 %copy-start.8 = (f32[512]{0:T(512)S(1)}, f32[512]{0:T(512)}, u32[]{:S(2)}) copy-start(f32[512]{0:T(512)} %param.15) | copy-start | bytes 6148
  65.4 8.5 %all-to-all-start.4 = ((bf16[4,16,1536]{2,1,0:T(8,128)(2,1)}), bf16[4,16,1536]{2,1,0:T(8,128)(2,1)S(1)}, u32[]{:S(2)}, u32[]{:S(2)}) async-start(bf16[4,16,1536]{2,1,0:T(8,128)(2,1)} %bitcast.13), calls=%async_computation.4 | async-start | bytes 393216 | tf_op jit(solution)/shard_map/all_to_all | solution.py:17
  74.6 16.0 %all-to-all-start.5 = ((bf16[16,3,4,128]{3,2,1,0:T(4,128)(2,1)}), bf16[16,3,4,128]{3,2,1,0:T(4,128)(2,1)S(1)}, u32[]{:S(2)}, u32[]{:S(2)}) async-start(bf16[16,3,4,128]{3,2,1,0:T(4,128)(2,1)} %reshape.125), calls=%async_computation.5 | async-start | bytes 98304 | tf_op jit(solution)/shard_map/all_to_all | solution.py:17
  79.0 40.2 %copy-start.3 = (f32[512,125]{1,0:T(8,128)S(1)}, f32[512,125]{1,0:T(8,128)}, u32[]{:S(2)}) copy-start(f32[512,125]{1,0:T(8,128)} %targets_ref.1) | copy-start | bytes 768004
  91.3 14.9 %all-to-all-start.6 = ((bf16[16,3,4,128]{3,2,1,0:T(4,128)(2,1)}), bf16[16,3,4,128]{3,2,1,0:T(4,128)(2,1)S(1)}, u32[]{:S(2)}, u32[]{:S(2)}) async-start(bf16[16,3,4,128]{3,2,1,0:T(4,128)(2,1)} %broadcast_in_dim.57), calls=%async_computation.6 | async-start | bytes 98304 | tf_op jit(solution)/shard_map/all_to_all | solution.py:17
  106.4 25.5 %copy-start.1 = (f32[1024,125]{1,0:T(8,128)S(1)}, f32[1024,125]{1,0:T(8,128)}, u32[]{:S(2)}) copy-start(f32[1024,125]{1,0:T(8,128)} %weights_ref.1) | copy-start | bytes 1536004
  107.3 24.5 %all-to-all-start.7 = ((bf16[32,16,640]{2,1,0:T(8,128)(2,1)}), bf16[32,16,640]{2,1,0:T(8,128)(2,1)}, u32[]{:S(2)}, u32[]{:S(2)}) async-start(bf16[32,16,640]{2,1,0:T(8,128)(2,1)} %bitcast.19), calls=%async_computation.7 | async-start | bytes 1310720 | tf_op jit(solution)/shard_map/all_to_all | solution.py:17
  131.9 1.0 copy-start.2
  132.9 0.9 copy-start.4
  133.8 0.9 copy-start.5

commit v6 on v5

--- a/solution.py
+++ b/solution.py
@@ -19,12 +19,6 @@
 
 def copied_to_all(shard, axes):
     return exchanged(jnp.broadcast_to(shard, (lax.axis_size(axes), *shard.shape)), axes)
-
-
-def one_hot(rows, length):
-    return (lax.broadcasted_iota(jnp.int32, (rows.shape[0], length), 1) == rows[:, None]).astype(
-        jnp.bfloat16
-    )
 
 
 def one_hot_columns(rows, length):
@@ -76,17 +70,16 @@
     out_ref[...] = found[: out_ref.shape[0]].astype(jnp.bfloat16)
 
 
-def slot_kernel(at_ref, rows_ref, arrived_ref, out_ref, *, count, nx, nz):
+def slot_kernel(at_ref, rows_ref, arrived_ref, out_ref, *, count):
     slice_at, step, nout = at_ref[1], at_ref[2], at_ref[3]
     rows = rows_ref[...]
     line = lax.broadcasted_iota(jnp.int32, (arrived_ref.shape[0], 1), 0)
     scale = (1 << 16) // ROUND + 1
-    source = (line * scale) >> 16
-    place = (source & (nz - 1)) * nx + (source >> (nz.bit_length() - 1))
+    place = (line * scale) >> 16
     start = rows_below(rows, place * count)
     stop = rows_below(rows, place * count + count)
     lead = start + ((slice_at - start) & (nout - 1))
-    position = lead + (line - source * ROUND + step) * nout
+    position = lead + (line - place * ROUND + step) * nout
     slots = lax.broadcasted_iota(jnp.int32, (1, LANES), 1) * nout + slice_at
     fits = (jnp.where(position < stop, position, -1) == slots).astype(jnp.float32)
     feats = lax.dot_general(
@@ -129,11 +122,10 @@
 def tail_kernel(
     at_ref,
     arrived_ref,
-    line_targets_ref,
+    line_ref,
+    scale_ref,
     sub_vecs_ref,
     batch_spread_ref,
-    to_batch_ref,
-    scale_ref,
     weights_ref,
     targets_ref,
     updated_ref,
@@ -142,21 +134,39 @@
     del at_ref
     low = jnp.bfloat16
     columns = weights_ref.shape[1]
-    prediction = arrived_ref[:, :LANES][:, :columns]
-    residual = prediction.astype(jnp.float32) - line_targets_ref[...]
+    count, ranks = line_ref.shape[1], scale_ref.shape[1]
+    to_line = (lax.broadcasted_iota(jnp.int32, (count, count), 0) == line_ref[...]).astype(
+        jnp.float32
+    )
+    to_line = to_line.astype(low)
+    residual = (
+        lax.dot_general(
+            to_line,
+            arrived_ref[:, :LANES],
+            (((0,), (0,)), ((), ())),
+            preferred_element_type=jnp.float32,
+        )[:, :columns]
+        - targets_ref[...]
+    )
+    residual_ref[...] = residual
+    residual = residual.astype(low)
     coefficient = lax.dot_general(
         arrived_ref[:, LANES:],
-        residual.astype(low),
+        dot(to_line, residual).astype(low),
         (((0,), (0,)), ((), ())),
         preferred_element_type=jnp.float32,
     )
-    correction = (step_size * scale_ref[...] * coefficient).astype(low)
+    square = (ranks, ranks)
+    diagonal = lax.broadcasted_iota(jnp.int32, square, 0) == lax.broadcasted_iota(
+        jnp.int32, square, 1
+    )
+    scale = jnp.sum(jnp.where(diagonal, scale_ref[...], 0.0), axis=1, keepdims=True)
+    correction = (step_size * scale * coefficient).astype(low)
     updated_ref[...] = (
         weights_ref[...]
         + dot(sub_vecs_ref[...], correction)
-        + dot(batch_spread_ref[...], (-step_size * residual).astype(low))
-    )
-    residual_ref[...] = dot(to_batch_ref[...], prediction) - targets_ref[...]
+        - step_size * dot(batch_spread_ref[...], residual)
+    )
 
 
 def body(centers, weights, targets, batch_rows, subsample, eigvecs, eig_scale):
@@ -183,11 +193,10 @@
         at = places(turn)
         shape = jax.ShapeDtypeStruct((ROUND, feature_count), low)
         share = whole(pick_kernel, shape, 2)(at, batch_line, centers)
-        arrived = copied_to_all(share.reshape(-1, LANES), "z")
-        arrived = copied_to_all(arrived.reshape(-1, LANES), "x")
+        arrived = copied_to_all(share.reshape(-1, LANES), CTR)
         arrived = arrived.reshape(nctr * ROUND, feature_count)
         shape = jax.ShapeDtypeStruct((block, feature_count), low)
-        slot = functools.partial(slot_kernel, count=row_count, nx=nx, nz=nz)
+        slot = functools.partial(slot_kernel, count=row_count)
         return whole(slot, shape, 2)(at, batch_line, arrived)
 
     def more(carry):
@@ -200,14 +209,13 @@
     _, feats = lax.while_loop(more, next_round, (jnp.int32(1), feats))
 
     weights_low = jnp.pad(weights.astype(low), ((0, 0), (0, LANES - columns)))
-    ahead = [(i, (i + 1) % ny) for i in range(ny)]
-    back = [(i, (i - 1) % ny) for i in range(ny)]
-    one, three = lax.ppermute(weights_low, "y", ahead), lax.ppermute(weights_low, "y", back)
-    half = row_count // 2
-    two = jnp.concatenate(
-        [lax.ppermute(one[:half], "y", ahead), lax.ppermute(three[half:], "y", back)]
-    )
-    mine = jnp.stack([weights_low, one, two, three])
+    mine = jnp.stack(
+        [weights_low]
+        + [
+            lax.ppermute(weights_low, "y", [(i, (i + dy) % ny) for i in range(ny)])
+            for dy in range(1, ny)
+        ]
+    )
     other = lax.ppermute(mine, "core", [(i, (i + 1) % ncore) for i in range(ncore)])
 
     sub_vecs = dot(one_hot_columns(subsample - base, row_count), eigvecs).astype(low)
@@ -215,9 +223,7 @@
     parts = products(places(0), feats, centers, right_norm[None, :], mine, other, sub_vecs)
 
     blocks = parts.shape[1] // LANES
-    arrived = exchanged(parts.reshape(nx, nz, parts.shape[1]), "x")
-    share = arrived.astype(jnp.float32).sum(axis=0).astype(low)
-    arrived = exchanged(share.reshape(nz, blocks // 4, 4, LANES), "z")
+    arrived = exchanged(parts.reshape(nctr, blocks // 4, 4, LANES), CTR)
     share = arrived.astype(jnp.float32).sum(axis=0).astype(low)
     share = copied_to_all(share, "z").reshape(nz, blocks, LANES)
     heads = jnp.moveaxis(share[:, :nout], 1, 0).reshape(ncore, ny, nz, LANES)
@@ -230,35 +236,20 @@
     arrived = arrived.reshape(batch, -1)
 
     rank = jnp.sum((batch_rows[None, :] < batch_rows[:, None]).astype(jnp.int32), axis=1)
-    line = (rank % nout) * block + rank // nout
-    to_batch = one_hot(line, batch)
-    line_rows = jnp.sum(
-        jnp.where(
-            lax.broadcasted_iota(jnp.int32, (batch, batch), 0) == line[None, :],
-            batch_rows[None, :],
-            0,
-        ),
-        axis=1,
-    )
-    line_targets = lax.dot_general(
-        to_batch.astype(jnp.float32),
-        targets,
-        (((0,), (0,)), ((), ())),
-        precision=lax.Precision.HIGHEST,
-    )
-    batch_spread = one_hot_columns(line_rows - base, row_count)
+    slot = rank // nout
+    line = (rank % nout) * block + (slot % nx) * nz + slot // nx
+    batch_spread = one_hot_columns(batch_rows - base, row_count)
     shapes = (
         jax.ShapeDtypeStruct(weights.shape, jnp.float32),
         jax.ShapeDtypeStruct(targets.shape, jnp.float32),
     )
-    return whole(tail_kernel, shapes, 8)(
+    return whole(tail_kernel, shapes, 7)(
         places(0),
         arrived,
-        line_targets,
+        line[None, :],
+        eig_scale[None, :],
         sub_vecs,
         batch_spread,
-        to_batch,
-        eig_scale[:, None],
         weights,
         targets,
     )

time: 139 us -> 133 us (0.957)
  blocking collectives: 0 us -> 32.4 us
  waiting for transfers between devices: 48.5 us -> 32.6 us
  starting transfers between devices: 61.6 us -> 46 us
  local copies, waits for them, and re-layouts: 7.78 us -> 3.72 us
  other arithmetic: 6.4 us -> 4.15 us
  matrix products: 2.52 us -> 0.72 us
  Pallas kernels: 9.66 us -> 11.4 us
    all_to_all x0 -> x1, blocking collectives: none -> 32.4 us  [exchanged(): return lax.all_to_all(pieces, axes, split_axis=0, concat_axis=0, tiled=True)]
    all_to_all x6 -> x3, waiting for transfers between devices: 48.5 us -> 23.6 us  [exchanged(): return lax.all_to_all(pieces, axes, split_axis=0, concat_axis=0, tiled=True)]
    all_to_all x6 -> x3, starting transfers between devices: 43.2 us -> 31 us  [exchanged(): return lax.all_to_all(pieces, axes, split_axis=0, concat_axis=0, tiled=True)]
    ppermute x4 -> x3, waiting for transfers between devices: 0.01 us -> 8.98 us  [body(): lax.ppermute(weights_low, 'y', [(i, (i + dy) % ny) for i in range(ny)])]
    ppermute x4 -> x3, starting transfers between devices: 14.2 us -> 10.1 us  [body(): lax.ppermute(weights_low, 'y', [(i, (i + dy) % ny) for i in range(ny)])]
    unnamed x20 -> x12, local copies, waits for them, and re-layouts: 2.98 us -> 0.04 us
    dot_general x1 -> x0, matrix products: 1.8 us -> none  [body(): lax.dot_general(to_batch.astype(jnp.float32), targets, (((0,), (0,)), (()...]
  transfers between devices with their start and end apart: 11 -> 7, of which waited for: 6 -> 4; matrix products, arithmetic and copies ran while one was open for 7% -> 4% of each run, Pallas kernels for 2% -> 1%
where the time goes in v6:
time: 133 us
  starting transfers between devices  46 us (35%)
  waiting for transfers between devices  32.6 us (25%)
  blocking collectives  32.4 us (24%)
  Pallas kernels  11.4 us (9%)
  other arithmetic  4.15 us (3%)
  local copies, waits for them, and re-layouts  3.72 us (3%)
    all_to_all x1, blocking collectives, exchanged(): return lax.all_to_all(pieces, axes, split_axis=0, concat_axis=0, tiled=True)  32.4 us
    all_to_all x3, starting transfers between devices, exchanged(): return lax.all_to_all(pieces, axes, split_axis=0, concat_axis=0, tiled=True)  31 us
    all_to_all x3, waiting for transfers between devices, exchanged(): return lax.all_to_all(pieces, axes, split_axis=0, concat_axis=0, tiled=True)  23.6 us
    ppermute x3, starting transfers between devices, body(): lax.ppermute(weights_low, 'y', [(i, (i + dy) % ny) for i in range(ny)])  10.1 us
    ppermute x3, waiting for transfers between devices, body(): lax.ppermute(weights_low, 'y', [(i, (i + dy) % ny) for i in range(ny)])  8.98 us
    ppermute x1, starting transfers between devices, body(): lax.ppermute(mine, 'core', [(i, (i + 1) % ncore) for i in range(ncore)])  4.89 us
    pallas_call x1, Pallas kernels, body(): whole(tail_kernel, shapes, 7)  3.8 us
    pallas_call x1, Pallas kernels, products(): whole(products_kernel, shape, 6)  3.26 us
  transfers between devices with their start and end apart: 7, of which 4 were waited for; matrix products, arithmetic and copies ran while one was open for 4% of the time, Pallas kernels for 1%

profile of v6, /device:TPU:1, one launch (start us, length us, event | category | flops | bytes accessed | tf_op | source)
XLA Modules:
  0.0 132.5 jit_solution(10587791322999965156)
XLA Ops:
  0.7 0.1 pad_add_fusion.1.at_ref
  0.7 2.7 %shard_map.86 = bf16[3,1024]{1,0:T(4,128)(2,1)S(1)} custom-call(s32[4]{0:T(128)S(1)} %pad_add_fusion.1.at_ref, s32[1,512]{1,0:T(1,128)} %bitcast.37, bf16[1024,1024]{1,0:T(8,128)(2,1)} %centers_ref.3), custom_call_target="tpu_custom_call" | custom-call | tf_op jit(solution)/shard_map/pallas_call | solution.py:195
  3.5 0.8 broadcast_in_dim.18
  4.3 19.3 %all-to-all-start.1 = ((bf16[64,24,128]{2,1,0:T(8,128)(2,1)}), bf16[64,24,128]{2,1,0:T(8,128)(2,1)}, u32[]{:S(2)}, u32[]{:S(2)}) async-start(bf16[64,24,128]{2,1,0:T(8,128)(2,1)} %broadcast_in_dim.18), calls=%async_computation.1 | async-start | bytes 786432 | tf_op jit(solution)/shard_map/all_to_all | solution.py:17
  23.7 0.1 pad_bitcast_fusion
  23.8 4.6 %collective-permute-start.2 = (bf16[1024,128]{1,0:T(8,128)(2,1)S(1)}, bf16[1024,128]{1,0:T(8,128)(2,1)S(1)}, u32[]{:S(2)}, u32[]{:S(2)}) collective-permute-start(bf16[1024,128]{1,0:T(8,128)(2,1)S(1)} %get-tuple-element.56), channel_id=1, source_target_pairs={{0,384},{128,0},{256,128},{384,256},{1,385},{129,1},{257,129},{385... | collective-permute-start | bytes 786440 | tf_op jit(solution)/shard_map/ppermute | solution.py:215
  28.4 1.9 %collective-permute-start = (bf16[1024,128]{1,0:T(8,128)(2,1)S(1)}, bf16[1024,128]{1,0:T(8,128)(2,1)S(1)}, u32[]{:S(2)}, u32[]{:S(2)}) collective-permute-start(bf16[1024,128]{1,0:T(8,128)(2,1)S(1)} %get-tuple-element.56), channel_id=1, source_target_pairs={{0,128},{128,256},{256,384},{384,0},{1,129},{129,257},{257,385},{3... | collective-permute-start | bytes 786440 | tf_op jit(solution)/shard_map/ppermute | solution.py:215
  30.3 3.5 %collective-permute-start.1 = (bf16[1024,128]{1,0:T(8,128)(2,1)S(1)}, bf16[1024,128]{1,0:T(8,128)(2,1)S(1)}, u32[]{:S(2)}, u32[]{:S(2)}) collective-permute-start(bf16[1024,128]{1,0:T(8,128)(2,1)S(1)} %get-tuple-element.56), channel_id=1, source_target_pairs={{0,256},{128,384},{256,0},{384,128},{1,257},{129,385},{257,1},{385... | collective-permute-start | bytes 786440 | tf_op jit(solution)/shard_map/ppermute | solution.py:215
  33.9 5.4 %collective-permute-done = bf16[1024,128]{1,0:T(8,128)(2,1)S(1)} collective-permute-done((bf16[1024,128]{1,0:T(8,128)(2,1)S(1)}, bf16[1024,128]{1,0:T(8,128)(2,1)S(1)}, u32[]{:S(2)}, u32[]{:S(2)}) %collective-permute-start) | collective-permute-done | bytes 262176 | tf_op jit(solution)/shard_map/ppermute | solution.py:215
  39.3 3.6 %collective-permute-done.1 = bf16[1024,128]{1,0:T(8,128)(2,1)S(1)} collective-permute-done((bf16[1024,128]{1,0:T(8,128)(2,1)S(1)}, bf16[1024,128]{1,0:T(8,128)(2,1)S(1)}, u32[]{:S(2)}, u32[]{:S(2)}) %collective-permute-start.1) | collective-permute-done | bytes 262176 | tf_op jit(solution)/shard_map/ppermute | solution.py:215
  42.9 0.1 pad_maximum_fusion.mine_ref
  43.0 4.9 %collective-permute-start.3 = (bf16[4,1024,128]{2,1,0:T(8,128)(2,1)S(1)}, bf16[4,1024,128]{2,1,0:T(8,128)(2,1)}, u32[]{:S(2)}, u32[]{:S(2)}) collective-permute-start(bf16[4,1024,128]{2,1,0:T(8,128)(2,1)S(1)} %pad_maximum_fusion.mine_ref), channel_id=1, source_target_pairs={{0,64},{64,0},{1,65},{65,1},{2,66},{66,2},{3,67},{67,3},{4,68},{68... | collective-permute-start | bytes 3145736 | tf_op jit(solution)/shard_map/ppermute | solution.py:219
  47.9 0.2 convert_reduce_fusion.1
  48.1 0.7 reduce_max.9
  48.8 2.1 %multiply_reduce_fusion = f32[1024]{0:T(1024)S(1)} fusion(bf16[1024,1024]{1,0:T(8,128)(2,1)} %centers_ref.3), kind=kLoop, calls=%fused_computation.1 | loop fusion | flops 3144704 | bytes 2101248 | tf_op jit(solution)/shard_map/reduce_sum | solution.py:222
  50.9 0.7 fusion.2.vecs_ref.sub_vecs_ref
  51.7 1.2 reshape.195.arrived_ref
  52.8 1.6 %shard_map.87 = bf16[64,1024]{1,0:T(8,128)(2,1)} custom-call(s32[4]{0:T(128)S(1)} %pad_add_fusion.1.at_ref, s32[1,512]{1,0:T(1,128)S(1)} %bitcast.38, bf16[192,1024]{1,0:T(8,128)(2,1)S(1)} %reshape.195.arrived_ref), custom_call_target="tpu_custom_call" | custom-call | tf_op jit(solution)/shard_map/pallas_call | solution.py:200
  54.4 0.6 while.10
  55.1 3.3 %shard_map.88 = bf16[64,1536]{1,0:T(8,128)(2,1)S(1)} custom-call(s32[4]{0:T(128)S(1)} %pad_add_fusion.1.at_ref, bf16[64,1024]{1,0:T(8,128)(2,1)} %get-tuple-element.40.feats_ref, bf16[1024,1024]{1,0:T(8,128)(2,1)} %get-tuple-element.134, f32[1,1024]{1,0:T(1,128)S(1)} %bitcast.35, bf16[4,1024,128]{2,1,0:T(8,128)(2,1)S(1)} %pad_maximum_fusion.mine_ref, ...), custom_call_target="tpu_custom_call" | custom-call | tf_op jit(solution)/shard_map/pallas_call | solution.py:117
  58.3 0.1 reshape.196
  58.4 32.4 %all_to_all.26 = bf16[64,3,4,128]{3,2,1,0:T(4,128)(2,1)S(1)} all-to-all(bf16[64,3,4,128]{3,2,1,0:T(4,128)(2,1)S(1)} %reshape.196), channel_id=1, replica_groups=mesh['y'=4,'core'=2,'z'=16,'x'=4] {'z','x'}, dimensions={0} | all-to-all | bytes 393216 | tf_op jit(solution)/shard_map/all_to_all | solution.py:17
  90.8 0.1 reduce_sum.43
  90.9 0.6 broadcast_in_dim.38
  91.5 4.2 %all-to-all-start.3 = ((bf16[16,3,4,128]{3,2,1,0:T(4,128)(2,1)}), bf16[16,3,4,128]{3,2,1,0:T(4,128)(2,1)S(1)}, u32[]{:S(2)}, u32[]{:S(2)}) async-start(bf16[16,3,4,128]{3,2,1,0:T(4,128)(2,1)} %broadcast_in_dim.38), calls=%async_computation.3 | async-start | bytes 98304 | tf_op jit(solution)/shard_map/all_to_all | solution.py:17
  95.7 11.6 %all-to-all-done.3 = bf16[16,3,4,128]{3,2,1,0:T(4,128)(2,1)S(1)} async-done(((bf16[16,3,4,128]{3,2,1,0:T(4,128)(2,1)}), bf16[16,3,4,128]{3,2,1,0:T(4,128)(2,1)S(1)}, u32[]{:S(2)}, u32[]{:S(2)}) %all-to-all-start.3) | async-done | bytes 49184 | tf_op jit(solution)/shard_map/all_to_all | solution.py:17
  107.6 0.9 broadcast_in_dim.40
  108.5 7.5 %all-to-all-start.4 = ((bf16[32,16,640]{2,1,0:T(8,128)(2,1)}), bf16[32,16,640]{2,1,0:T(8,128)(2,1)}, u32[]{:S(2)}, u32[]{:S(2)}) async-start(bf16[32,16,640]{2,1,0:T(8,128)(2,1)} %bitcast.16), calls=%async_computation.4 | async-start | bytes 1310720 | tf_op jit(solution)/shard_map/all_to_all | solution.py:17
  116.0 0.2 convert_reduce_fusion
  116.3 0.4 fusion.1.batch_spread_ref
  116.7 12.0 %all-to-all-done.4 = bf16[32,16,640]{2,1,0:T(8,128)(2,1)} async-done(((bf16[32,16,640]{2,1,0:T(8,128)(2,1)}), bf16[32,16,640]{2,1,0:T(8,128)(2,1)}, u32[]{:S(2)}, u32[]{:S(2)}) %all-to-all-start.4) | async-done | bytes 655392 | tf_op jit(solution)/shard_map/all_to_all | solution.py:17
  128.7 3.8 %shard_map.89 = (f32[1024,125]{1,0:T(8,128)}, f32[512,125]{1,0:T(8,128)}) custom-call(s32[4]{0:T(128)S(1)} %pad_add_fusion.1.at_ref, bf16[512,640]{1,0:T(8,128)(2,1)} %bitcast.17.arrived_ref, s32[1,512]{1,0:T(1,128)S(1)} %fusion.9.line_ref, f32[1,512]{1,0:T(1,128)S(1)} %bitcast.36, bf16[1024,512]{1,0:T(8,128)(2,1)S(1)} %fusion.2.vecs_ref.sub_vecs_ref, ...), custom_call_target="tpu_custom_call" | custom-call | tf_op jit(solution)/shard_map/pallas_call | solution.py:246
  (31 shorter events, 0.3 us)
Async XLA Ops:
  0.6 50.3 %copy-start = (bf16[512,512]{1,0:T(8,128)(2,1)S(1)}, bf16[512,512]{1,0:T(8,128)(2,1)}, u32[]{:S(2)}) copy-start(bf16[512,512]{1,0:T(8,128)(2,1)} %param.14) | copy-start | bytes 1572868
  0.6 2.8 %copy-start.1 = (f32[1024,125]{1,0:T(8,128)S(1)}, f32[1024,125]{1,0:T(8,128)}, u32[]{:S(2)}) copy-start(f32[1024,125]{1,0:T(8,128)} %weights_ref.1) | copy-start | bytes 1536004
  3.5 44.4 %copy-start.4 = (s32[512]{0:T(512)S(1)}, s32[512]{0:T(512)}, u32[]{:S(2)}) copy-start(s32[512]{0:T(512)} %param.12) | copy-start | bytes 6148
  3.5 45.3 %copy-start.5 = (s32[512]{0:T(512)S(1)}, s32[512]{0:T(512)}, u32[]{:S(2)}) copy-start(s32[512]{0:T(512)} %param.13) | copy-start | bytes 6148
  4.3 47.3 %all-to-all-start.1 = ((bf16[64,24,128]{2,1,0:T(8,128)(2,1)}), bf16[64,24,128]{2,1,0:T(8,128)(2,1)}, u32[]{:S(2)}, u32[]{:S(2)}) async-start(bf16[64,24,128]{2,1,0:T(8,128)(2,1)} %broadcast_in_dim.18), calls=%async_computation.1 | async-start | bytes 786432 | tf_op jit(solution)/shard_map/all_to_all | solution.py:17
  23.8 10.1 %collective-permute-start.2 = (bf16[1024,128]{1,0:T(8,128)(2,1)S(1)}, bf16[1024,128]{1,0:T(8,128)(2,1)S(1)}, u32[]{:S(2)}, u32[]{:S(2)}) collective-permute-start(bf16[1024,128]{1,0:T(8,128)(2,1)S(1)} %get-tuple-element.56), channel_id=1, source_target_pairs={{0,384},{128,0},{256,128},{384,256},{1,385},{129,1},{257,129},{385... | collective-permute-start | bytes 786440 | tf_op jit(solution)/shard_map/ppermute | solution.py:215
  28.4 10.9 %collective-permute-start = (bf16[1024,128]{1,0:T(8,128)(2,1)S(1)}, bf16[1024,128]{1,0:T(8,128)(2,1)S(1)}, u32[]{:S(2)}, u32[]{:S(2)}) collective-permute-start(bf16[1024,128]{1,0:T(8,128)(2,1)S(1)} %get-tuple-element.56), channel_id=1, source_target_pairs={{0,128},{128,256},{256,384},{384,0},{1,129},{129,257},{257,385},{3... | collective-permute-start | bytes 786440 | tf_op jit(solution)/shard_map/ppermute | solution.py:215
  30.3 12.5 %collective-permute-start.1 = (bf16[1024,128]{1,0:T(8,128)(2,1)S(1)}, bf16[1024,128]{1,0:T(8,128)(2,1)S(1)}, u32[]{:S(2)}, u32[]{:S(2)}) collective-permute-start(bf16[1024,128]{1,0:T(8,128)(2,1)S(1)} %get-tuple-element.56), channel_id=1, source_target_pairs={{0,256},{128,384},{256,0},{384,128},{1,257},{129,385},{257,1},{385... | collective-permute-start | bytes 786440 | tf_op jit(solution)/shard_map/ppermute | solution.py:215
  43.0 11.4 %collective-permute-start.3 = (bf16[4,1024,128]{2,1,0:T(8,128)(2,1)S(1)}, bf16[4,1024,128]{2,1,0:T(8,128)(2,1)}, u32[]{:S(2)}, u32[]{:S(2)}) collective-permute-start(bf16[4,1024,128]{2,1,0:T(8,128)(2,1)S(1)} %pad_maximum_fusion.mine_ref), channel_id=1, source_target_pairs={{0,64},{64,0},{1,65},{65,1},{2,66},{66,2},{3,67},{67,3},{4,68},{68... | collective-permute-start | bytes 3145736 | tf_op jit(solution)/shard_map/ppermute | solution.py:219
  91.5 15.8 %all-to-all-start.3 = ((bf16[16,3,4,128]{3,2,1,0:T(4,128)(2,1)}), bf16[16,3,4,128]{3,2,1,0:T(4,128)(2,1)S(1)}, u32[]{:S(2)}, u32[]{:S(2)}) async-start(bf16[16,3,4,128]{3,2,1,0:T(4,128)(2,1)} %broadcast_in_dim.38), calls=%async_computation.3 | async-start | bytes 98304 | tf_op jit(solution)/shard_map/all_to_all | solution.py:17
  95.7 33.0 %copy-start.2 = (f32[512,125]{1,0:T(8,128)S(1)}, f32[512,125]{1,0:T(8,128)}, u32[]{:S(2)}) copy-start(f32[512,125]{1,0:T(8,128)} %targets_ref.1) | copy-start | bytes 768004
  95.7 33.0 %copy-start.3 = (f32[512]{0:T(512)S(1)}, f32[512]{0:T(512)}, u32[]{:S(2)}) copy-start(f32[512]{0:T(512)} %param.15) | copy-start | bytes 6148
  108.5 20.3 %all-to-all-start.4 = ((bf16[32,16,640]{2,1,0:T(8,128)(2,1)}), bf16[32,16,640]{2,1,0:T(8,128)(2,1)}, u32[]{:S(2)}, u32[]{:S(2)}) async-start(bf16[32,16,640]{2,1,0:T(8,128)(2,1)} %bitcast.16), calls=%async_computation.4 | async-start | bytes 1310720 | tf_op jit(solution)/shard_map/all_to_all | solution.py:17

commit v7 on v6

--- a/solution.py
+++ b/solution.py
@@ -209,13 +209,10 @@
     _, feats = lax.while_loop(more, next_round, (jnp.int32(1), feats))
 
     weights_low = jnp.pad(weights.astype(low), ((0, 0), (0, LANES - columns)))
-    mine = jnp.stack(
-        [weights_low]
-        + [
-            lax.ppermute(weights_low, "y", [(i, (i + dy) % ny) for i in range(ny)])
-            for dy in range(1, ny)
-        ]
-    )
+    ring = [[(i, (i + dy) % ny) for i in range(ny)] for dy in range(ny)]
+    two = lax.ppermute(weights_low, "y", ring[2])
+    one, three = (lax.ppermute(weights_low, "y", ring[dy]) for dy in (1, 3))
+    mine = jnp.stack([weights_low, one, two, three])
     other = lax.ppermute(mine, "core", [(i, (i + 1) % ncore) for i in range(ncore)])
 
     sub_vecs = dot(one_hot_columns(subsample - base, row_count), eigvecs).astype(low)

time: 133 us -> 133 us (level)
  no operation moved by 1% of the time
where the time goes in v7:
time: 133 us
  starting transfers between devices  46 us (35%)
  waiting for transfers between devices  32.6 us (25%)
  blocking collectives  32.4 us (24%)
  Pallas kernels  11.4 us (9%)
  other arithmetic  4.15 us (3%)
  local copies, waits for them, and re-layouts  3.72 us (3%)
    all_to_all x1, blocking collectives, exchanged(): return lax.all_to_all(pieces, axes, split_axis=0, concat_axis=0, tiled=True)  32.4 us
    all_to_all x3, starting transfers between devices, exchanged(): return lax.all_to_all(pieces, axes, split_axis=0, concat_axis=0, tiled=True)  31 us
    all_to_all x3, waiting for transfers between devices, exchanged(): return lax.all_to_all(pieces, axes, split_axis=0, concat_axis=0, tiled=True)  23.6 us
    ppermute x2, starting transfers between devices, body(): one, three = (lax.ppermute(weights_low, 'y', ring[dy]) for dy in (1, 3))  6.56 us
    ppermute x2, waiting for transfers between devices, body(): one, three = (lax.ppermute(weights_low, 'y', ring[dy]) for dy in (1, 3))  5.37 us
    ppermute x1, starting transfers between devices, body(): lax.ppermute(mine, 'core', [(i, (i + 1) % ncore) for i in range(ncore)])  4.89 us
    pallas_call x1, Pallas kernels, body(): whole(tail_kernel, shapes, 7)  3.8 us
    ppermute x1, waiting for transfers between devices, body(): two = lax.ppermute(weights_low, 'y', ring[2])  3.61 us
  transfers between devices with their start and end apart: 7, of which 4 were waited for; matrix products, arithmetic and copies ran while one was open for 4% of the time, Pallas kernels for 1%

profile of v7, /device:TPU:1, one launch (start us, length us, event | category | flops | bytes accessed | tf_op | source)
XLA Modules:
  0.0 132.5 jit_solution(10587791322999965156)
XLA Ops:
  0.7 0.1 pad_add_fusion.1.at_ref
  0.7 2.7 %shard_map.86 = bf16[3,1024]{1,0:T(4,128)(2,1)S(1)} custom-call(s32[4]{0:T(128)S(1)} %pad_add_fusion.1.at_ref, s32[1,512]{1,0:T(1,128)} %bitcast.37, bf16[1024,1024]{1,0:T(8,128)(2,1)} %centers_ref.3), custom_call_target="tpu_custom_call" | custom-call | tf_op jit(solution)/shard_map/pallas_call | solution.py:195
  3.5 0.8 broadcast_in_dim.18
  4.3 19.3 %all-to-all-start.1 = ((bf16[64,24,128]{2,1,0:T(8,128)(2,1)}), bf16[64,24,128]{2,1,0:T(8,128)(2,1)}, u32[]{:S(2)}, u32[]{:S(2)}) async-start(bf16[64,24,128]{2,1,0:T(8,128)(2,1)} %broadcast_in_dim.18), calls=%async_computation.1 | async-start | bytes 786432 | tf_op jit(solution)/shard_map/all_to_all | solution.py:17
  23.7 0.1 pad_bitcast_fusion
  23.8 4.6 %collective-permute-start.2 = (bf16[1024,128]{1,0:T(8,128)(2,1)S(1)}, bf16[1024,128]{1,0:T(8,128)(2,1)S(1)}, u32[]{:S(2)}, u32[]{:S(2)}) collective-permute-start(bf16[1024,128]{1,0:T(8,128)(2,1)S(1)} %get-tuple-element.56), channel_id=1, source_target_pairs={{0,384},{128,0},{256,128},{384,256},{1,385},{129,1},{257,129},{385... | collective-permute-start | bytes 786440 | tf_op jit(solution)/shard_map/ppermute | solution.py:214
  28.4 1.9 %collective-permute-start = (bf16[1024,128]{1,0:T(8,128)(2,1)S(1)}, bf16[1024,128]{1,0:T(8,128)(2,1)S(1)}, u32[]{:S(2)}, u32[]{:S(2)}) collective-permute-start(bf16[1024,128]{1,0:T(8,128)(2,1)S(1)} %get-tuple-element.56), channel_id=1, source_target_pairs={{0,128},{128,256},{256,384},{384,0},{1,129},{129,257},{257,385},{3... | collective-permute-start | bytes 786440 | tf_op jit(solution)/shard_map/ppermute | solution.py:214
  30.3 3.5 %collective-permute-start.1 = (bf16[1024,128]{1,0:T(8,128)(2,1)S(1)}, bf16[1024,128]{1,0:T(8,128)(2,1)S(1)}, u32[]{:S(2)}, u32[]{:S(2)}) collective-permute-start(bf16[1024,128]{1,0:T(8,128)(2,1)S(1)} %get-tuple-element.56), channel_id=1, source_target_pairs={{0,256},{128,384},{256,0},{384,128},{1,257},{129,385},{257,1},{385... | collective-permute-start | bytes 786440 | tf_op jit(solution)/shard_map/ppermute | solution.py:213
  33.9 5.4 %collective-permute-done = bf16[1024,128]{1,0:T(8,128)(2,1)S(1)} collective-permute-done((bf16[1024,128]{1,0:T(8,128)(2,1)S(1)}, bf16[1024,128]{1,0:T(8,128)(2,1)S(1)}, u32[]{:S(2)}, u32[]{:S(2)}) %collective-permute-start) | collective-permute-done | bytes 262176 | tf_op jit(solution)/shard_map/ppermute | solution.py:214
  39.3 3.6 %collective-permute-done.1 = bf16[1024,128]{1,0:T(8,128)(2,1)S(1)} collective-permute-done((bf16[1024,128]{1,0:T(8,128)(2,1)S(1)}, bf16[1024,128]{1,0:T(8,128)(2,1)S(1)}, u32[]{:S(2)}, u32[]{:S(2)}) %collective-permute-start.1) | collective-permute-done | bytes 262176 | tf_op jit(solution)/shard_map/ppermute | solution.py:213
  42.9 0.1 pad_maximum_fusion.mine_ref
  43.0 4.9 %collective-permute-start.3 = (bf16[4,1024,128]{2,1,0:T(8,128)(2,1)S(1)}, bf16[4,1024,128]{2,1,0:T(8,128)(2,1)}, u32[]{:S(2)}, u32[]{:S(2)}) collective-permute-start(bf16[4,1024,128]{2,1,0:T(8,128)(2,1)S(1)} %pad_maximum_fusion.mine_ref), channel_id=1, source_target_pairs={{0,64},{64,0},{1,65},{65,1},{2,66},{66,2},{3,67},{67,3},{4,68},{68... | collective-permute-start | bytes 3145736 | tf_op jit(solution)/shard_map/ppermute | solution.py:216
  47.9 0.2 convert_reduce_fusion.1
  48.1 0.7 reduce_max.9
  48.8 2.1 %multiply_reduce_fusion = f32[1024]{0:T(1024)S(1)} fusion(bf16[1024,1024]{1,0:T(8,128)(2,1)} %centers_ref.3), kind=kLoop, calls=%fused_computation.1 | loop fusion | flops 3144704 | bytes 2101248 | tf_op jit(solution)/shard_map/reduce_sum | solution.py:219
  50.9 0.7 fusion.2.vecs_ref.sub_vecs_ref
  51.7 1.2 reshape.195.arrived_ref
  52.8 1.6 %shard_map.87 = bf16[64,1024]{1,0:T(8,128)(2,1)} custom-call(s32[4]{0:T(128)S(1)} %pad_add_fusion.1.at_ref, s32[1,512]{1,0:T(1,128)S(1)} %bitcast.38, bf16[192,1024]{1,0:T(8,128)(2,1)S(1)} %reshape.195.arrived_ref), custom_call_target="tpu_custom_call" | custom-call | tf_op jit(solution)/shard_map/pallas_call | solution.py:200
  54.4 0.6 while.10
  55.1 3.3 %shard_map.88 = bf16[64,1536]{1,0:T(8,128)(2,1)S(1)} custom-call(s32[4]{0:T(128)S(1)} %pad_add_fusion.1.at_ref, bf16[64,1024]{1,0:T(8,128)(2,1)} %get-tuple-element.40.feats_ref, bf16[1024,1024]{1,0:T(8,128)(2,1)} %get-tuple-element.134, f32[1,1024]{1,0:T(1,128)S(1)} %bitcast.35, bf16[4,1024,128]{2,1,0:T(8,128)(2,1)S(1)} %pad_maximum_fusion.mine_ref, ...), custom_call_target="tpu_custom_call" | custom-call | tf_op jit(solution)/shard_map/pallas_call | solution.py:117
  58.3 0.1 reshape.196
  58.4 32.4 %all_to_all.26 = bf16[64,3,4,128]{3,2,1,0:T(4,128)(2,1)S(1)} all-to-all(bf16[64,3,4,128]{3,2,1,0:T(4,128)(2,1)S(1)} %reshape.196), channel_id=1, replica_groups=mesh['y'=4,'core'=2,'z'=16,'x'=4] {'z','x'}, dimensions={0} | all-to-all | bytes 393216 | tf_op jit(solution)/shard_map/all_to_all | solution.py:17
  90.8 0.1 reduce_sum.43
  90.9 0.6 broadcast_in_dim.38
  91.5 4.2 %all-to-all-start.3 = ((bf16[16,3,4,128]{3,2,1,0:T(4,128)(2,1)}), bf16[16,3,4,128]{3,2,1,0:T(4,128)(2,1)S(1)}, u32[]{:S(2)}, u32[]{:S(2)}) async-start(bf16[16,3,4,128]{3,2,1,0:T(4,128)(2,1)} %broadcast_in_dim.38), calls=%async_computation.3 | async-start | bytes 98304 | tf_op jit(solution)/shard_map/all_to_all | solution.py:17
  95.7 11.6 %all-to-all-done.3 = bf16[16,3,4,128]{3,2,1,0:T(4,128)(2,1)S(1)} async-done(((bf16[16,3,4,128]{3,2,1,0:T(4,128)(2,1)}), bf16[16,3,4,128]{3,2,1,0:T(4,128)(2,1)S(1)}, u32[]{:S(2)}, u32[]{:S(2)}) %all-to-all-start.3) | async-done | bytes 49184 | tf_op jit(solution)/shard_map/all_to_all | solution.py:17
  107.6 0.9 broadcast_in_dim.40
  108.5 7.5 %all-to-all-start.4 = ((bf16[32,16,640]{2,1,0:T(8,128)(2,1)}), bf16[32,16,640]{2,1,0:T(8,128)(2,1)}, u32[]{:S(2)}, u32[]{:S(2)}) async-start(bf16[32,16,640]{2,1,0:T(8,128)(2,1)} %bitcast.16), calls=%async_computation.4 | async-start | bytes 1310720 | tf_op jit(solution)/shard_map/all_to_all | solution.py:17
  116.0 0.2 convert_reduce_fusion
  116.3 0.4 fusion.1.batch_spread_ref
  116.7 12.0 %all-to-all-done.4 = bf16[32,16,640]{2,1,0:T(8,128)(2,1)} async-done(((bf16[32,16,640]{2,1,0:T(8,128)(2,1)}), bf16[32,16,640]{2,1,0:T(8,128)(2,1)}, u32[]{:S(2)}, u32[]{:S(2)}) %all-to-all-start.4) | async-done | bytes 655392 | tf_op jit(solution)/shard_map/all_to_all | solution.py:17
  128.7 3.8 %shard_map.89 = (f32[1024,125]{1,0:T(8,128)}, f32[512,125]{1,0:T(8,128)}) custom-call(s32[4]{0:T(128)S(1)} %pad_add_fusion.1.at_ref, bf16[512,640]{1,0:T(8,128)(2,1)} %bitcast.17.arrived_ref, s32[1,512]{1,0:T(1,128)S(1)} %fusion.9.line_ref, f32[1,512]{1,0:T(1,128)S(1)} %bitcast.36, bf16[1024,512]{1,0:T(8,128)(2,1)S(1)} %fusion.2.vecs_ref.sub_vecs_ref, ...), custom_call_target="tpu_custom_call" | custom-call | tf_op jit(solution)/shard_map/pallas_call | solution.py:243
  (31 shorter events, 0.3 us)
Async XLA Ops:
  0.6 50.3 %copy-start = (bf16[512,512]{1,0:T(8,128)(2,1)S(1)}, bf16[512,512]{1,0:T(8,128)(2,1)}, u32[]{:S(2)}) copy-start(bf16[512,512]{1,0:T(8,128)(2,1)} %param.14) | copy-start | bytes 1572868
  0.6 2.8 %copy-start.1 = (f32[1024,125]{1,0:T(8,128)S(1)}, f32[1024,125]{1,0:T(8,128)}, u32[]{:S(2)}) copy-start(f32[1024,125]{1,0:T(8,128)} %weights_ref.1) | copy-start | bytes 1536004
  3.5 44.4 %copy-start.4 = (s32[512]{0:T(512)S(1)}, s32[512]{0:T(512)}, u32[]{:S(2)}) copy-start(s32[512]{0:T(512)} %param.12) | copy-start | bytes 6148
  3.5 45.3 %copy-start.5 = (s32[512]{0:T(512)S(1)}, s32[512]{0:T(512)}, u32[]{:S(2)}) copy-start(s32[512]{0:T(512)} %param.13) | copy-start | bytes 6148
  4.3 47.3 %all-to-all-start.1 = ((bf16[64,24,128]{2,1,0:T(8,128)(2,1)}), bf16[64,24,128]{2,1,0:T(8,128)(2,1)}, u32[]{:S(2)}, u32[]{:S(2)}) async-start(bf16[64,24,128]{2,1,0:T(8,128)(2,1)} %broadcast_in_dim.18), calls=%async_computation.1 | async-start | bytes 786432 | tf_op jit(solution)/shard_map/all_to_all | solution.py:17
  23.8 10.1 %collective-permute-start.2 = (bf16[1024,128]{1,0:T(8,128)(2,1)S(1)}, bf16[1024,128]{1,0:T(8,128)(2,1)S(1)}, u32[]{:S(2)}, u32[]{:S(2)}) collective-permute-start(bf16[1024,128]{1,0:T(8,128)(2,1)S(1)} %get-tuple-element.56), channel_id=1, source_target_pairs={{0,384},{128,0},{256,128},{384,256},{1,385},{129,1},{257,129},{385... | collective-permute-start | bytes 786440 | tf_op jit(solution)/shard_map/ppermute | solution.py:214
  28.4 10.9 %collective-permute-start = (bf16[1024,128]{1,0:T(8,128)(2,1)S(1)}, bf16[1024,128]{1,0:T(8,128)(2,1)S(1)}, u32[]{:S(2)}, u32[]{:S(2)}) collective-permute-start(bf16[1024,128]{1,0:T(8,128)(2,1)S(1)} %get-tuple-element.56), channel_id=1, source_target_pairs={{0,128},{128,256},{256,384},{384,0},{1,129},{129,257},{257,385},{3... | collective-permute-start | bytes 786440 | tf_op jit(solution)/shard_map/ppermute | solution.py:214
  30.3 12.5 %collective-permute-start.1 = (bf16[1024,128]{1,0:T(8,128)(2,1)S(1)}, bf16[1024,128]{1,0:T(8,128)(2,1)S(1)}, u32[]{:S(2)}, u32[]{:S(2)}) collective-permute-start(bf16[1024,128]{1,0:T(8,128)(2,1)S(1)} %get-tuple-element.56), channel_id=1, source_target_pairs={{0,256},{128,384},{256,0},{384,128},{1,257},{129,385},{257,1},{385... | collective-permute-start | bytes 786440 | tf_op jit(solution)/shard_map/ppermute | solution.py:213
  43.0 11.4 %collective-permute-start.3 = (bf16[4,1024,128]{2,1,0:T(8,128)(2,1)S(1)}, bf16[4,1024,128]{2,1,0:T(8,128)(2,1)}, u32[]{:S(2)}, u32[]{:S(2)}) collective-permute-start(bf16[4,1024,128]{2,1,0:T(8,128)(2,1)S(1)} %pad_maximum_fusion.mine_ref), channel_id=1, source_target_pairs={{0,64},{64,0},{1,65},{65,1},{2,66},{66,2},{3,67},{67,3},{4,68},{68... | collective-permute-start | bytes 3145736 | tf_op jit(solution)/shard_map/ppermute | solution.py:216
  91.5 15.8 %all-to-all-start.3 = ((bf16[16,3,4,128]{3,2,1,0:T(4,128)(2,1)}), bf16[16,3,4,128]{3,2,1,0:T(4,128)(2,1)S(1)}, u32[]{:S(2)}, u32[]{:S(2)}) async-start(bf16[16,3,4,128]{3,2,1,0:T(4,128)(2,1)} %broadcast_in_dim.38), calls=%async_computation.3 | async-start | bytes 98304 | tf_op jit(solution)/shard_map/all_to_all | solution.py:17
  95.7 33.0 %copy-start.2 = (f32[512,125]{1,0:T(8,128)S(1)}, f32[512,125]{1,0:T(8,128)}, u32[]{:S(2)}) copy-start(f32[512,125]{1,0:T(8,128)} %targets_ref.1) | copy-start | bytes 768004
  95.7 33.0 %copy-start.3 = (f32[512]{0:T(512)S(1)}, f32[512]{0:T(512)}, u32[]{:S(2)}) copy-start(f32[512]{0:T(512)} %param.15) | copy-start | bytes 6148
  108.5 20.3 %all-to-all-start.4 = ((bf16[32,16,640]{2,1,0:T(8,128)(2,1)}), bf16[32,16,640]{2,1,0:T(8,128)(2,1)}, u32[]{:S(2)}, u32[]{:S(2)}) async-start(bf16[32,16,640]{2,1,0:T(8,128)(2,1)} %bitcast.16), calls=%async_computation.4 | async-start | bytes 1310720 | tf_op jit(solution)/shard_map/all_to_all | solution.py:17

commit v8 on v6

--- a/solution.py
+++ b/solution.py
@@ -15,10 +15,6 @@
 
 def exchanged(pieces, axes):
     return lax.all_to_all(pieces, axes, split_axis=0, concat_axis=0, tiled=True)
-
-
-def copied_to_all(shard, axes):
-    return exchanged(jnp.broadcast_to(shard, (lax.axis_size(axes), *shard.shape)), axes)
 
 
 def one_hot_columns(rows, length):
@@ -52,7 +48,7 @@
     return jnp.sum((rows < edge).astype(jnp.float32), axis=1, keepdims=True).astype(jnp.int32)
 
 
-def pick_kernel(at_ref, rows_ref, centers_ref, out_ref):
+def pick_kernel(at_ref, rows_ref, centers_ref, out_ref, norm_ref, most_ref, *, nctr):
     count = centers_ref.shape[0]
     base, slice_at, step, nout = at_ref[0] * count, at_ref[1], at_ref[2], at_ref[3]
     rows = rows_ref[...]
@@ -68,6 +64,12 @@
         pick, centers_ref[...], (((0,), (0,)), ((), ())), preferred_element_type=jnp.float32
     )
     out_ref[...] = found[: out_ref.shape[0]].astype(jnp.bfloat16)
+    wide = centers_ref[...].astype(jnp.float32)
+    norm = jnp.sum(wide * wide, axis=1, keepdims=True)
+    norm_ref[...] = jnp.transpose(jnp.broadcast_to(norm, (count, LANES)))[:1]
+    edges = lax.broadcasted_iota(jnp.int32, (nctr, 1), 0) * count
+    most = jnp.max(rows_below(rows, edges + count) - rows_below(rows, edges), axis=0, keepdims=True)
+    most_ref[...] = most
 
 
 def slot_kernel(at_ref, rows_ref, arrived_ref, out_ref, *, count):
@@ -181,9 +183,6 @@
     block = batch // nout
     base = place * row_count
 
-    edges = jnp.arange(nctr, dtype=jnp.int32)[:, None] * row_count
-    owned = (batch_rows[None, :] >= edges) & (batch_rows[None, :] < edges + row_count)
-    most = jnp.max(jnp.sum(owned.astype(jnp.int32), axis=1))
     batch_line = batch_rows[None, :]
 
     def places(turn):
@@ -191,21 +190,28 @@
 
     def round_of(turn):
         at = places(turn)
-        shape = jax.ShapeDtypeStruct((ROUND, feature_count), low)
-        share = whole(pick_kernel, shape, 2)(at, batch_line, centers)
-        arrived = copied_to_all(share.reshape(-1, LANES), CTR)
+        shapes = (
+            jax.ShapeDtypeStruct((ROUND, feature_count), low),
+            jax.ShapeDtypeStruct((1, row_count), jnp.float32),
+            jax.ShapeDtypeStruct((1, 1), jnp.int32),
+        )
+        pick = functools.partial(pick_kernel, nctr=nctr)
+        share, norm, most = whole(pick, shapes, 2)(at, batch_line, centers)
+        arrived = lax.all_gather(share.reshape(-1, LANES), CTR, axis=0, tiled=True)
         arrived = arrived.reshape(nctr * ROUND, feature_count)
         shape = jax.ShapeDtypeStruct((block, feature_count), low)
         slot = functools.partial(slot_kernel, count=row_count)
-        return whole(slot, shape, 2)(at, batch_line, arrived)
+        return whole(slot, shape, 2)(at, batch_line, arrived), norm, most
+
+    feats, right_norm, most = round_of(0)
+    most = most[0, 0]
 
     def more(carry):
         return carry[0] * (ROUND * nout) < most
 
     def next_round(carry):
-        return carry[0] + 1, carry[1] + round_of(carry[0])
-
-    feats = round_of(0)
+        return carry[0] + 1, carry[1] + round_of(carry[0])[0]
+
     _, feats = lax.while_loop(more, next_round, (jnp.int32(1), feats))
 
     weights_low = jnp.pad(weights.astype(low), ((0, 0), (0, LANES - columns)))
@@ -219,13 +225,12 @@
     other = lax.ppermute(mine, "core", [(i, (i + 1) % ncore) for i in range(ncore)])
 
     sub_vecs = dot(one_hot_columns(subsample - base, row_count), eigvecs).astype(low)
-    right_norm = jnp.sum(jnp.square(centers.astype(jnp.float32)), axis=1)
-    parts = products(places(0), feats, centers, right_norm[None, :], mine, other, sub_vecs)
+    parts = products(places(0), feats, centers, right_norm, mine, other, sub_vecs)
 
     blocks = parts.shape[1] // LANES
     arrived = exchanged(parts.reshape(nctr, blocks // 4, 4, LANES), CTR)
     share = arrived.astype(jnp.float32).sum(axis=0).astype(low)
-    share = copied_to_all(share, "z").reshape(nz, blocks, LANES)
+    share = lax.all_gather(share.reshape(blocks, LANES), "z", axis=0)
     heads = jnp.moveaxis(share[:, :nout], 1, 0).reshape(ncore, ny, nz, LANES)
     heads = by_owner(by_owner(heads, 0, "core"), 1, "y")
     heads = jnp.moveaxis(heads, 0, 1).reshape(nout, nz, LANES)

time: 133 us -> 209 us (1.57)
  blocking collectives: 32.4 us -> 99 us
  starting transfers between devices: 46 us -> 61.3 us
    all_gather x0 -> x2, blocking collectives: none -> 99 us  [the longest x1 77.8 us: round_of(): arrived = lax.all_gather(share.reshape(-1, LANES), CTR, axis=0, tiled=True)]
    all_to_all x1 -> x0, blocking collectives: 32.4 us -> none  [exchanged(): return lax.all_to_all(pieces, axes, split_axis=0, concat_axis=0, tiled=True)]
    ppermute x1, starting transfers between devices: 4.89 us -> 27.3 us  [body(): lax.ppermute(mine, 'core', [(i, (i + 1) % ncore) for i in range(ncore)])]
    ppermute x3, waiting for transfers between devices: 8.98 us -> 0.01 us  [body(): lax.ppermute(weights_low, 'y', [(i, (i + dy) % ny) for i in range(ny)])]
    all_to_all x3 -> x2, starting transfers between devices: 31 us -> 23.2 us  [exchanged(): return lax.all_to_all(pieces, axes, split_axis=0, concat_axis=0, tiled=True)]
    all_to_all x3 -> x2, waiting for transfers between devices: 23.6 us -> 29.5 us  [exchanged(): return lax.all_to_all(pieces, axes, split_axis=0, concat_axis=0, tiled=True)]
    reduce_sum x2 -> x0, other arithmetic: 2.25 us -> none  [the longest x1 2.07 us: body(): right_norm = jnp.sum(jnp.square(centers.astype(jnp.float32)), axis=1)]
  transfers between devices with their start and end apart: 7 -> 6, of which waited for: 4 -> 3; matrix products, arithmetic and copies ran while one was open for 4% -> 1% of each run, Pallas kernels for 1% -> 2%
where the time goes in v8:
time: 209 us
  blocking collectives  99 us (47%)
  starting transfers between devices  61.3 us (29%)
  waiting for transfers between devices  30.6 us (15%)
  Pallas kernels  11.3 us (5%)
  other arithmetic  2.28 us (1%)
    all_gather x1, blocking collectives, round_of(): arrived = lax.all_gather(share.reshape(-1, LANES), CTR, axis=0, tiled=True)  77.8 us
    all_to_all x2, waiting for transfers between devices, exchanged(): return lax.all_to_all(pieces, axes, split_axis=0, concat_axis=0, tiled=True)  29.5 us
    ppermute x1, starting transfers between devices, body(): lax.ppermute(mine, 'core', [(i, (i + 1) % ncore) for i in range(ncore)])  27.3 us
    all_to_all x2, starting transfers between devices, exchanged(): return lax.all_to_all(pieces, axes, split_axis=0, concat_axis=0, tiled=True)  23.2 us
    all_gather x1, blocking collectives, body(): share = lax.all_gather(share.reshape(blocks, LANES), 'z', axis=0)  21.1 us
    ppermute x3, starting transfers between devices, body(): lax.ppermute(weights_low, 'y', [(i, (i + dy) % ny) for i in range(ny)])  10.9 us
  transfers between devices with their start and end apart: 6, of which 3 were waited for; matrix products, arithmetic and copies ran while one was open for 1% of the time, Pallas kernels for 2%

profile of v8, /device:TPU:1, one launch (start us, length us, event | category | flops | bytes accessed | tf_op | source)
XLA Modules:
  0.0 208.7 jit_solution(13993941382677705795)
XLA Ops:
  0.6 0.0 copy-start
  0.6 1.1 convert_element_type.17
  1.8 0.0 copy-start.4
  1.8 0.1 pad_bitcast_fusion
  1.9 0.0 copy-start.5
  1.9 5.5 %collective-permute-start.2 = (bf16[1024,128]{1,0:T(8,128)(2,1)S(1)}, bf16[1024,128]{1,0:T(8,128)(2,1)S(1)}, u32[]{:S(2)}, u32[]{:S(2)}) collective-permute-start(bf16[1024,128]{1,0:T(8,128)(2,1)S(1)} %get-tuple-element.63), channel_id=1, source_target_pairs={{0,384},{128,0},{256,128},{384,256},{1,385},{129,1},{257,129},{385... | collective-permute-start | bytes 786440 | tf_op jit(solution)/shard_map/ppermute | solution.py:221
  7.3 1.9 collective-permute-start
  9.3 3.5 %collective-permute-start.1 = (bf16[1024,128]{1,0:T(8,128)(2,1)S(1)}, bf16[1024,128]{1,0:T(8,128)(2,1)S(1)}, u32[]{:S(2)}, u32[]{:S(2)}) collective-permute-start(bf16[1024,128]{1,0:T(8,128)(2,1)S(1)} %get-tuple-element.63), channel_id=1, source_target_pairs={{0,256},{128,384},{256,0},{384,128},{1,257},{129,385},{257,1},{385... | collective-permute-start | bytes 786440 | tf_op jit(solution)/shard_map/ppermute | solution.py:221
  12.8 0.1 pad_add_fusion.1.at_ref
  12.9 3.3 %shard_map.86 = (bf16[3,1024]{1,0:T(4,128)(2,1)S(1)}, f32[1,1024]{1,0:T(1,128)S(1)}, s32[1,1]{1,0:T(1,128)}) custom-call(s32[4]{0:T(128)S(1)} %pad_add_fusion.1.at_ref, s32[1,512]{1,0:T(1,128)} %bitcast.34, bf16[1024,1024]{1,0:T(8,128)(2,1)} %centers_ref.3), custom_call_target="tpu_custom_call" | custom-call | tf_op jit(solution)/shard_map/pallas_call | solution.py:199
  16.3 77.8 %all_gather.9 = bf16[1536,128]{1,0:T(8,128)(2,1)S(1)} all-gather(bf16[24,128]{1,0:T(8,128)(2,1)S(1)} %reshape.183), channel_id=1, replica_groups=mesh['y'=4,'core'=2,'z'=16,'x'=4] {'z','x'}, dimensions={0}, use_global_device_ids=true | all-gather | bytes 399360 | tf_op jit(solution)/shard_map/all_gather | solution.py:200
  94.1 0.2 reshape.184.arrived_ref
  94.3 0.9 shard_map.87
  95.3 0.0 collective-permute-done.2
  95.3 0.0 collective-permute-done.1
  95.3 0.1 pad_maximum_fusion.mine_ref
  95.4 27.3 %collective-permute-start.3 = (bf16[4,1024,128]{2,1,0:T(8,128)(2,1)S(1)}, bf16[4,1024,128]{2,1,0:T(8,128)(2,1)}, u32[]{:S(2)}, u32[]{:S(2)}) collective-permute-start(bf16[4,1024,128]{2,1,0:T(8,128)(2,1)S(1)} %pad_maximum_fusion.mine_ref), channel_id=1, source_target_pairs={{0,64},{64,0},{1,65},{65,1},{2,66},{66,2},{3,67},{67,3},{4,68},{68... | collective-permute-start | bytes 3145736 | tf_op jit(solution)/shard_map/ppermute | solution.py:225
  122.7 0.7 fusion.2.vecs_ref.sub_vecs_ref
  123.5 0.6 while.10
  124.0 1.1 collective-permute-done.3.other_ref
  125.1 3.2 %shard_map.88 = bf16[64,1536]{1,0:T(8,128)(2,1)S(1)} custom-call(s32[4]{0:T(128)S(1)} %pad_add_fusion.1.at_ref, bf16[64,1024]{1,0:T(8,128)(2,1)S(1)} %get-tuple-element.46.feats_ref, bf16[1024,1024]{1,0:T(8,128)(2,1)} %get-tuple-element.141, f32[1,1024]{1,0:T(1,128)S(1)} %get-tuple-element.47.norm_ref, bf16[4,1024,128]{2,1,0:T(8,128)(2,1)S(1)} %pad_maximum_fusion.mine_ref, ...), custom_call_target="tpu_custom_call" | custom-call | tf_op jit(solution)/shard_map/pallas_call | solution.py:119
  128.3 0.7 reshape.185
  129.1 9.2 %all-to-all-start = ((bf16[64,3,4,128]{3,2,1,0:T(4,128)(2,1)}), bf16[64,3,4,128]{3,2,1,0:T(4,128)(2,1)S(1)}, u32[]{:S(2)}, u32[]{:S(2)}) async-start(bf16[64,3,4,128]{3,2,1,0:T(4,128)(2,1)} %reshape.185), calls=%async_computation | async-start | bytes 393216 | tf_op jit(solution)/shard_map/all_to_all | solution.py:17
  138.3 17.6 %all-to-all-done = bf16[64,3,4,128]{3,2,1,0:T(4,128)(2,1)S(1)} async-done(((bf16[64,3,4,128]{3,2,1,0:T(4,128)(2,1)}), bf16[64,3,4,128]{3,2,1,0:T(4,128)(2,1)S(1)}, u32[]{:S(2)}, u32[]{:S(2)}) %all-to-all-start) | async-done | bytes 196640 | tf_op jit(solution)/shard_map/all_to_all | solution.py:17
  155.9 0.1 reduce_sum.23
  156.1 21.1 %all_gather.10 = bf16[16,12,128]{2,1,0:T(8,128)(2,1)S(1)} all-gather(bf16[1,12,128]{2,1,0:T(8,128)(2,1)S(1)} %all_gather_reshape.3), channel_id=1, replica_groups=mesh['y'=4,'core'=2,'z'=16,'x'=4] {'z'}, dimensions={0}, use_global_device_ids=true | all-gather | bytes 52224 | tf_op jit(solution)/shard_map/all_gather | solution.py:233
  177.4 0.9 broadcast_in_dim.10
  178.4 13.9 %all-to-all-start.1 = ((bf16[32,16,640]{2,1,0:T(8,128)(2,1)}), bf16[32,16,640]{2,1,0:T(8,128)(2,1)}, u32[]{:S(2)}, u32[]{:S(2)}) async-start(bf16[32,16,640]{2,1,0:T(8,128)(2,1)} %bitcast.15), calls=%async_computation.1 | async-start | bytes 1310720 | tf_op jit(solution)/shard_map/all_to_all | solution.py:17
  192.3 0.2 convert_reduce_fusion
  192.6 0.4 fusion.1.batch_spread_ref
  193.0 11.9 %all-to-all-done.1 = bf16[32,16,640]{2,1,0:T(8,128)(2,1)} async-done(((bf16[32,16,640]{2,1,0:T(8,128)(2,1)}), bf16[32,16,640]{2,1,0:T(8,128)(2,1)}, u32[]{:S(2)}, u32[]{:S(2)}) %all-to-all-start.1) | async-done | bytes 655392 | tf_op jit(solution)/shard_map/all_to_all | solution.py:17
  204.9 3.8 %shard_map.89 = (f32[1024,125]{1,0:T(8,128)}, f32[512,125]{1,0:T(8,128)}) custom-call(s32[4]{0:T(128)S(1)} %pad_add_fusion.1.at_ref, bf16[512,640]{1,0:T(8,128)(2,1)} %bitcast.16.arrived_ref, s32[1,512]{1,0:T(1,128)S(1)} %fusion.9.line_ref, f32[1,512]{1,0:T(1,128)S(1)} %bitcast.33, bf16[1024,512]{1,0:T(8,128)(2,1)S(1)} %fusion.2.vecs_ref.sub_vecs_ref, ...), custom_call_target="tpu_custom_call" | custom-call | tf_op jit(solution)/shard_map/pallas_call | solution.py:251
  (26 shorter events, 0.3 us)
Async XLA Ops:
  0.6 122.1 %copy-start = (bf16[512,512]{1,0:T(8,128)(2,1)S(1)}, bf16[512,512]{1,0:T(8,128)(2,1)}, u32[]{:S(2)}) copy-start(bf16[512,512]{1,0:T(8,128)(2,1)} %param.14) | copy-start | bytes 1572868
  1.8 92.5 %copy-start.4 = (s32[512]{0:T(512)S(1)}, s32[512]{0:T(512)}, u32[]{:S(2)}) copy-start(s32[512]{0:T(512)} %param.12) | copy-start | bytes 6148
  1.9 93.4 %copy-start.5 = (s32[512]{0:T(512)S(1)}, s32[512]{0:T(512)}, u32[]{:S(2)}) copy-start(s32[512]{0:T(512)} %param.13) | copy-start | bytes 6148
  1.9 93.4 %collective-permute-start.2 = (bf16[1024,128]{1,0:T(8,128)(2,1)S(1)}, bf16[1024,128]{1,0:T(8,128)(2,1)S(1)}, u32[]{:S(2)}, u32[]{:S(2)}) collective-permute-start(bf16[1024,128]{1,0:T(8,128)(2,1)S(1)} %get-tuple-element.63), channel_id=1, source_target_pairs={{0,384},{128,0},{256,128},{384,256},{1,385},{129,1},{257,129},{385... | collective-permute-start | bytes 786440 | tf_op jit(solution)/shard_map/ppermute | solution.py:221
  7.3 87.9 %collective-permute-start = (bf16[1024,128]{1,0:T(8,128)(2,1)S(1)}, bf16[1024,128]{1,0:T(8,128)(2,1)S(1)}, u32[]{:S(2)}, u32[]{:S(2)}) collective-permute-start(bf16[1024,128]{1,0:T(8,128)(2,1)S(1)} %get-tuple-element.63), channel_id=1, source_target_pairs={{0,128},{128,256},{256,384},{384,0},{1,129},{129,257},{257,385},{3... | collective-permute-start | bytes 786440 | tf_op jit(solution)/shard_map/ppermute | solution.py:221
  9.3 86.0 %collective-permute-start.1 = (bf16[1024,128]{1,0:T(8,128)(2,1)S(1)}, bf16[1024,128]{1,0:T(8,128)(2,1)S(1)}, u32[]{:S(2)}, u32[]{:S(2)}) collective-permute-start(bf16[1024,128]{1,0:T(8,128)(2,1)S(1)} %get-tuple-element.63), channel_id=1, source_target_pairs={{0,256},{128,384},{256,0},{384,128},{1,257},{129,385},{257,1},{385... | collective-permute-start | bytes 786440 | tf_op jit(solution)/shard_map/ppermute | solution.py:221
  95.4 29.7 %collective-permute-start.3 = (bf16[4,1024,128]{2,1,0:T(8,128)(2,1)S(1)}, bf16[4,1024,128]{2,1,0:T(8,128)(2,1)}, u32[]{:S(2)}, u32[]{:S(2)}) collective-permute-start(bf16[4,1024,128]{2,1,0:T(8,128)(2,1)S(1)} %pad_maximum_fusion.mine_ref), channel_id=1, source_target_pairs={{0,64},{64,0},{1,65},{65,1},{2,66},{66,2},{3,67},{67,3},{4,68},{68... | collective-permute-start | bytes 3145736 | tf_op jit(solution)/shard_map/ppermute | solution.py:225
  129.1 26.9 %all-to-all-start = ((bf16[64,3,4,128]{3,2,1,0:T(4,128)(2,1)}), bf16[64,3,4,128]{3,2,1,0:T(4,128)(2,1)S(1)}, u32[]{:S(2)}, u32[]{:S(2)}) async-start(bf16[64,3,4,128]{3,2,1,0:T(4,128)(2,1)} %reshape.185), calls=%async_computation | async-start | bytes 393216 | tf_op jit(solution)/shard_map/all_to_all | solution.py:17
  177.2 27.7 %copy-start.1 = (f32[1024,125]{1,0:T(8,128)S(1)}, f32[1024,125]{1,0:T(8,128)}, u32[]{:S(2)}) copy-start(f32[1024,125]{1,0:T(8,128)} %weights_ref.1) | copy-start | bytes 1536004
  177.2 27.7 %copy-start.2 = (f32[512,125]{1,0:T(8,128)S(1)}, f32[512,125]{1,0:T(8,128)}, u32[]{:S(2)}) copy-start(f32[512,125]{1,0:T(8,128)} %targets_ref.1) | copy-start | bytes 768004
  177.2 27.7 %copy-start.3 = (f32[512]{0:T(512)S(1)}, f32[512]{0:T(512)}, u32[]{:S(2)}) copy-start(f32[512]{0:T(512)} %param.15) | copy-start | bytes 6148
  178.4 26.6 %all-to-all-start.1 = ((bf16[32,16,640]{2,1,0:T(8,128)(2,1)}), bf16[32,16,640]{2,1,0:T(8,128)(2,1)}, u32[]{:S(2)}, u32[]{:S(2)}) async-start(bf16[32,16,640]{2,1,0:T(8,128)(2,1)} %bitcast.15), calls=%async_computation.1 | async-start | bytes 1310720 | tf_op jit(solution)/shard_map/all_to_all | solution.py:17

commit v9 on v8

--- a/solution.py
+++ b/solution.py
@@ -17,6 +17,10 @@
     return lax.all_to_all(pieces, axes, split_axis=0, concat_axis=0, tiled=True)
 
 
+def copied_to_all(shard, axes):
+    return exchanged(jnp.broadcast_to(shard, (lax.axis_size(axes), *shard.shape)), axes)
+
+
 def one_hot_columns(rows, length):
     return (lax.broadcasted_iota(jnp.int32, (length, rows.shape[0]), 0) == rows[None, :]).astype(
         jnp.bfloat16
@@ -33,12 +37,14 @@
     return lax.dynamic_slice_in_dim(back, size - 1 - lax.axis_index(name), size, axis=dim)
 
 
-def whole(kernel, shape, count):
+def whole(kernel, shape, count, left=0, scratch=()):
     vmem = pl.BlockSpec(memory_space=pltpu.VMEM)
+    hbm = pl.BlockSpec(memory_space=pltpu.HBM)
     return pl.pallas_call(
         kernel,
         out_shape=shape,
-        in_specs=[pl.BlockSpec(memory_space=pltpu.SMEM)] + [vmem] * count,
+        in_specs=[pl.BlockSpec(memory_space=pltpu.SMEM)] + [vmem] * count + [hbm] * left,
+        scratch_shapes=scratch,
         out_specs=jax.tree.map(lambda _: vmem, shape),
         compiler_params=pltpu.CompilerParams(vmem_limit_bytes=12 << 20),
     )
@@ -128,12 +134,16 @@
     scale_ref,
     sub_vecs_ref,
     batch_spread_ref,
+    targets_ref,
     weights_ref,
-    targets_ref,
     updated_ref,
     residual_ref,
+    held_ref,
+    done,
 ):
     del at_ref
+    fetch = pltpu.make_async_copy(weights_ref, held_ref, done)
+    fetch.start()
     low = jnp.bfloat16
     columns = weights_ref.shape[1]
     count, ranks = line_ref.shape[1], scale_ref.shape[1]
@@ -164,8 +174,9 @@
     )
     scale = jnp.sum(jnp.where(diagonal, scale_ref[...], 0.0), axis=1, keepdims=True)
     correction = (step_size * scale * coefficient).astype(low)
+    fetch.wait()
     updated_ref[...] = (
-        weights_ref[...]
+        held_ref[...]
         + dot(sub_vecs_ref[...], correction)
         - step_size * dot(batch_spread_ref[...], residual)
     )
@@ -197,7 +208,7 @@
         )
         pick = functools.partial(pick_kernel, nctr=nctr)
         share, norm, most = whole(pick, shapes, 2)(at, batch_line, centers)
-        arrived = lax.all_gather(share.reshape(-1, LANES), CTR, axis=0, tiled=True)
+        arrived = copied_to_all(share.reshape(-1, LANES), CTR)
         arrived = arrived.reshape(nctr * ROUND, feature_count)
         shape = jax.ShapeDtypeStruct((block, feature_count), low)
         slot = functools.partial(slot_kernel, count=row_count)
@@ -215,13 +226,11 @@
     _, feats = lax.while_loop(more, next_round, (jnp.int32(1), feats))
 
     weights_low = jnp.pad(weights.astype(low), ((0, 0), (0, LANES - columns)))
-    mine = jnp.stack(
-        [weights_low]
-        + [
-            lax.ppermute(weights_low, "y", [(i, (i + dy) % ny) for i in range(ny)])
-            for dy in range(1, ny)
-        ]
-    )
+    ahead = [(i, (i + 1) % ny) for i in range(ny)]
+    back = [(i, (i - 1) % ny) for i in range(ny)]
+    one, three = lax.ppermute(weights_low, "y", ahead), lax.ppermute(weights_low, "y", back)
+    two = lax.ppermute(one, "y", ahead)
+    mine = jnp.stack([weights_low, one, two, three])
     other = lax.ppermute(mine, "core", [(i, (i + 1) % ncore) for i in range(ncore)])
 
     sub_vecs = dot(one_hot_columns(subsample - base, row_count), eigvecs).astype(low)
@@ -230,7 +239,7 @@
     blocks = parts.shape[1] // LANES
     arrived = exchanged(parts.reshape(nctr, blocks // 4, 4, LANES), CTR)
     share = arrived.astype(jnp.float32).sum(axis=0).astype(low)
-    share = lax.all_gather(share.reshape(blocks, LANES), "z", axis=0)
+    share = copied_to_all(share, "z").reshape(nz, blocks, LANES)
     heads = jnp.moveaxis(share[:, :nout], 1, 0).reshape(ncore, ny, nz, LANES)
     heads = by_owner(by_owner(heads, 0, "core"), 1, "y")
     heads = jnp.moveaxis(heads, 0, 1).reshape(nout, nz, LANES)
@@ -248,15 +257,16 @@
         jax.ShapeDtypeStruct(weights.shape, jnp.float32),
         jax.ShapeDtypeStruct(targets.shape, jnp.float32),
     )
-    return whole(tail_kernel, shapes, 7)(
+    scratch = (pltpu.VMEM(weights.shape, jnp.float32), pltpu.SemaphoreType.DMA)
+    return whole(tail_kernel, shapes, 6, 1, scratch)(
         places(0),
         arrived,
         line[None, :],
         eig_scale[None, :],
         sub_vecs,
         batch_spread,
+        targets,
         weights,
-        targets,
     )
 
 

time: 209 us -> 131 us (0.63)
  blocking collectives: 99 us -> 32.1 us
  starting transfers between devices: 61.3 us -> 43.9 us
  waiting for transfers between devices: 30.6 us -> 34.8 us
    all_gather x2 -> x0, blocking collectives: 99 us -> none  [the longest x1 77.8 us: round_of(): arrived = lax.all_gather(share.reshape(-1, LANES), CTR, axis=0, tiled=True)]
    all_to_all x0 -> x1, blocking collectives: none -> 32.1 us  [exchanged(): return lax.all_to_all(pieces, axes, split_axis=0, concat_axis=0, tiled=True)]
    ppermute x1, starting transfers between devices: 27.3 us -> 4.3 us  [body(): lax.ppermute(mine, 'core', [(i, (i + 1) % ncore) for i in range(ncore)])]
    ppermute x3, waiting for transfers between devices: 0.01 us -> 11.2 us  [the longest x1 7.5 us: body(): two = lax.ppermute(one, 'y', ahead)]
    all_to_all x2 -> x3, starting transfers between devices: 23.2 us -> 31.1 us  [exchanged(): return lax.all_to_all(pieces, axes, split_axis=0, concat_axis=0, tiled=True)]
    all_to_all x2 -> x3, waiting for transfers between devices: 29.5 us -> 23.6 us  [exchanged(): return lax.all_to_all(pieces, axes, split_axis=0, concat_axis=0, tiled=True)]
    ppermute x3, starting transfers between devices: 10.9 us -> 8.47 us  [the longest x1 3.36 us: body(): lax.ppermute(weights_low, 'y', back)]
  transfers between devices with their start and end apart: 6 -> 7, of which waited for: 3 -> 4; matrix products, arithmetic and copies ran while one was open for 1% -> 2% of each run, Pallas kernels for 2% -> 1%
where the time goes in v9:
time: 131 us; the launch traced here: 130 us
  starting transfers between devices  43.9 us (34%)
  waiting for transfers between devices  34.8 us (27%)
  blocking collectives  32.1 us (25%)
  Pallas kernels  12.2 us (9%)
  local copies, waits for them, and re-layouts  3.74 us (3%)
    all_to_all x1, blocking collectives, exchanged(): return lax.all_to_all(pieces, axes, split_axis=0, concat_axis=0, tiled=True)  32.1 us
    all_to_all x3, starting transfers between devices, exchanged(): return lax.all_to_all(pieces, axes, split_axis=0, concat_axis=0, tiled=True)  31.1 us
    all_to_all x3, waiting for transfers between devices, exchanged(): return lax.all_to_all(pieces, axes, split_axis=0, concat_axis=0, tiled=True)  23.6 us
    ppermute x1, waiting for transfers between devices, body(): two = lax.ppermute(one, 'y', ahead)  7.5 us
    ppermute x1, starting transfers between devices, body(): lax.ppermute(mine, 'core', [(i, (i + 1) % ncore) for i in range(ncore)])  4.3 us
    pallas_call x1, Pallas kernels, body(): whole(tail_kernel, shapes, 6, 1, scratch)  3.96 us
    ppermute x1, waiting for transfers between devices, body(): lax.ppermute(weights_low, 'y', ahead)  3.68 us
    pallas_call x1, Pallas kernels, round_of(): share, norm, most = whole(pick, shapes, 2)(at, batch_line, centers)  3.43 us
  transfers between devices with their start and end apart: 7, of which 4 were waited for; matrix products, arithmetic and copies ran while one was open for 2% of the time, Pallas kernels for 1%

profile of v9, /device:TPU:1, one launch (start us, length us, event | category | flops | bytes accessed | tf_op | source)
XLA Modules:
  0.0 130.2 jit_solution(9130102464445735582)
XLA Ops:
  0.6 0.0 copy-start
  0.7 0.1 pad_add_fusion.1.at_ref
  0.7 3.4 %shard_map.86 = (bf16[3,1024]{1,0:T(4,128)(2,1)S(1)}, f32[1,1024]{1,0:T(1,128)S(1)}, s32[1,1]{1,0:T(1,128)}) custom-call(s32[4]{0:T(128)S(1)} %pad_add_fusion.1.at_ref, s32[1,512]{1,0:T(1,128)} %bitcast.36, bf16[1024,1024]{1,0:T(8,128)(2,1)} %centers_ref.3), custom_call_target="tpu_custom_call" | custom-call | tf_op jit(solution)/shard_map/pallas_call | solution.py:210
  4.2 0.8 broadcast_in_dim.30
  5.0 19.5 %all-to-all-start.1 = ((bf16[64,24,128]{2,1,0:T(8,128)(2,1)}), bf16[64,24,128]{2,1,0:T(8,128)(2,1)}, u32[]{:S(2)}, u32[]{:S(2)}) async-start(bf16[64,24,128]{2,1,0:T(8,128)(2,1)} %broadcast_in_dim.30), calls=%async_computation.1 | async-start | bytes 786432 | tf_op jit(solution)/shard_map/all_to_all | solution.py:17
  24.5 0.1 pad_bitcast_fusion
  24.6 3.2 %collective-permute-start = (bf16[1024,128]{1,0:T(8,128)(2,1)S(1)}, bf16[1024,128]{1,0:T(8,128)(2,1)S(1)}, u32[]{:S(2)}, u32[]{:S(2)}) collective-permute-start(bf16[1024,128]{1,0:T(8,128)(2,1)S(1)} %get-tuple-element.63), channel_id=1, source_target_pairs={{0,128},{128,256},{256,384},{384,0},{1,129},{129,257},{257,385},{3... | collective-permute-start | bytes 786440 | tf_op jit(solution)/shard_map/ppermute | solution.py:231
  27.8 3.4 %collective-permute-start.2 = (bf16[1024,128]{1,0:T(8,128)(2,1)S(1)}, bf16[1024,128]{1,0:T(8,128)(2,1)S(1)}, u32[]{:S(2)}, u32[]{:S(2)}) collective-permute-start(bf16[1024,128]{1,0:T(8,128)(2,1)S(1)} %get-tuple-element.63), channel_id=1, source_target_pairs={{0,384},{128,0},{256,128},{384,256},{1,385},{129,1},{257,129},{385... | collective-permute-start | bytes 786440 | tf_op jit(solution)/shard_map/ppermute | solution.py:231
  31.2 3.7 %collective-permute-done = bf16[1024,128]{1,0:T(8,128)(2,1)S(1)} collective-permute-done((bf16[1024,128]{1,0:T(8,128)(2,1)S(1)}, bf16[1024,128]{1,0:T(8,128)(2,1)S(1)}, u32[]{:S(2)}, u32[]{:S(2)}) %collective-permute-start) | collective-permute-done | bytes 262176 | tf_op jit(solution)/shard_map/ppermute | solution.py:231
  34.9 1.9 %collective-permute-start.1 = (bf16[1024,128]{1,0:T(8,128)(2,1)S(1)}, bf16[1024,128]{1,0:T(8,128)(2,1)S(1)}, u32[]{:S(2)}, u32[]{:S(2)}) collective-permute-start(bf16[1024,128]{1,0:T(8,128)(2,1)S(1)} %collective-permute-done), channel_id=1, source_target_pairs={{0,128},{128,256},{256,384},{384,0},{1,129},{129,257},{257,385},{3... | collective-permute-start | bytes 786440 | tf_op jit(solution)/shard_map/ppermute | solution.py:232
  36.8 7.5 %collective-permute-done.1 = bf16[1024,128]{1,0:T(8,128)(2,1)S(1)} collective-permute-done((bf16[1024,128]{1,0:T(8,128)(2,1)S(1)}, bf16[1024,128]{1,0:T(8,128)(2,1)S(1)}, u32[]{:S(2)}, u32[]{:S(2)}) %collective-permute-start.1) | collective-permute-done | bytes 262176 | tf_op jit(solution)/shard_map/ppermute | solution.py:232
  44.3 0.1 pad_maximum_fusion.mine_ref
  44.4 0.0 copy-start.4
  44.4 4.3 %collective-permute-start.3 = (bf16[4,1024,128]{2,1,0:T(8,128)(2,1)S(1)}, bf16[4,1024,128]{2,1,0:T(8,128)(2,1)}, u32[]{:S(2)}, u32[]{:S(2)}) collective-permute-start(bf16[4,1024,128]{2,1,0:T(8,128)(2,1)S(1)} %pad_maximum_fusion.mine_ref), channel_id=1, source_target_pairs={{0,64},{64,0},{1,65},{65,1},{2,66},{66,2},{3,67},{67,3},{4,68},{68... | collective-permute-start | bytes 3145736 | tf_op jit(solution)/shard_map/ppermute | solution.py:234
  48.8 0.7 fusion.2.vecs_ref.sub_vecs_ref
  49.5 1.2 reshape.187.arrived_ref
  50.7 1.6 %shard_map.87 = bf16[64,1024]{1,0:T(8,128)(2,1)} custom-call(s32[4]{0:T(128)S(1)} %pad_add_fusion.1.at_ref, s32[1,512]{1,0:T(1,128)S(1)} %bitcast.37, bf16[192,1024]{1,0:T(8,128)(2,1)S(1)} %reshape.187.arrived_ref), custom_call_target="tpu_custom_call" | custom-call | tf_op jit(solution)/shard_map/pallas_call | solution.py:215
  52.3 0.6 while.10
  52.8 3.3 %shard_map.88 = bf16[64,1536]{1,0:T(8,128)(2,1)S(1)} custom-call(s32[4]{0:T(128)S(1)} %pad_add_fusion.1.at_ref, bf16[64,1024]{1,0:T(8,128)(2,1)} %get-tuple-element.46.feats_ref, bf16[1024,1024]{1,0:T(8,128)(2,1)} %get-tuple-element.141, f32[1,1024]{1,0:T(1,128)S(1)} %get-tuple-element.47.norm_ref, bf16[4,1024,128]{2,1,0:T(8,128)(2,1)S(1)} %pad_maximum_fusion.mine_ref, ...), custom_call_target="tpu_custom_call" | custom-call | tf_op jit(solution)/shard_map/pallas_call | solution.py:125
  56.1 0.1 reshape.188
  56.2 32.1 %all_to_all.26 = bf16[64,3,4,128]{3,2,1,0:T(4,128)(2,1)S(1)} all-to-all(bf16[64,3,4,128]{3,2,1,0:T(4,128)(2,1)S(1)} %reshape.188), channel_id=1, replica_groups=mesh['y'=4,'core'=2,'z'=16,'x'=4] {'z','x'}, dimensions={0} | all-to-all | bytes 393216 | tf_op jit(solution)/shard_map/all_to_all | solution.py:17
  88.3 0.1 reduce_sum.23
  88.4 0.6 broadcast_in_dim.31
  89.0 4.2 %all-to-all-start.3 = ((bf16[16,3,4,128]{3,2,1,0:T(4,128)(2,1)}), bf16[16,3,4,128]{3,2,1,0:T(4,128)(2,1)S(1)}, u32[]{:S(2)}, u32[]{:S(2)}) async-start(bf16[16,3,4,128]{3,2,1,0:T(4,128)(2,1)} %broadcast_in_dim.31), calls=%async_computation.3 | async-start | bytes 98304 | tf_op jit(solution)/shard_map/all_to_all | solution.py:17
  93.2 0.0 copy-start.3
  93.2 11.6 %all-to-all-done.3 = bf16[16,3,4,128]{3,2,1,0:T(4,128)(2,1)S(1)} async-done(((bf16[16,3,4,128]{3,2,1,0:T(4,128)(2,1)}), bf16[16,3,4,128]{3,2,1,0:T(4,128)(2,1)S(1)}, u32[]{:S(2)}, u32[]{:S(2)}) %all-to-all-start.3) | async-done | bytes 49184 | tf_op jit(solution)/shard_map/all_to_all | solution.py:17
  105.0 0.9 broadcast_in_dim.33
  106.0 7.5 %all-to-all-start.4 = ((bf16[32,16,640]{2,1,0:T(8,128)(2,1)}), bf16[32,16,640]{2,1,0:T(8,128)(2,1)}, u32[]{:S(2)}, u32[]{:S(2)}) async-start(bf16[32,16,640]{2,1,0:T(8,128)(2,1)} %bitcast.16), calls=%async_computation.4 | async-start | bytes 1310720 | tf_op jit(solution)/shard_map/all_to_all | solution.py:17
  113.5 0.2 convert_reduce_fusion
  113.8 0.4 fusion.1.batch_spread_ref
  114.2 12.0 %all-to-all-done.4 = bf16[32,16,640]{2,1,0:T(8,128)(2,1)} async-done(((bf16[32,16,640]{2,1,0:T(8,128)(2,1)}), bf16[32,16,640]{2,1,0:T(8,128)(2,1)}, u32[]{:S(2)}, u32[]{:S(2)}) %all-to-all-start.4) | async-done | bytes 655392 | tf_op jit(solution)/shard_map/all_to_all | solution.py:17
  126.2 4.0 %shard_map.89 = (f32[1024,125]{1,0:T(8,128)}, f32[512,125]{1,0:T(8,128)}) custom-call(s32[4]{0:T(128)S(1)} %pad_add_fusion.1.at_ref, bf16[512,640]{1,0:T(8,128)(2,1)} %bitcast.17.arrived_ref, s32[1,512]{1,0:T(1,128)S(1)} %fusion.9.line_ref, f32[1,512]{1,0:T(1,128)S(1)} %bitcast.35, bf16[1024,512]{1,0:T(8,128)(2,1)S(1)} %fusion.2.vecs_ref.sub_vecs_ref, ...), custom_call_target="tpu_custom_call" | custom-call | tf_op jit(solution)/shard_map/pallas_call | solution.py:261
  (27 shorter events, 0.3 us)
Async XLA Ops:
  0.6 48.1 %copy-start = (bf16[512,512]{1,0:T(8,128)(2,1)S(1)}, bf16[512,512]{1,0:T(8,128)(2,1)}, u32[]{:S(2)}) copy-start(bf16[512,512]{1,0:T(8,128)(2,1)} %param.14) | copy-start | bytes 1572868
  0.6 23.8 %copy-start.1 = (f32[1024,125]{1,0:T(8,128)S(1)}, f32[1024,125]{1,0:T(8,128)}, u32[]{:S(2)}) copy-start(f32[1024,125]{1,0:T(8,128)} %weights_ref.1) | copy-start | bytes 1536004
  5.0 43.7 %copy-start.5 = (s32[512]{0:T(512)S(1)}, s32[512]{0:T(512)}, u32[]{:S(2)}) copy-start(s32[512]{0:T(512)} %param.13) | copy-start | bytes 6148
  5.0 44.5 %all-to-all-start.1 = ((bf16[64,24,128]{2,1,0:T(8,128)(2,1)}), bf16[64,24,128]{2,1,0:T(8,128)(2,1)}, u32[]{:S(2)}, u32[]{:S(2)}) async-start(bf16[64,24,128]{2,1,0:T(8,128)(2,1)} %broadcast_in_dim.30), calls=%async_computation.1 | async-start | bytes 786432 | tf_op jit(solution)/shard_map/all_to_all | solution.py:17
  24.6 10.3 %collective-permute-start = (bf16[1024,128]{1,0:T(8,128)(2,1)S(1)}, bf16[1024,128]{1,0:T(8,128)(2,1)S(1)}, u32[]{:S(2)}, u32[]{:S(2)}) collective-permute-start(bf16[1024,128]{1,0:T(8,128)(2,1)S(1)} %get-tuple-element.63), channel_id=1, source_target_pairs={{0,128},{128,256},{256,384},{384,0},{1,129},{129,257},{257,385},{3... | collective-permute-start | bytes 786440 | tf_op jit(solution)/shard_map/ppermute | solution.py:231
  27.8 9.0 %collective-permute-start.2 = (bf16[1024,128]{1,0:T(8,128)(2,1)S(1)}, bf16[1024,128]{1,0:T(8,128)(2,1)S(1)}, u32[]{:S(2)}, u32[]{:S(2)}) collective-permute-start(bf16[1024,128]{1,0:T(8,128)(2,1)S(1)} %get-tuple-element.63), channel_id=1, source_target_pairs={{0,384},{128,0},{256,128},{384,256},{1,385},{129,1},{257,129},{385... | collective-permute-start | bytes 786440 | tf_op jit(solution)/shard_map/ppermute | solution.py:231
  34.9 9.4 %collective-permute-start.1 = (bf16[1024,128]{1,0:T(8,128)(2,1)S(1)}, bf16[1024,128]{1,0:T(8,128)(2,1)S(1)}, u32[]{:S(2)}, u32[]{:S(2)}) collective-permute-start(bf16[1024,128]{1,0:T(8,128)(2,1)S(1)} %collective-permute-done), channel_id=1, source_target_pairs={{0,128},{128,256},{256,384},{384,0},{1,129},{129,257},{257,385},{3... | collective-permute-start | bytes 786440 | tf_op jit(solution)/shard_map/ppermute | solution.py:232
  44.4 6.3 %copy-start.4 = (s32[512]{0:T(512)S(1)}, s32[512]{0:T(512)}, u32[]{:S(2)}) copy-start(s32[512]{0:T(512)} %param.12) | copy-start | bytes 6148
  44.4 8.4 %collective-permute-start.3 = (bf16[4,1024,128]{2,1,0:T(8,128)(2,1)S(1)}, bf16[4,1024,128]{2,1,0:T(8,128)(2,1)}, u32[]{:S(2)}, u32[]{:S(2)}) collective-permute-start(bf16[4,1024,128]{2,1,0:T(8,128)(2,1)S(1)} %pad_maximum_fusion.mine_ref), channel_id=1, source_target_pairs={{0,64},{64,0},{1,65},{65,1},{2,66},{66,2},{3,67},{67,3},{4,68},{68... | collective-permute-start | bytes 3145736 | tf_op jit(solution)/shard_map/ppermute | solution.py:234
  89.0 15.8 %all-to-all-start.3 = ((bf16[16,3,4,128]{3,2,1,0:T(4,128)(2,1)}), bf16[16,3,4,128]{3,2,1,0:T(4,128)(2,1)S(1)}, u32[]{:S(2)}, u32[]{:S(2)}) async-start(bf16[16,3,4,128]{3,2,1,0:T(4,128)(2,1)} %broadcast_in_dim.31), calls=%async_computation.3 | async-start | bytes 98304 | tf_op jit(solution)/shard_map/all_to_all | solution.py:17
  93.2 33.0 %copy-start.2 = (f32[512,125]{1,0:T(8,128)S(1)}, f32[512,125]{1,0:T(8,128)}, u32[]{:S(2)}) copy-start(f32[512,125]{1,0:T(8,128)} %targets_ref.1) | copy-start | bytes 768004
  93.2 33.0 %copy-start.3 = (f32[512]{0:T(512)S(1)}, f32[512]{0:T(512)}, u32[]{:S(2)}) copy-start(f32[512]{0:T(512)} %param.15) | copy-start | bytes 6148
  106.0 20.2 %all-to-all-start.4 = ((bf16[32,16,640]{2,1,0:T(8,128)(2,1)}), bf16[32,16,640]{2,1,0:T(8,128)(2,1)}, u32[]{:S(2)}, u32[]{:S(2)}) async-start(bf16[32,16,640]{2,1,0:T(8,128)(2,1)} %bitcast.16), calls=%async_computation.4 | async-start | bytes 1310720 | tf_op jit(solution)/shard_map/all_to_all | solution.py:17

commit v10 on v4

--- a/solution.py
+++ b/solution.py
@@ -49,7 +49,7 @@
         kernel,
         out_shape=shape,
         in_specs=[pl.BlockSpec(memory_space=pltpu.SMEM)] + [vmem] * count,
-        out_specs=vmem,
+        out_specs=jax.tree.map(lambda _: vmem, shape),
         compiler_params=pltpu.CompilerParams(vmem_limit_bytes=12 << 20),
     )
 
@@ -58,7 +58,7 @@
     return jnp.sum((rows < edge).astype(jnp.float32), axis=1, keepdims=True).astype(jnp.int32)
 
 
-def pick_kernel(at_ref, rows_ref, centers_ref, out_ref):
+def pick_kernel(at_ref, rows_ref, centers_ref, out_ref, norm_ref, most_ref, *, nctr):
     count = centers_ref.shape[0]
     base, slice_at, step, nout = at_ref[0] * count, at_ref[1], at_ref[2], at_ref[3]
     rows = rows_ref[...]
@@ -74,6 +74,12 @@
         pick, centers_ref[...], (((0,), (0,)), ((), ())), preferred_element_type=jnp.float32
     )
     out_ref[...] = found[: out_ref.shape[0]].astype(jnp.bfloat16)
+    wide = centers_ref[...].astype(jnp.float32)
+    norm = jnp.sum(wide * wide, axis=1, keepdims=True)
+    norm_ref[...] = jnp.transpose(jnp.broadcast_to(norm, (count, LANES)))[:1]
+    edges = lax.broadcasted_iota(jnp.int32, (nctr, 1), 0) * count
+    most = jnp.max(rows_below(rows, edges + count) - rows_below(rows, edges), axis=0, keepdims=True)
+    most_ref[...] = most
 
 
 def slot_kernel(at_ref, rows_ref, arrived_ref, out_ref, *, count):
@@ -137,9 +143,6 @@
     block = batch // nout
     base = place * row_count
 
-    edges = jnp.arange(nctr, dtype=jnp.int32)[:, None] * row_count
-    owned = (batch_rows[None, :] >= edges) & (batch_rows[None, :] < edges + row_count)
-    most = jnp.max(jnp.sum(owned.astype(jnp.int32), axis=1))
     batch_line = batch_rows[None, :]
 
     def places(turn):
@@ -147,21 +150,28 @@
 
     def round_of(turn):
         at = places(turn)
-        shape = jax.ShapeDtypeStruct((ROUND, feature_count), low)
-        share = whole(pick_kernel, shape, 2)(at, batch_line, centers)
+        shapes = (
+            jax.ShapeDtypeStruct((ROUND, feature_count), low),
+            jax.ShapeDtypeStruct((1, row_count), jnp.float32),
+            jax.ShapeDtypeStruct((1, 1), jnp.int32),
+        )
+        pick = functools.partial(pick_kernel, nctr=nctr)
+        share, norm, most = whole(pick, shapes, 2)(at, batch_line, centers)
         arrived = copied_to_all(share.reshape(-1, LANES), CTR)
         arrived = arrived.reshape(nctr * ROUND, feature_count)
         shape = jax.ShapeDtypeStruct((block, feature_count), low)
         slot = functools.partial(slot_kernel, count=row_count)
-        return whole(slot, shape, 2)(at, batch_line, arrived)
+        return whole(slot, shape, 2)(at, batch_line, arrived), norm, most
+
+    feats, right_norm, most = round_of(0)
+    most = most[0, 0]
 
     def more(carry):
         return carry[0] * (ROUND * nout) < most
 
     def next_round(carry):
-        return carry[0] + 1, carry[1] + round_of(carry[0])
-
-    feats = round_of(0)
+        return carry[0] + 1, carry[1] + round_of(carry[0])[0]
+
     _, feats = lax.while_loop(more, next_round, (jnp.int32(1), feats))
 
     weights_low = jnp.pad(weights.astype(low), ((0, 0), (0, LANES - columns)))
@@ -175,8 +185,7 @@
     other = lax.ppermute(mine, "core", [(i, (i + 1) % ncore) for i in range(ncore)])
 
     sub_vecs = dot(one_hot_columns(subsample - base, row_count), eigvecs).astype(low)
-    right_norm = jnp.sum(jnp.square(centers.astype(jnp.float32)), axis=1)
-    parts = products(places(0), feats, centers, right_norm[None, :], mine, other, sub_vecs)
+    parts = products(places(0), feats, centers, right_norm, mine, other, sub_vecs)
 
     blocks = parts.shape[1] // LANES
     arrived = exchanged(parts.reshape(nctr, blocks // 4, 4, LANES), CTR)

time: 133 us -> 131 us (0.985)
  other arithmetic: 5.26 us -> 2.34 us
    reduce_sum x2 -> x0, other arithmetic: 2.25 us -> none  [the longest x1 2.07 us: body(): right_norm = jnp.sum(jnp.square(centers.astype(jnp.float32)), axis=1)]
  transfers between devices with their start and end apart: 8 -> 8, of which waited for: 5 -> 6; matrix products, arithmetic and copies ran while one was open for 5% -> 3% of each run, Pallas kernels for 1% -> 1%
where the time goes in v10:
time: 131 us; the launch traced here: 130 us
  starting transfers between devices  60.1 us (46%)
  waiting for transfers between devices  48.5 us (37%)
  Pallas kernels  7.68 us (6%)
  matrix products  6.41 us (5%)
  local copies, waits for them, and re-layouts  3.42 us (3%)
  other arithmetic  2.34 us (2%)
    all_to_all x4, starting transfers between devices, exchanged(): return lax.all_to_all(pieces, axes, split_axis=0, concat_axis=0, tiled=True)  45 us
    all_to_all x4, waiting for transfers between devices, exchanged(): return lax.all_to_all(pieces, axes, split_axis=0, concat_axis=0, tiled=True)  39.2 us
    ppermute x3, starting transfers between devices, body(): lax.ppermute(weights_low, 'y', [(i, (i + dy) % ny) for i in range(ny)])  10.1 us
    ppermute x3, waiting for transfers between devices, body(): lax.ppermute(weights_low, 'y', [(i, (i + dy) % ny) for i in range(ny)])  8.87 us
    ppermute x1, starting transfers between devices, body(): lax.ppermute(mine, 'core', [(i, (i + 1) % ncore) for i in range(ncore)])  5 us
    pallas_call x1, Pallas kernels, round_of(): share, norm, most = whole(pick, shapes, 2)(at, batch_line, centers)  3.48 us
    dot_general x3, matrix products, dot(): return jnp.dot(left, right, preferred_element_type=jnp.float32)  3.31 us
    pallas_call x1, Pallas kernels, products(): whole(products_kernel, shape, 6)  3.26 us
  transfers between devices with their start and end apart: 8, of which 6 were waited for; matrix products, arithmetic and copies ran while one was open for 3% of the time, Pallas kernels for 1%

profile of v10, /device:TPU:1, one launch (start us, length us, event | category | flops | bytes accessed | tf_op | source)
XLA Modules:
  0.0 130.1 jit_solution(13382282365281939127)
XLA Ops:
  0.7 3.5 %shard_map.86 = (bf16[3,1024]{1,0:T(4,128)(2,1)S(1)}, f32[1,1024]{1,0:T(1,128)S(1)}, s32[1,1]{1,0:T(1,128)}) custom-call(s32[4]{0:T(128)S(1)} %pad_add_fusion.1.at_ref, s32[1,512]{1,0:T(1,128)} %bitcast.37, bf16[1024,1024]{1,0:T(8,128)(2,1)} %centers_ref.3), custom_call_target="tpu_custom_call" | custom-call | tf_op jit(solution)/shard_map/pallas_call | solution.py:159
  4.3 0.8 broadcast_in_dim.25
  5.1 19.1 %all-to-all-start.1 = ((bf16[64,24,128]{2,1,0:T(8,128)(2,1)}), bf16[64,24,128]{2,1,0:T(8,128)(2,1)S(1)}, u32[]{:S(2)}, u32[]{:S(2)}) async-start(bf16[64,24,128]{2,1,0:T(8,128)(2,1)} %broadcast_in_dim.25), calls=%async_computation.1 | async-start | bytes 786432 | tf_op jit(solution)/shard_map/all_to_all | solution.py:17
  24.3 4.6 %collective-permute-start.2 = (bf16[1024,128]{1,0:T(8,128)(2,1)S(1)}, bf16[1024,128]{1,0:T(8,128)(2,1)S(1)}, u32[]{:S(2)}, u32[]{:S(2)}) collective-permute-start(bf16[1024,128]{1,0:T(8,128)(2,1)S(1)} %get-tuple-element.67), channel_id=1, source_target_pairs={{0,384},{128,0},{256,128},{384,256},{1,385},{129,1},{257,129},{385... | collective-permute-start | bytes 786440 | tf_op jit(solution)/shard_map/ppermute | solution.py:181
  28.9 1.9 %collective-permute-start = (bf16[1024,128]{1,0:T(8,128)(2,1)S(1)}, bf16[1024,128]{1,0:T(8,128)(2,1)S(1)}, u32[]{:S(2)}, u32[]{:S(2)}) collective-permute-start(bf16[1024,128]{1,0:T(8,128)(2,1)S(1)} %get-tuple-element.67), channel_id=1, source_target_pairs={{0,128},{128,256},{256,384},{384,0},{1,129},{129,257},{257,385},{3... | collective-permute-start | bytes 786440 | tf_op jit(solution)/shard_map/ppermute | solution.py:181
  30.9 3.5 %collective-permute-start.1 = (bf16[1024,128]{1,0:T(8,128)(2,1)S(1)}, bf16[1024,128]{1,0:T(8,128)(2,1)S(1)}, u32[]{:S(2)}, u32[]{:S(2)}) collective-permute-start(bf16[1024,128]{1,0:T(8,128)(2,1)S(1)} %get-tuple-element.67), channel_id=1, source_target_pairs={{0,256},{128,384},{256,0},{384,128},{1,257},{129,385},{257,1},{385... | collective-permute-start | bytes 786440 | tf_op jit(solution)/shard_map/ppermute | solution.py:181
  34.4 5.3 %collective-permute-done = bf16[1024,128]{1,0:T(8,128)(2,1)S(1)} collective-permute-done((bf16[1024,128]{1,0:T(8,128)(2,1)S(1)}, bf16[1024,128]{1,0:T(8,128)(2,1)S(1)}, u32[]{:S(2)}, u32[]{:S(2)}) %collective-permute-start) | collective-permute-done | bytes 262176 | tf_op jit(solution)/shard_map/ppermute | solution.py:181
  39.7 3.6 %collective-permute-done.1 = bf16[1024,128]{1,0:T(8,128)(2,1)S(1)} collective-permute-done((bf16[1024,128]{1,0:T(8,128)(2,1)S(1)}, bf16[1024,128]{1,0:T(8,128)(2,1)S(1)}, u32[]{:S(2)}, u32[]{:S(2)}) %collective-permute-start.1) | collective-permute-done | bytes 262176 | tf_op jit(solution)/shard_map/ppermute | solution.py:181
  43.4 5.0 %collective-permute-start.3 = (bf16[4,1024,128]{2,1,0:T(8,128)(2,1)S(1)}, bf16[4,1024,128]{2,1,0:T(8,128)(2,1)}, u32[]{:S(2)}, u32[]{:S(2)}) collective-permute-start(bf16[4,1024,128]{2,1,0:T(8,128)(2,1)S(1)} %pad_maximum_fusion.mine_ref), channel_id=1, source_target_pairs={{0,64},{64,0},{1,65},{65,1},{2,66},{66,2},{3,67},{67,3},{4,68},{68... | collective-permute-start | bytes 3145736 | tf_op jit(solution)/shard_map/ppermute | solution.py:185
  48.5 0.7 fusion.6.vecs_ref
  49.2 0.2 reshape.163.arrived_ref
  49.4 0.9 shard_map.87
  50.3 0.5 collective-permute-done.3.other_ref
  50.8 0.6 while.10
  51.5 3.3 %shard_map.88 = bf16[64,1536]{1,0:T(8,128)(2,1)S(1)} custom-call(s32[4]{0:T(128)S(1)} %pad_add_fusion.1.at_ref, bf16[64,1024]{1,0:T(8,128)(2,1)S(1)} %get-tuple-element.49.feats_ref, bf16[1024,1024]{1,0:T(8,128)(2,1)} %get-tuple-element.145, f32[1,1024]{1,0:T(1,128)S(1)} %get-tuple-element.50.norm_ref, bf16[4,1024,128]{2,1,0:T(8,128)(2,1)S(1)} %pad_maximum_fusion.mine_ref, ...), custom_call_target="tpu_custom_call" | custom-call | tf_op jit(solution)/shard_map/pallas_call | solution.py:129
  54.8 0.7 reshape.164
  55.5 14.5 %all-to-all-start.2 = ((bf16[64,3,4,128]{3,2,1,0:T(4,128)(2,1)}), bf16[64,3,4,128]{3,2,1,0:T(4,128)(2,1)S(1)}, u32[]{:S(2)}, u32[]{:S(2)}) async-start(bf16[64,3,4,128]{3,2,1,0:T(4,128)(2,1)} %reshape.164), calls=%async_computation.2 | async-start | bytes 393216 | tf_op jit(solution)/shard_map/all_to_all | solution.py:17
  70.0 0.2 convert_reduce_fusion
  70.3 17.3 %all-to-all-done.2 = bf16[64,3,4,128]{3,2,1,0:T(4,128)(2,1)S(1)} async-done(((bf16[64,3,4,128]{3,2,1,0:T(4,128)(2,1)}), bf16[64,3,4,128]{3,2,1,0:T(4,128)(2,1)S(1)}, u32[]{:S(2)}, u32[]{:S(2)}) %all-to-all-start.2) | async-done | bytes 196640 | tf_op jit(solution)/shard_map/all_to_all | solution.py:17
  87.8 0.6 broadcast_in_dim.42
  88.4 4.4 %all-to-all-start.3 = ((bf16[16,3,4,128]{3,2,1,0:T(4,128)(2,1)}), bf16[16,3,4,128]{3,2,1,0:T(4,128)(2,1)S(1)}, u32[]{:S(2)}, u32[]{:S(2)}) async-start(bf16[16,3,4,128]{3,2,1,0:T(4,128)(2,1)} %broadcast_in_dim.42), calls=%async_computation.3 | async-start | bytes 98304 | tf_op jit(solution)/shard_map/all_to_all | solution.py:17
  92.8 1.8 %fusion.11 = f32[512,125]{1,0:T(8,128)} fusion(f32[512,125]{1,0:T(8,128)S(1)} %copy-done.1, s32[512]{0:T(512)S(1)} %fusion.28), kind=kOutput, calls=%fused_computation.19 | convolution fusion | flops 393478144 | bytes 514048 | tf_op jit(solution)/shard_map/dot_general | solution.py:215
  94.6 0.2 select_reduce_fusion
  94.8 9.6 %all-to-all-done.3 = bf16[16,3,4,128]{3,2,1,0:T(4,128)(2,1)S(1)} async-done(((bf16[16,3,4,128]{3,2,1,0:T(4,128)(2,1)}), bf16[16,3,4,128]{3,2,1,0:T(4,128)(2,1)S(1)}, u32[]{:S(2)}, u32[]{:S(2)}) %all-to-all-start.3) | async-done | bytes 49184 | tf_op jit(solution)/shard_map/all_to_all | solution.py:17
  104.7 0.9 broadcast_in_dim.44
  105.6 6.9 %all-to-all-start.4 = ((bf16[32,16,640]{2,1,0:T(8,128)(2,1)}), bf16[32,16,640]{2,1,0:T(8,128)(2,1)S(1)}, u32[]{:S(2)}, u32[]{:S(2)}) async-start(bf16[32,16,640]{2,1,0:T(8,128)(2,1)} %bitcast.16), calls=%async_computation.4 | async-start | bytes 1310720 | tf_op jit(solution)/shard_map/all_to_all | solution.py:17
  112.5 0.4 fusion.5
  113.0 12.2 %all-to-all-done.4 = bf16[32,16,640]{2,1,0:T(8,128)(2,1)S(1)} async-done(((bf16[32,16,640]{2,1,0:T(8,128)(2,1)}), bf16[32,16,640]{2,1,0:T(8,128)(2,1)S(1)}, u32[]{:S(2)}, u32[]{:S(2)}) %all-to-all-start.4) | async-done | bytes 655392 | tf_op jit(solution)/shard_map/all_to_all | solution.py:17
  125.2 1.1 convolution_subtract_fusion
  126.3 1.0 multiply_convert_fusion
  127.2 1.3 %fusion.10 = bf16[512,125]{1,0:T(8,128)(2,1)S(1)} fusion(bf16[512,640]{1,0:T(8,128)(2,1)S(1)} %bitcast.36, f32[512,125]{1,0:T(8,128)} %fusion.11, f32[512]{0:T(512)S(1)} %broadcast_multiply_fusion), kind=kOutput, calls=%fused_computation.13 | convolution fusion | flops 65856000 | bytes 1041408 | tf_op jit(solution)/shard_map/dot_general | solution.py:227
  128.6 1.5 %fusion.7 = f32[1024,125]{1,0:T(8,128)} fusion(f32[1024,125]{1,0:T(8,128)S(1)} %copy-done.4, bf16[1024,512]{1,0:T(8,128)(2,1)S(1)} %fusion.5, bf16[1024,512]{1,0:T(8,128)(2,1)S(1)} %fusion.6.vecs_ref, bf16[512,125]{1,0:T(8,128)(2,1)S(1)} %multiply_convert_fusion, bf16[512,125]{1,0:T(8,128)(2,1)S(1)} %fusion.10), kind=kOutput, calls=%fused_computation.10 | convolution fusion | flops 266978304 | bytes 3377152 | tf_op jit(solution)/shard_map/dot_general | solution.py:37
  (38 shorter events, 0.7 us)
Async XLA Ops:
  0.6 47.8 %copy-start = (bf16[512,512]{1,0:T(8,128)(2,1)S(1)}, bf16[512,512]{1,0:T(8,128)(2,1)}, u32[]{:S(2)}) copy-start(bf16[512,512]{1,0:T(8,128)(2,1)} %param.14) | copy-start | bytes 1572868
  0.6 3.6 %copy-start.3 = (f32[1024,125]{1,0:T(8,128)S(1)}, f32[1024,125]{1,0:T(8,128)}, u32[]{:S(2)}) copy-start(f32[1024,125]{1,0:T(8,128)} %param.10) | copy-start | bytes 1536004
  4.3 44.2 %copy-start.6 = (s32[512]{0:T(512)S(1)}, s32[512]{0:T(512)}, u32[]{:S(2)}) copy-start(s32[512]{0:T(512)} %param.13) | copy-start | bytes 6148
  5.1 44.1 %all-to-all-start.1 = ((bf16[64,24,128]{2,1,0:T(8,128)(2,1)}), bf16[64,24,128]{2,1,0:T(8,128)(2,1)S(1)}, u32[]{:S(2)}, u32[]{:S(2)}) async-start(bf16[64,24,128]{2,1,0:T(8,128)(2,1)} %broadcast_in_dim.25), calls=%async_computation.1 | async-start | bytes 786432 | tf_op jit(solution)/shard_map/all_to_all | solution.py:17
  24.3 10.1 %collective-permute-start.2 = (bf16[1024,128]{1,0:T(8,128)(2,1)S(1)}, bf16[1024,128]{1,0:T(8,128)(2,1)S(1)}, u32[]{:S(2)}, u32[]{:S(2)}) collective-permute-start(bf16[1024,128]{1,0:T(8,128)(2,1)S(1)} %get-tuple-element.67), channel_id=1, source_target_pairs={{0,384},{128,0},{256,128},{384,256},{1,385},{129,1},{257,129},{385... | collective-permute-start | bytes 786440 | tf_op jit(solution)/shard_map/ppermute | solution.py:181
  28.9 10.7 %collective-permute-start = (bf16[1024,128]{1,0:T(8,128)(2,1)S(1)}, bf16[1024,128]{1,0:T(8,128)(2,1)S(1)}, u32[]{:S(2)}, u32[]{:S(2)}) collective-permute-start(bf16[1024,128]{1,0:T(8,128)(2,1)S(1)} %get-tuple-element.67), channel_id=1, source_target_pairs={{0,128},{128,256},{256,384},{384,0},{1,129},{129,257},{257,385},{3... | collective-permute-start | bytes 786440 | tf_op jit(solution)/shard_map/ppermute | solution.py:181
  30.9 12.4 %collective-permute-start.1 = (bf16[1024,128]{1,0:T(8,128)(2,1)S(1)}, bf16[1024,128]{1,0:T(8,128)(2,1)S(1)}, u32[]{:S(2)}, u32[]{:S(2)}) collective-permute-start(bf16[1024,128]{1,0:T(8,128)(2,1)S(1)} %get-tuple-element.67), channel_id=1, source_target_pairs={{0,256},{128,384},{256,0},{384,128},{1,257},{129,385},{257,1},{385... | collective-permute-start | bytes 786440 | tf_op jit(solution)/shard_map/ppermute | solution.py:181
  43.4 6.0 %copy-start.5 = (s32[512]{0:T(512)S(1)}, s32[512]{0:T(512)}, u32[]{:S(2)}) copy-start(s32[512]{0:T(512)} %param.12) | copy-start | bytes 6148
  43.4 7.4 %collective-permute-start.3 = (bf16[4,1024,128]{2,1,0:T(8,128)(2,1)S(1)}, bf16[4,1024,128]{2,1,0:T(8,128)(2,1)}, u32[]{:S(2)}, u32[]{:S(2)}) collective-permute-start(bf16[4,1024,128]{2,1,0:T(8,128)(2,1)S(1)} %pad_maximum_fusion.mine_ref), channel_id=1, source_target_pairs={{0,64},{64,0},{1,65},{65,1},{2,66},{66,2},{3,67},{67,3},{4,68},{68... | collective-permute-start | bytes 3145736 | tf_op jit(solution)/shard_map/ppermute | solution.py:185
  51.5 41.3 %copy-start.1 = (f32[512,125]{1,0:T(8,128)S(1)}, f32[512,125]{1,0:T(8,128)}, u32[]{:S(2)}) copy-start(f32[512,125]{1,0:T(8,128)} %param.11) | copy-start | bytes 768004
  55.5 32.1 %all-to-all-start.2 = ((bf16[64,3,4,128]{3,2,1,0:T(4,128)(2,1)}), bf16[64,3,4,128]{3,2,1,0:T(4,128)(2,1)S(1)}, u32[]{:S(2)}, u32[]{:S(2)}) async-start(bf16[64,3,4,128]{3,2,1,0:T(4,128)(2,1)} %reshape.164), calls=%async_computation.2 | async-start | bytes 393216 | tf_op jit(solution)/shard_map/all_to_all | solution.py:17
  88.4 16.1 %all-to-all-start.3 = ((bf16[16,3,4,128]{3,2,1,0:T(4,128)(2,1)}), bf16[16,3,4,128]{3,2,1,0:T(4,128)(2,1)S(1)}, u32[]{:S(2)}, u32[]{:S(2)}) async-start(bf16[16,3,4,128]{3,2,1,0:T(4,128)(2,1)} %broadcast_in_dim.42), calls=%async_computation.3 | async-start | bytes 98304 | tf_op jit(solution)/shard_map/all_to_all | solution.py:17
  94.8 18.1 %copy-start.7 = (f32[512]{0:T(512)S(1)}, f32[512]{0:T(512)}, u32[]{:S(2)}) copy-start(f32[512]{0:T(512)} %param.15) | copy-start | bytes 6148
  94.8 30.4 %copy-start.2 = (f32[512,125]{1,0:T(8,128)S(1)}, f32[512,125]{1,0:T(8,128)}, u32[]{:S(2)}) copy-start(f32[512,125]{1,0:T(8,128)} %param.11) | copy-start | bytes 768004
  105.6 19.6 %all-to-all-start.4 = ((bf16[32,16,640]{2,1,0:T(8,128)(2,1)}), bf16[32,16,640]{2,1,0:T(8,128)(2,1)S(1)}, u32[]{:S(2)}, u32[]{:S(2)}) async-start(bf16[32,16,640]{2,1,0:T(8,128)(2,1)} %bitcast.16), calls=%async_computation.4 | async-start | bytes 1310720 | tf_op jit(solution)/shard_map/all_to_all | solution.py:17
  125.2 3.4 %copy-start.4 = (f32[1024,125]{1,0:T(8,128)S(1)}, f32[1024,125]{1,0:T(8,128)}, u32[]{:S(2)}) copy-start(f32[1024,125]{1,0:T(8,128)} %param.10) | copy-start | bytes 1536004
